TPU v7x, 32 devices: a whole 2x2x4 slice. The times are simulated.
32 devices in a mesh: expert: 8 (over y, x, core), shard: 4 (over z).
Axes of the slice: x: 2, y: 2, z: 4, core: 2. Of those that a mesh axis runs over, the one named last changes fastest.
Arguments:
- hidden_in: bfloat16 [8192, 2048], P(('expert', 'shard')), may hold values from -6 to 6
- g_attn: bfloat16 [2048], P(('expert', 'shard')), may hold values from 0.5 to 1.5
- w_query: bfloat16 [2048, 4096], P(('expert', 'shard')), may hold values from -0.125 to 0.125
- w_key: bfloat16 [2048, 512], P(('expert', 'shard')), may hold values from -0.125 to 0.125
- w_value: bfloat16 [2048, 512], P(('expert', 'shard')), may hold values from -0.125 to 0.125
- g_query: bfloat16 [128], P(('expert', 'shard')), may hold values from 0.5 to 1.5
- g_key: bfloat16 [128], P(('expert', 'shard')), may hold values from 0.5 to 1.5
- w_out: bfloat16 [4096, 2048], P(('expert', 'shard')), may hold values from -1.5 to 1.5
- g_ffn: bfloat16 [2048], P(('expert', 'shard')), may hold values from 0.5 to 1.5
- w_router: bfloat16 [2048, 32], P(('expert', 'shard')), may hold values from -0.125 to 0.125
- w_gate: bfloat16 [32, 2048, 768], P(('expert', 'shard')), may hold values from -0.125 to 0.125
- w_up: bfloat16 [32, 2048, 768], P(('expert', 'shard')), may hold values from -0.125 to 0.125
- w_down: bfloat16 [32, 768, 2048], P(('expert', 'shard')), may hold values from -0.625 to 0.625
- routes: int32 [8192, 8], P(('expert', 'shard')), may hold values from 0 to 31, all different within a row; in each aligned block of 256 rows (0 to 255, 256 to 511, ...) at most 128 rows name the same one
- cotangent: bfloat16 [8192, 2048], P(('expert', 'shard')), may hold values from -6 to 6
Outputs:
- block_out: bfloat16 [8192, 2048], P(('expert', 'shard'))
- grad_input: bfloat16 [8192, 2048], P(('expert', 'shard'))
- grad_g_attn: float32 [2048], P(('expert', 'shard'))
- grad_w_query: float32 [2048, 4096], P(('expert', 'shard'))
- grad_w_key: float32 [2048, 512], P(('expert', 'shard'))
- grad_w_value: float32 [2048, 512], P(('expert', 'shard'))
- grad_g_query: float32 [128], P(('expert', 'shard'))
- grad_g_key: float32 [128], P(('expert', 'shard'))
- grad_w_out: float32 [4096, 2048], P(('expert', 'shard'))
- grad_g_ffn: float32 [2048], P(('expert', 'shard'))
- grad_router: float32 [2048, 32], P(('expert', 'shard'))
- grad_w_gate: float32 [32, 2048, 768], P(('expert', 'shard'))
- grad_w_up: float32 [32, 2048, 768], P(('expert', 'shard'))
- grad_w_down: float32 [32, 768, 2048], P(('expert', 'shard'))
Inputs may be any that keep to these rules, and one draw needn't show every extreme that they name: `routes`: each row names 8 different experts; among the rows of one device no expert is named more than 128 times.
All inputs are finite; a program needn't handle non-finite values.
Results may differ from a plain program's by a relative error of at most 0.025.
Values may be sent and summed in bfloat16 or wider, within the bound.
A program may use at most 448 MiB of HBM per device.

v0:
```python
import jax
import jax.numpy as jnp
from jax import lax
from jax.sharding import PartitionSpec as P

HQ = 32
HK = 4
HD = 128


epsilon = 1e-06
theta_base = 1000000.0


def matmul(left, right):
    return jnp.dot(left, right, preferred_element_type=jnp.float32)


def matmul_tn(left, right):
    return lax.dot_general(
        left, right, (((0,), (0,)), ((), ())), preferred_element_type=jnp.float32
    )


def matmul_nt(left, right):
    return lax.dot_general(
        left, right, (((1,), (1,)), ((), ())), preferred_element_type=jnp.float32
    )


def norm_rows(values, gain_vec):
    return (
        values * lax.rsqrt(jnp.mean(values * values, axis=-1, keepdims=True) + epsilon) * gain_vec
    )


def norm_back(values, gain_vec, upstream):
    scaling = lax.rsqrt(jnp.mean(values * values, axis=-1, keepdims=True) + epsilon)
    gain_grad = jnp.sum(upstream * values * scaling, axis=0)
    weighted = upstream * gain_vec
    inner_sum = jnp.mean(weighted * values, axis=-1, keepdims=True)
    return (scaling * weighted - values * (scaling * scaling * scaling) * inner_sum, gain_grad)


def rotary(values, positions):
    head_width = values.shape[-1]
    half_width = head_width // 2
    frequency = theta_base ** (-2.0 * jnp.arange(half_width, dtype=jnp.float32) / head_width)
    angles = positions.astype(jnp.float32)[:, None] * frequency[None, :]
    cosine = jnp.concatenate([jnp.cos(angles), jnp.cos(angles)], axis=-1)[:, None, :]
    sine_part = jnp.concatenate([jnp.sin(angles), jnp.sin(angles)], axis=-1)[:, None, :]
    turned = jnp.concatenate([-values[..., half_width:], values[..., :half_width]], axis=-1)
    return values * cosine + turned * sine_part


def head_prep(projected, gain_vec, positions, head_count, factor):
    shaped = projected.reshape(projected.shape[0], head_count, projected.shape[1] // head_count)
    return rotary(norm_rows(shaped, gain_vec), positions) * factor


def head_forward(query_block, key_block, value_block, allowed):
    scores = jnp.einsum("rgd,sd->rgs", query_block, key_block, preferred_element_type=jnp.float32)
    raised = jnp.where(allowed[:, None, :], jnp.exp(scores), 0.0)
    totals = jnp.sum(raised, axis=-1)
    probs_low = (raised / totals[..., None]).astype(jnp.bfloat16)
    return (
        jnp.einsum("rgs,sd->rgd", probs_low, value_block, preferred_element_type=jnp.float32),
        totals,
    )


def head_backward(query_block, key_block, value_block, totals, upstream, allowed):
    scores = jnp.einsum("rgd,sd->rgs", query_block, key_block, preferred_element_type=jnp.float32)
    raised = jnp.where(allowed[:, None, :], jnp.exp(scores), 0.0)
    probs_f = raised / totals[..., None]
    probs_low = probs_f.astype(jnp.bfloat16)
    grad_probs = jnp.einsum(
        "rgd,sd->rgs", upstream, value_block, preferred_element_type=jnp.float32
    )
    inner_sum = jnp.sum(probs_f * grad_probs, axis=-1, keepdims=True)
    grad_scores = (probs_f * (grad_probs - inner_sum)).astype(jnp.bfloat16)
    grad_query = jnp.einsum(
        "rgs,sd->rgd", grad_scores, key_block, preferred_element_type=jnp.float32
    )
    grad_key = jnp.einsum(
        "rgs,rgd->sd", grad_scores, query_block, preferred_element_type=jnp.float32
    )
    grad_value = jnp.einsum("rgs,rgd->sd", probs_low, upstream, preferred_element_type=jnp.float32)
    return (grad_query, grad_key, grad_value)


def per_device(
    hidden_in,
    g_attn,
    w_query,
    w_key,
    w_value,
    g_query,
    g_key,
    w_out,
    g_ffn,
    w_router,
    w_gate,
    w_up,
    w_down,
    routes,
    cotangent,
):
    tok_rows = hidden_in.shape[0]
    model_width = hidden_in.shape[1]
    top_count = routes.shape[1]
    expert_count = lax.axis_size(("expert", "shard")) * w_gate.shape[0]
    capacity = 2 * tok_rows * top_count // expert_count
    shard_count = lax.axis_size("shard")
    shard_pos = lax.axis_index("shard")
    seq_len = tok_rows * shard_count
    group_size = HQ // HK
    factor = HD ** (-0.5)
    sectioned = (
        lax.all_gather(w_query, "shard", axis=0, tiled=True),
        lax.all_gather(w_key, "shard", axis=0, tiled=True),
        lax.all_gather(w_value, "shard", axis=0, tiled=True),
        lax.all_gather(w_out, "shard", axis=0, tiled=True),
        lax.all_gather(w_router, "shard", axis=0, tiled=True),
        lax.all_gather(g_attn, "shard", axis=0, tiled=True),
        lax.all_gather(g_ffn, "shard", axis=0, tiled=True),
        lax.all_gather(g_query, "shard", axis=0, tiled=True),
        lax.all_gather(g_key, "shard", axis=0, tiled=True),
    )
    query_in = sectioned[0]
    out_in = sectioned[3]
    gathered = (
        lax.all_gather(query_in, "expert", axis=0, tiled=True),
        lax.all_gather(sectioned[1], "expert", axis=0, tiled=True),
        lax.all_gather(sectioned[2], "expert", axis=0, tiled=True),
        lax.all_gather(out_in, "expert", axis=0, tiled=True),
        lax.all_gather(sectioned[4], "expert", axis=0, tiled=True),
        lax.all_gather(sectioned[5], "expert", axis=0, tiled=True),
        lax.all_gather(sectioned[6], "expert", axis=0, tiled=True),
        lax.all_gather(sectioned[7], "expert", axis=0, tiled=True),
        lax.all_gather(sectioned[8], "expert", axis=0, tiled=True),
    )
    wq_use, wk_full, wv_full, wo_use, wr_full = (
        gathered[0],
        gathered[1],
        gathered[2],
        gathered[3],
        gathered[4],
    )
    attn_gain = gathered[5].astype(jnp.float32)
    ffn_gain = gathered[6].astype(jnp.float32)
    query_gain = gathered[7].astype(jnp.float32)
    key_gain = gathered[8].astype(jnp.float32)
    positions = shard_pos * tok_rows + jnp.arange(tok_rows, dtype=jnp.int32)
    inputs_f = hidden_in.astype(jnp.float32)
    normed_low = norm_rows(inputs_f, attn_gain).astype(jnp.bfloat16)
    k_proj = matmul(normed_low, wk_full)
    v_proj = matmul(normed_low, wv_full)
    k_rot, k_pull = jax.vjp(
        lambda projected, gain_vec: head_prep(projected, gain_vec, positions, HK, 1.0),
        k_proj,
        key_gain,
    )
    k_low = k_rot.reshape(tok_rows, HK * HD).astype(jnp.bfloat16)
    v_low = v_proj.astype(jnp.bfloat16)
    q_proj = matmul(normed_low, wq_use)
    q_rot, q_pull = jax.vjp(
        lambda projected, gain_vec: head_prep(projected, gain_vec, positions, HQ, factor),
        q_proj,
        query_gain,
    )
    q_low = q_rot.astype(jnp.bfloat16)
    allowed = jnp.arange(seq_len, dtype=jnp.int32)[None, :] <= positions[:, None]
    keys_all, values_all = (
        lax.all_gather(k_low, "shard", axis=0, tiled=True),
        lax.all_gather(v_low, "shard", axis=0, tiled=True),
    )
    q_heads = q_low.reshape(tok_rows, HK, group_size, HD).transpose(1, 0, 2, 3)
    k_heads = keys_all.reshape(seq_len, HK, HD).transpose(1, 0, 2)
    v_heads = values_all.reshape(seq_len, HK, HD).transpose(1, 0, 2)

    def attend(pieces):
        return head_forward(pieces[0], pieces[1], pieces[2], allowed)

    head_outs, totals = lax.map(attend, (q_heads, k_heads, v_heads))
    mix_low = head_outs.transpose(1, 0, 2, 3).reshape(tok_rows, HQ * HD).astype(jnp.bfloat16)
    attn_out = matmul(mix_low, wo_use)
    residual = inputs_f + attn_out
    ffn_low = norm_rows(residual, ffn_gain).astype(jnp.bfloat16)
    logits = matmul(ffn_low, wr_full)
    expert_ids = jnp.arange(expert_count, dtype=jnp.int32)
    picked_mask = routes[:, :, None] == expert_ids[None, None, :]
    picked = jnp.sum(jnp.where(picked_mask, logits[:, None, :], 0.0), axis=-1)
    raised_gate = jnp.exp(picked)
    gate_probs = raised_gate / jnp.sum(raised_gate, axis=-1, keepdims=True)
    flat_routes = routes.reshape(-1)
    pair_count = tok_rows * top_count
    hit_table = (flat_routes[:, None] == expert_ids[None, :]).astype(jnp.int32)
    earlier = jnp.cumsum(hit_table, axis=0) - hit_table
    slot_index = jnp.sum(earlier * hit_table, axis=1)
    pair_place = flat_routes * capacity + slot_index
    slot_owner = (
        jnp.full((expert_count * capacity,), pair_count, jnp.int32)
        .at[pair_place]
        .set(jnp.arange(pair_count, dtype=jnp.int32))
    )
    token_of = jnp.where(slot_owner == pair_count, tok_rows, slot_owner // top_count)
    padded = jnp.concatenate([ffn_low, jnp.zeros((1, model_width), jnp.bfloat16)], axis=0)
    outgoing = jnp.take(padded, token_of, axis=0).reshape(expert_count, capacity, model_width)
    incoming = lax.all_to_all(
        outgoing, ("expert", "shard"), split_axis=0, concat_axis=0, tiled=True
    )
    expert_rows = incoming.reshape(expert_count * capacity, model_width)
    gate_act = matmul(expert_rows, w_gate[0])
    up_act = matmul(expert_rows, w_up[0])
    gate_sig = jax.nn.sigmoid(gate_act)
    activated = gate_act * gate_sig
    hidden_low = (activated * up_act).astype(jnp.bfloat16)
    expert_out = (
        matmul(hidden_low, w_down[0])
        .astype(jnp.bfloat16)
        .reshape(expert_count, capacity, model_width)
    )
    returned = lax.all_to_all(
        expert_out, ("expert", "shard"), split_axis=0, concat_axis=0, tiled=True
    )
    per_pair = jnp.take(returned.reshape(expert_count * capacity, model_width), pair_place, axis=0)
    per_pair = per_pair.reshape(tok_rows, top_count, model_width).astype(jnp.float32)
    block_out = (residual + jnp.sum(gate_probs[:, :, None] * per_pair, axis=1)).astype(jnp.bfloat16)
    upstream = cotangent.astype(jnp.float32)
    grad_pair = (
        (gate_probs[:, :, None] * upstream[:, None, :])
        .astype(jnp.bfloat16)
        .reshape(pair_count, model_width)
    )
    grad_gates = jnp.sum(per_pair * upstream[:, None, :], axis=-1)
    grad_padded = jnp.concatenate([grad_pair, jnp.zeros((1, model_width), jnp.bfloat16)], axis=0)
    grad_outgoing = jnp.take(grad_padded, slot_owner, axis=0).reshape(
        expert_count, capacity, model_width
    )
    grad_incoming = lax.all_to_all(
        grad_outgoing, ("expert", "shard"), split_axis=0, concat_axis=0, tiled=True
    )
    grad_incoming = grad_incoming.reshape(expert_count * capacity, model_width)
    grad_wdown = matmul_tn(hidden_low, grad_incoming)
    grad_hidden = matmul_nt(grad_incoming, w_down[0])
    grad_gate_act = (grad_hidden * up_act * gate_sig * (1.0 + gate_act * (1.0 - gate_sig))).astype(
        jnp.bfloat16
    )
    grad_up_act = (grad_hidden * activated).astype(jnp.bfloat16)
    grad_wgate = matmul_tn(expert_rows, grad_gate_act)
    grad_wup = matmul_tn(expert_rows, grad_up_act)
    grad_rows = (matmul_nt(grad_gate_act, w_gate[0]) + matmul_nt(grad_up_act, w_up[0])).astype(
        jnp.bfloat16
    )
    grad_returned = lax.all_to_all(
        grad_rows.reshape(expert_count, capacity, model_width),
        ("expert", "shard"),
        split_axis=0,
        concat_axis=0,
        tiled=True,
    )
    grad_taken = jnp.take(
        grad_returned.reshape(expert_count * capacity, model_width), pair_place, axis=0
    )
    grad_ffn = jnp.sum(
        grad_taken.reshape(tok_rows, top_count, model_width).astype(jnp.float32), axis=1
    )
    grad_picked = gate_probs * (
        grad_gates - jnp.sum(gate_probs * grad_gates, axis=-1, keepdims=True)
    )
    grad_logits = jnp.sum(jnp.where(picked_mask, grad_picked[:, :, None], 0.0), axis=1).astype(
        jnp.bfloat16
    )
    grad_wrouter = matmul_tn(ffn_low, grad_logits)
    grad_ffn = grad_ffn + matmul_nt(grad_logits, wr_full)
    grad_second, grad_ffn_gain = norm_back(residual, ffn_gain, grad_ffn)
    grad_residual = upstream + grad_second
    grad_attn_low = grad_residual.astype(jnp.bfloat16)
    grad_wout = matmul_tn(mix_low, grad_attn_low)
    grad_mix = matmul_nt(grad_attn_low, wo_use).astype(jnp.bfloat16)
    grad_heads = grad_mix.reshape(tok_rows, HK, group_size, HD).transpose(1, 0, 2, 3)

    def attend_back(pieces):
        return head_backward(pieces[0], pieces[1], pieces[2], pieces[3], pieces[4], allowed)

    grad_qheads, grad_kheads, grad_vheads = lax.map(
        attend_back, (q_heads, k_heads, v_heads, totals, grad_heads)
    )
    grad_q_rot = grad_qheads.transpose(1, 0, 2, 3).reshape(tok_rows, HQ, HD)
    grad_keys = grad_kheads.transpose(1, 0, 2).reshape(seq_len, HK * HD)
    grad_values = grad_vheads.transpose(1, 0, 2).reshape(seq_len, HK * HD)
    grad_k_rot, grad_v_proj = (
        lax.psum_scatter(
            grad_keys.astype(jnp.bfloat16), "shard", scatter_dimension=0, tiled=True
        ).astype(jnp.float32),
        lax.psum_scatter(
            grad_values.astype(jnp.bfloat16), "shard", scatter_dimension=0, tiled=True
        ).astype(jnp.float32),
    )
    grad_q_proj, grad_query_gain = q_pull(grad_q_rot)
    grad_q_low = grad_q_proj.astype(jnp.bfloat16)
    grad_wquery = matmul_tn(normed_low, grad_q_low)
    grad_normed_q = matmul_nt(grad_q_low, wq_use)
    grad_k_proj, grad_key_gain = k_pull(grad_k_rot.reshape(tok_rows, HK, HD))
    grad_k_low = grad_k_proj.astype(jnp.bfloat16)
    grad_v_low = grad_v_proj.astype(jnp.bfloat16)
    grad_wkey = matmul_tn(normed_low, grad_k_low)
    grad_wvalue = matmul_tn(normed_low, grad_v_low)
    grad_normed = grad_normed_q + matmul_nt(grad_k_low, wk_full) + matmul_nt(grad_v_low, wv_full)
    grad_front, grad_attn_gain = norm_back(inputs_f, attn_gain, grad_normed)
    grad_input = (grad_residual + grad_front).astype(jnp.bfloat16)
    expert_summed = (
        lax.psum_scatter(
            grad_wquery.astype(jnp.bfloat16), "expert", scatter_dimension=0, tiled=True
        ).astype(jnp.float32),
        lax.psum_scatter(
            grad_wkey.astype(jnp.bfloat16), "expert", scatter_dimension=0, tiled=True
        ).astype(jnp.float32),
        lax.psum_scatter(
            grad_wvalue.astype(jnp.bfloat16), "expert", scatter_dimension=0, tiled=True
        ).astype(jnp.float32),
        lax.psum_scatter(
            grad_wout.astype(jnp.bfloat16), "expert", scatter_dimension=0, tiled=True
        ).astype(jnp.float32),
        lax.psum_scatter(
            grad_wrouter.astype(jnp.bfloat16), "expert", scatter_dimension=0, tiled=True
        ).astype(jnp.float32),
        lax.psum_scatter(
            grad_attn_gain.astype(jnp.bfloat16), "expert", scatter_dimension=0, tiled=True
        ).astype(jnp.float32),
        lax.psum_scatter(
            grad_ffn_gain.astype(jnp.bfloat16), "expert", scatter_dimension=0, tiled=True
        ).astype(jnp.float32),
        lax.psum_scatter(
            grad_query_gain.astype(jnp.bfloat16), "expert", scatter_dimension=0, tiled=True
        ).astype(jnp.float32),
        lax.psum_scatter(
            grad_key_gain.astype(jnp.bfloat16), "expert", scatter_dimension=0, tiled=True
        ).astype(jnp.float32),
    )
    query_grad = expert_summed[0]
    out_grad = expert_summed[3]
    reduced = (
        lax.psum_scatter(
            query_grad.astype(jnp.bfloat16), "shard", scatter_dimension=0, tiled=True
        ).astype(jnp.float32),
        lax.psum_scatter(
            expert_summed[1].astype(jnp.bfloat16), "shard", scatter_dimension=0, tiled=True
        ).astype(jnp.float32),
        lax.psum_scatter(
            expert_summed[2].astype(jnp.bfloat16), "shard", scatter_dimension=0, tiled=True
        ).astype(jnp.float32),
        lax.psum_scatter(
            out_grad.astype(jnp.bfloat16), "shard", scatter_dimension=0, tiled=True
        ).astype(jnp.float32),
        lax.psum_scatter(
            expert_summed[4].astype(jnp.bfloat16), "shard", scatter_dimension=0, tiled=True
        ).astype(jnp.float32),
        lax.psum_scatter(
            expert_summed[5].astype(jnp.bfloat16), "shard", scatter_dimension=0, tiled=True
        ).astype(jnp.float32),
        lax.psum_scatter(
            expert_summed[6].astype(jnp.bfloat16), "shard", scatter_dimension=0, tiled=True
        ).astype(jnp.float32),
        lax.psum_scatter(
            expert_summed[7].astype(jnp.bfloat16), "shard", scatter_dimension=0, tiled=True
        ).astype(jnp.float32),
        lax.psum_scatter(
            expert_summed[8].astype(jnp.bfloat16), "shard", scatter_dimension=0, tiled=True
        ).astype(jnp.float32),
    )
    return (
        block_out,
        grad_input,
        reduced[5],
        reduced[0],
        reduced[1],
        reduced[2],
        reduced[7],
        reduced[8],
        reduced[3],
        reduced[6],
        reduced[4],
        grad_wgate[None],
        grad_wup[None],
        grad_wdown[None],
    )


def solution(mesh):
    in_specs = (
        P(("expert", "shard"), None),
        P(("expert", "shard")),
        P(("expert", "shard"), None),
        P(("expert", "shard"), None),
        P(("expert", "shard"), None),
        P(("expert", "shard")),
        P(("expert", "shard")),
        P(("expert", "shard"), None),
        P(("expert", "shard")),
        P(("expert", "shard"), None),
        P(("expert", "shard"), None, None),
        P(("expert", "shard"), None, None),
        P(("expert", "shard"), None, None),
        P(("expert", "shard"), None),
        P(("expert", "shard"), None),
    )
    out_specs = (
        P(("expert", "shard"), None),
        P(("expert", "shard"), None),
        P(("expert", "shard")),
        P(("expert", "shard"), None),
        P(("expert", "shard"), None),
        P(("expert", "shard"), None),
        P(("expert", "shard")),
        P(("expert", "shard")),
        P(("expert", "shard"), None),
        P(("expert", "shard")),
        P(("expert", "shard"), None),
        P(("expert", "shard"), None, None),
        P(("expert", "shard"), None, None),
        P(("expert", "shard"), None, None),
    )
    return jax.shard_map(
        per_device, mesh=mesh, in_specs=in_specs, out_specs=out_specs, check_vma=False
    )
```

profile of v0, /device:TPU:18, one launch (start us, length us, event | category | flops | bytes accessed | tf_op | source)
XLA Modules:
  0.0 2901.9 jit_solution(9193923614473446767)
XLA Ops:
  7.2 14.3 all_gather.71
  21.6 14.9 all_gather.66
  44.0 10.0 all-reduce.23
  55.2 10.9 all-reduce.21
  66.1 9.7 all-gather
  94.8 32.3 %all-gather.12.cloned.1.call-done = bf16[256,4096]{1,0:T(8,128)(2,1)} async-done(((bf16[64,4096]{1,0:T(8,128)(2,1)}), bf16[256,4096]{1,0:T(8,128)(2,1)}) %all-gather.12.cloned.1.call-update) | async-done | bytes 2097168 | tf_op jit(solution)/shard_map/all_gather | solution.py:120
  127.1 45.8 %all-gather.24.cloned.1.call-done = bf16[512,2048]{1,0:T(8,128)(2,1)} async-done(((bf16[128,2048]{1,0:T(8,128)(2,1)}), bf16[512,2048]{1,0:T(8,128)(2,1)}) %all-gather.24.cloned.1.call-update) | async-done | bytes 2097168 | tf_op jit(solution)/shard_map/all_gather | solution.py:123
  185.1 15.9 reduce-window.6
  218.8 13.0 all-gather.18.cloned.1.call-done
  234.1 89.3 %all-gather.14.cloned.1.call-done = bf16[2048,4096]{1,0:T(8,128)(2,1)} async-done(((bf16[256,4096]{1,0:T(8,128)(2,1)}), bf16[2048,4096]{1,0:T(8,128)(2,1)}) %all-gather.14.cloned.1.call-update) | async-done | bytes 16777232 | tf_op jit(solution)/shard_map/all_gather | solution.py:133
  323.4 12.7 fusion.114
  365.4 31.8 %while.28 = (s32[]{:T(128)}, bf16[4,256,8,128]{1,3,2,0:T(8,128)(2,1)}, f32[4,256,8]{1,2,0:T(8,128)}, bf16[4,256,8,128]{3,1,2,0:T(8,128)(2,1)}, bf16[4,1024,128]{...) while((s32[]{:T(128)}, bf16[4,256,8,128]{1,3,2,0:T(8,128)(2,1)}, ...), condition=%wide.region_5.6_spmd.clone, body=%wide.region_3.5_spmd.clone.sunk | while | flops 1084487680 | bytes 36474008 | solution.py:185
  397.2 17.8 all-gather.26.cloned.1.call-done
  415.0 11.2 multiply_reduce_fusion.6
  429.9 32.7 %gather_fusion = bf16[4096,2048]{1,0:T(8,128)(2,1)} fusion(bf16[257,2048]{1,0:T(8,128)(2,1)} %concatenate.31, s32[4096]{0:T(1024)S(1)} %get-tuple-element.239), kind=kCustom, calls=%fused_computation.2 | custom fusion | bytes 33570816 | tf_op jit(solution)/shard_map/jit(_take)/gather | solution.py:209
  462.6 17.0 broadcast_select_fusion.1
  479.6 366.3 %all_to_all.20 = bf16[32,128,2048]{2,1,0:T(8,128)(2,1)S(1)} all-to-all(bf16[32,128,2048]{2,1,0:T(8,128)(2,1)S(1)} %broadcast_select_fusion.1), channel_id=1, replica_groups=mesh['expert'=8,'shard'=4] {'expert','shard'}, dimensions={0} | all-to-all | bytes 33554432 | tf_op jit(solution)/shard_map/all_to_all | solution.py:210
  851.6 16.2 fusion.69
  867.8 24.8 multiply_convert_fusion.3
  892.6 18.9 convolution_convert_fusion
  916.6 368.8 %all-gather.2 = bf16[4,64,32]{1,2,0:T(8,128)(2,1)S(1)} all-gather(bf16[1,64,32]{1,2,0:T(8,128)(2,1)S(1)} %bitcast.347), channel_id=1, replica_groups=mesh['expert'=8,'shard'=4] {'shard'}, dimensions={0}, use_global_device_ids=true | all-gather | bytes 20480 | tf_op jit(solution)/shard_map/all_gather | solution.py:124
  1288.3 15.8 all_gather.79
  1306.5 24.5 gather_fusion.2
  1352.5 35.8 %gather_fusion.1 = bf16[4096,2048]{1,0:T(8,128)(2,1)} fusion(bf16[2049,2048]{1,0:T(8,128)(2,1)} %concatenate.32, s32[4096]{0:T(1024)S(1)} %copy-done.63), kind=kCustom, calls=%fused_computation.3 | custom fusion | bytes 33570816 | tf_op jit(solution)/shard_map/jit(_take)/gather | solution.py:238
  1396.8 368.2 %all_to_all.21 = bf16[32,128,2048]{2,1,0:T(8,128)(2,1)} all-to-all(bf16[32,128,2048]{2,1,0:T(8,128)(2,1)S(1)} %broadcast_select_fusion), channel_id=1, replica_groups=mesh['expert'=8,'shard'=4] {'expert','shard'}, dimensions={0} | all-to-all | bytes 33554432 | tf_op jit(solution)/shard_map/all_to_all | solution.py:241
  1765.0 28.7 multiply_convert_fusion.1
  1793.8 22.8 fusion.67
  1816.6 23.6 add_convert_fusion
  1845.4 371.6 %all-to-all-done.3 = bf16[32,128,2048]{2,1,0:T(8,128)(2,1)} async-done(((bf16[32,128,2048]{2,1,0:T(8,128)(2,1)}), bf16[32,128,2048]{2,1,0:T(8,128)(2,1)}, u32[]{:S(2)}, u32[]{:S(2)}) %all-to-all-start.3) | async-done | bytes 16777248 | tf_op jit(solution)/shard_map/all_to_all | solution.py:256
  2217.0 24.6 gather_fusion.3
  2241.6 17.3 convert_reduce_fusion
  2263.0 10.9 fusion.82
  2275.3 47.8 %while.29 = (s32[]{:T(128)}, f32[4,256,8,128]{3,1,2,0:T(8,128)}, bf16[4,1024,128]{1,2,0:T(8,128)(2,1)}, bf16[4,1024,128]{1,2,0:T(8,128)(2,1)}, bf16[4,256,8,128]...) while((s32[]{:T(128)}, f32[4,256,8,128]{3,1,2,0:T(8,128)}, ...), condition=%wide.region_21.23_spmd.clone, body=%wide.region_19.22_spmd.clone.sunk | while | flops 2701391872 | bytes 97827112 | solution.py:287
  2324.7 23.4 reduce-scatter.15.cloned.1.call-done
  2356.1 20.0 reduce-scatter.17.cloned.1.call-done
  2379.3 33.9 %reduce-scatter.35.cloned.1.call-done = bf16[256,32]{0,1:T(8,128)(2,1)} async-done(((bf16[2048,32]{0,1:T(8,128)(2,1)}), bf16[256,32]{0,1:T(8,128)(2,1)}) %reduce-scatter.35.cloned.1.call-update) | async-done | bytes 16400 | tf_op jit(solution)/shard_map/reduce_scatter | solution.py:326
  2414.8 10.2 convolution_convert_fusion.1
  2457.6 44.3 %reduce-scatter.27.cloned.1.call-done = bf16[256,512]{1,0:T(8,128)(2,1)} async-done(((bf16[2048,512]{1,0:T(8,128)(2,1)}), bf16[256,512]{1,0:T(8,128)(2,1)}) %reduce-scatter.27.cloned.1.call-update) | async-done | bytes 262160 | tf_op jit(solution)/shard_map/reduce_scatter | solution.py:320
  2504.6 17.5 reduce-scatter.37.cloned.1.call-done
  2523.5 118.3 %reduce-scatter.31.cloned.1.call-done = bf16[512,2048]{1,0:T(8,128)(2,1)} async-done(((bf16[4096,2048]{1,0:T(8,128)(2,1)}), bf16[512,2048]{1,0:T(8,128)(2,1)}) %reduce-scatter.31.cloned.1.call-update) | async-done | bytes 2097168 | tf_op jit(solution)/shard_map/reduce_scatter | solution.py:323
  2641.8 21.1 convolution_bitcast_fusion.3
  2662.9 23.7 convolution_bitcast_fusion.4
  2686.6 74.8 %reduce-scatter.19.cloned.1.call-done = bf16[256,4096]{1,0:T(8,128)(2,1)} async-done(((bf16[2048,4096]{1,0:T(8,128)(2,1)}), bf16[256,4096]{1,0:T(8,128)(2,1)}) %reduce-scatter.19.cloned.1.call-update) | async-done | bytes 2097168 | tf_op jit(solution)/shard_map/reduce_scatter | solution.py:314
  2761.4 20.6 convolution_bitcast_fusion.2
  2782.0 9.6 fusion.122
  2797.2 10.5 all-reduce.20
  2827.1 20.4 reduce-scatter.33.cloned.1.call-done
  2849.6 42.9 %reduce-scatter.21.cloned.1.call-done = bf16[64,4096]{1,0:T(8,128)(2,1)} async-done(((bf16[256,4096]{1,0:T(8,128)(2,1)}), bf16[64,4096]{1,0:T(8,128)(2,1)}) %reduce-scatter.21.cloned.1.call-update) | async-done | bytes 524304 | tf_op jit(solution)/shard_map/reduce_scatter | solution.py:345
  (459 shorter events, 302.7 us)
Async XLA Ops:
  7.2 885.4 %copy-start = (bf16[1,768,2048]{2,1,0:T(8,128)(2,1)S(1)}, bf16[1,768,2048]{2,1,0:T(8,128)(2,1)}, u32[]{:S(2)}) copy-start(bf16[1,768,2048]{2,1,0:T(8,128)(2,1)} %param.33) | copy-start | bytes 9437188
  7.2 73.2 %all-gather.20.cloned.1.call-start = ((), (), s32[]{:S(2)}) async-start(), calls=%async_computation.20 | async-start | bytes 2359296 | tf_op jit(solution)/shard_map/all_gather | solution.py:135
  21.6 62.3 %all-gather.16.cloned.1.call-start = ((), (), s32[]{:S(2)}) async-start(), calls=%async_computation.18 | async-start | bytes 2359296 | tf_op jit(solution)/shard_map/all_gather | solution.py:134
  36.6 90.5 %all-gather.12.cloned.1.call-start = ((), (), s32[]{:S(2)}) async-start(), calls=%async_computation.16 | async-start | bytes 2621440 | tf_op jit(solution)/shard_map/all_gather | solution.py:120
  37.3 135.7 %all-gather.24.cloned.1.call-start = ((), (), s32[]{:S(2)}) async-start(), calls=%async_computation.22 | async-start | bytes 2621440 | tf_op jit(solution)/shard_map/all_gather | solution.py:123
  37.9 178.5 %all-gather.22.cloned.1.call-start = ((), (), s32[]{:S(2)}) async-start(), calls=%async_computation.21 | async-start | bytes 1310720 | tf_op jit(solution)/shard_map/all_gather | solution.py:176
  75.8 247.6 %copy-start.42 = (f32[8,1,256]{2,1,0:T(1,128)}, f32[8,1,256]{2,1,0:T(1,128)S(1)}, u32[]{:S(2)}) copy-start(f32[8,1,256]{2,1,0:T(1,128)S(1)} %convert_element_type.284) | copy-start | bytes 24580
  76.9 282.6 %copy-start.22 = (f32[256,128]{1,0:T(8,128)}, f32[256,128]{1,0:T(8,128)S(1)}, u32[]{:S(2)}) copy-start(f32[256,128]{1,0:T(8,128)S(1)} %copy.151) | copy-start | bytes 393220
  83.8 147.9 %all-gather.18.cloned.1.call-start = ((), (), s32[]{:S(2)}) async-start(), calls=%async_computation.19 | async-start | bytes 1310720 | tf_op jit(solution)/shard_map/all_gather | solution.py:175
  93.3 79.7 %copy-start.50 = (s32[256,8]{0,1:T(8,128)S(1)}, s32[256,8]{0,1:T(8,128)}, u32[]{:S(2)}) copy-start(s32[256,8]{0,1:T(8,128)} %param.34) | copy-start | bytes 24580
  93.3 80.1 %copy-start.85 = (bf16[128]{0:T(256)(128)(2,1)S(1)}, bf16[128]{0:T(256)(128)(2,1)}, u32[]{:S(2)}) copy-start(bf16[128]{0:T(256)(128)(2,1)} %get-tuple-element.200) | copy-start | bytes 772
  93.3 80.7 %copy-start.84 = (bf16[256]{0:T(256)(128)(2,1)S(1)}, bf16[256]{0:T(256)(128)(2,1)}, u32[]{:S(2)}) copy-start(bf16[256]{0:T(256)(128)(2,1)} %get-tuple-element.209) | copy-start | bytes 1540
  94.8 228.6 %all-gather.14.cloned.1.call-start = ((), (), s32[]{:S(2)}) async-start(), calls=%async_computation.17 | async-start | bytes 18874368 | tf_op jit(solution)/shard_map/all_gather | solution.py:133
  127.1 287.9 %all-gather.26.cloned.1.call-start = ((), (), s32[]{:S(2)}) async-start(), calls=%async_computation.23 | async-start | bytes 18874368 | tf_op jit(solution)/shard_map/all_gather | solution.py:136
  173.3 162.8 %copy-start.46 = (s32[2048]{0:T(1024)}, s32[2048]{0:T(1024)S(1)}, u32[]{:S(2)}) copy-start(s32[2048]{0:T(1024)S(1)} %eq.44) | copy-start | bytes 24580
  206.0 117.4 %copy-start.65 = (f32[256]{0:T(256)S(1)}, f32[256]{0:T(256)}, u32[]{:S(2)}) copy-start(f32[256]{0:T(256)} %copy-done.64) | copy-start | bytes 3076
  397.2 29.0 copy-start.55
  426.9 35.7 %copy-start.72 = (f32[256]{0:T(256)}, f32[256]{0:T(256)S(1)}, u32[]{:S(2)}) copy-start(f32[256]{0:T(256)S(1)} %get-tuple-element.245) | copy-start | bytes 3076
  479.6 372.0 %copy-start.82 = (bf16[1,2048,768]{2,1,0:T(8,128)(2,1)S(1)}, bf16[1,2048,768]{2,1,0:T(8,128)(2,1)}, u32[]{:S(2)}) copy-start(bf16[1,2048,768]{2,1,0:T(8,128)(2,1)} %param.31) | copy-start | bytes 9437188
  911.5 392.6 %copy-start.47 = (s32[2048]{0:T(1024)S(1)}, s32[2048]{0:T(1024)}, u32[]{:S(2)}) copy-start(s32[2048]{0:T(1024)} %copy-done.46) | copy-start | bytes 24580
  911.5 392.6 %copy-start.49 = (s32[2048]{0:T(1024)S(1)}, s32[2048]{0:T(1024)}, u32[]{:S(2)}) copy-start(s32[2048]{0:T(1024)} %copy-done.48) | copy-start | bytes 24580
  911.5 395.0 %all-to-all-start.1 = ((bf16[32,128,2048]{2,1,0:T(8,128)(2,1)}), bf16[32,128,2048]{2,1,0:T(8,128)(2,1)}, u32[]{:S(2)}, u32[]{:S(2)}) async-start(bf16[32,128,2048]{2,1,0:T(8,128)(2,1)} %bitcast.313), calls=%async_computation.1 | async-start | bytes 33554432 | tf_op jit(solution)/shard_map/all_to_all | solution.py:224
  916.6 389.9 %copy-start.51 = (s32[256,8]{0,1:T(8,128)S(1)}, s32[256,8]{0,1:T(8,128)}, u32[]{:S(2)}) copy-start(s32[256,8]{0,1:T(8,128)} %param.34) | copy-start | bytes 24580
  1304.1 26.9 copy-start.68
  1304.8 26.3 copy-start.57
  1352.5 35.8 %copy-start.70 = (pred[32,128]{1,0:T(8,128)(4,1)S(1)}, pred[32,128]{1,0:T(8,128)(4,1)}, u32[]{:S(2)}) copy-start(pred[32,128]{1,0:T(8,128)(4,1)} %get-tuple-element.236) | copy-start | bytes 12292
  1840.3 376.7 %copy-start.58 = (s32[2048]{0:T(1024)S(1)}, s32[2048]{0:T(1024)}, u32[]{:S(2)}) copy-start(s32[2048]{0:T(1024)} %copy-done.57) | copy-start | bytes 24580
  1840.3 376.7 %all-to-all-start.3 = ((bf16[32,128,2048]{2,1,0:T(8,128)(2,1)}), bf16[32,128,2048]{2,1,0:T(8,128)(2,1)}, u32[]{:S(2)}, u32[]{:S(2)}) async-start(bf16[32,128,2048]{2,1,0:T(8,128)(2,1)} %bitcast.314), calls=%async_computation.3 | async-start | bytes 33554432 | tf_op jit(solution)/shard_map/all_to_all | solution.py:256
  1845.2 502.9 %reduce-scatter.15.cloned.1.call-start = ((), (), s32[]{:S(2)}) async-start(), calls=%async_computation.24 | async-start | bytes 1310720 | tf_op jit(solution)/shard_map/reduce_scatter | solution.py:294
  2275.2 48.5 %copy-start.12 = (bf16[256,2048]{1,0:T(8,128)(2,1)S(1)}, bf16[256,2048]{1,0:T(8,128)(2,1)}, u32[]{:S(2)}) copy-start(bf16[256,2048]{1,0:T(8,128)(2,1)} %copy-done.11) | copy-start | bytes 3145732
  2323.0 26.2 copy-start.26
  2323.0 26.8 copy-start.14
  2323.0 26.8 copy-start.21
  2323.0 26.8 copy-start.23
  2323.1 53.0 %reduce-scatter.17.cloned.1.call-start = ((), (), s32[]{:S(2)}) async-start(), calls=%async_computation.25 | async-start | bytes 1310720 | tf_op jit(solution)/shard_map/reduce_scatter | solution.py:297
  2323.7 89.6 %reduce-scatter.35.cloned.1.call-start = ((), (), s32[]{:S(2)}) async-start(), calls=%async_computation.34 | async-start | bytes 147456 | tf_op jit(solution)/shard_map/reduce_scatter | solution.py:326
  2324.7 132.8 %reduce-scatter.23.cloned.1.call-start = ((), (), s32[]{:S(2)}) async-start(), calls=%async_computation.28 | async-start | bytes 2359296 | tf_op jit(solution)/shard_map/reduce_scatter | solution.py:317
  2356.0 58.8 %copy-start.8 = (f32[256,2048]{1,0:T(8,128)S(1)}, f32[256,2048]{1,0:T(8,128)}, u32[]{:S(2)}) copy-start(f32[256,2048]{1,0:T(8,128)} %get-tuple-element.224) | copy-start | bytes 6291460
  2356.0 145.9 %reduce-scatter.27.cloned.1.call-start = ((), (), s32[]{:S(2)}) async-start(), calls=%async_computation.30 | async-start | bytes 2359296 | tf_op jit(solution)/shard_map/reduce_scatter | solution.py:320
  2379.3 142.8 %reduce-scatter.37.cloned.1.call-start = ((), (), s32[]{:S(2)}) async-start(), calls=%async_computation.35 | async-start | bytes 81920
  2414.7 227.0 %reduce-scatter.31.cloned.1.call-start = ((), (), s32[]{:S(2)}) async-start(), calls=%async_computation.32 | async-start | bytes 18874368 | tf_op jit(solution)/shard_map/reduce_scatter | solution.py:323
  2425.1 336.3 %reduce-scatter.19.cloned.1.call-start = ((), (), s32[]{:S(2)}) async-start(), calls=%async_computation.26 | async-start | bytes 18874368 | tf_op jit(solution)/shard_map/reduce_scatter | solution.py:314
  2449.4 374.6 %reduce-scatter.25.cloned.1.call-start = ((), (), s32[]{:S(2)}) async-start(), calls=%async_computation.29 | async-start | bytes 327680 | tf_op jit(solution)/shard_map/reduce_scatter | solution.py:348
  2457.6 368.0 %reduce-scatter.29.cloned.1.call-start = ((), (), s32[]{:S(2)}) async-start(), calls=%async_computation.31 | async-start | bytes 327680 | tf_op jit(solution)/shard_map/reduce_scatter | solution.py:351
  2502.0 345.5 %reduce-scatter.33.cloned.1.call-start = ((), (), s32[]{:S(2)}) async-start(), calls=%async_computation.33 | async-start | bytes 2621440 | tf_op jit(solution)/shard_map/reduce_scatter | solution.py:354
  2641.8 250.7 %reduce-scatter.21.cloned.1.call-start = ((), (), s32[]{:S(2)}) async-start(), calls=%async_computation.27 | async-start | bytes 2621440 | tf_op jit(solution)/shard_map/reduce_scatter | solution.py:345
  2794.8 25.0 copy-start.79
  2819.8 74.8 %copy-start.1 = (bf16[1,768,2048]{2,1,0:T(8,128)(2,1)S(1)}, bf16[1,768,2048]{2,1,0:T(8,128)(2,1)}, u32[]{:S(2)}) copy-start(bf16[1,768,2048]{2,1,0:T(8,128)(2,1)} %param.33) | copy-start | bytes 9437188
  (84 other events, 414.8 us)
Sparse Core Ops, SparseCore 0:
  21.7 29.4 all-gather.19
  53.1 27.8 all-gather.15
  82.6 44.4 all-gather.11
  128.5 44.4 all-gather.23
  175.0 27.3 all-gather.21
  204.4 27.3 all-gather.17
  233.7 89.7 all-gather.13
  325.3 89.7 all-gather.25
  2323.2 24.8 reduce-scatter.14
  2350.3 25.7 reduce-scatter.16
  2379.7 33.5 reduce-scatter.34
  2416.4 41.0 reduce-scatter.22
  2460.8 41.0 reduce-scatter.26
  2504.6 17.4 reduce-scatter.36
  2525.5 116.2 reduce-scatter.30
  2645.2 116.1 reduce-scatter.18
  2763.5 18.2 reduce-scatter.24
  2783.9 18.2 reduce-scatter.28
  2804.4 43.0 reduce-scatter.32
  2849.6 42.8 reduce-scatter.20
where the time goes:
time: 2910 us; the launch traced here: 2900 us
  blocking collectives  1210 us (42%)
  waiting for transfers between devices  975 us (34%)
  matrix products  347 us (12%)
  local copies, waits for them, and re-layouts  205 us (7%)
  other arithmetic  134 us (5%)
    all_to_all x1, waiting for transfers between devices, per_device(): lax.all_to_all(grad_rows.reshape(expert_count, capacity, model_width), ('...  372 us
    all_gather x1, blocking collectives, per_device(): lax.all_gather(w_router, 'shard', axis=0, tiled=True)  369 us
    all_to_all x1, blocking collectives, per_device(): lax.all_to_all(grad_outgoing, ('expert', 'shard'), split_axis=0, concat_a...  368 us
    all_to_all x1, blocking collectives, per_device(): lax.all_to_all(outgoing, ('expert', 'shard'), split_axis=0, concat_axis=0...  366 us
    reduce_scatter x1, waiting for transfers between devices, per_device(): lax.psum_scatter(grad_wout.astype(jnp.bfloat16), 'expert', scatter_dimens...  118 us
    dot_general x8, matrix products, matmul_nt(): lax.dot_general(left, right, (((1,), (1,)), ((), ())), preferred_element_...  103 us
    dot_general x8, matrix products, matmul(): return jnp.dot(left, right, preferred_element_type=jnp.float32)  92.4 us
    dot_general x8, matrix products, matmul_tn(): lax.dot_general(left, right, (((0,), (0,)), ((), ())), preferred_element_...  90.2 us
  transfers between devices with their start and end apart: 22, of which 16 were waited for; matrix products, arithmetic and copies ran while one was open for 9% of the time, Pallas kernels for 0%

commit v1 on v0

v1 whole, which is shorter than its diff:
```python
import functools

import jax
import jax.numpy as jnp
from jax import lax
from jax.experimental import pallas as pl
from jax.experimental.pallas import tpu as pltpu
from jax.sharding import PartitionSpec as P

MESH = pl.DeviceIdType.MESH
NZ = 4

def placed():
    return lax.axis_size("expert") == 8 and lax.axis_size("shard") == NZ

def place():
    e = lax.axis_index("expert"); s = lax.axis_index("shard")
    return e // 4, lax.rem(e // 2, 2), lax.rem(e, 2), s

def dev(y, x, c, s):
    return (y * 4 + x * 2 + c, s)

def barrier_all(y, x, c, s):
    bar = pltpu.get_barrier_semaphore()
    def sig(d): pl.semaphore_signal(bar, inc=1, device_id=d, device_id_type=MESH)
    sig(dev(1 - y, x, c, s)); sig(dev(y, 1 - x, c, s)); sig(dev(y, x, 1 - c, s))
    @pl.when(s > 0)
    def _(): sig(dev(y, x, c, s - 1))
    @pl.when(s < NZ - 1)
    def _(): sig(dev(y, x, c, s + 1))
    pl.semaphore_wait(bar, 3 + jnp.where(s > 0, 1, 0) + jnp.where(s < NZ - 1, 1, 0))

def ag_kernel(n_arr, *refs):
    ins = refs[:n_arr]; outs = refs[n_arr:2 * n_arr]
    loc_sem, zs, zr, ps, pr, cs, cr = refs[2 * n_arr:]
    y, x, c, s = place()
    barrier_all(y, x, c, s)
    def rc(src, dst, ss, rs, d):
        return pltpu.make_async_remote_copy(src_ref=src, dst_ref=dst, send_sem=ss, recv_sem=rs, device_id=d, device_id_type=MESH)
    X = dev(y, 1 - x, c, s); Y = dev(1 - y, x, c, s); C = dev(y, x, 1 - c, s)
    A = range(n_arr)
    steps = [(0, 0)] + [(d, g) for d in range(1, NZ) for g in (1, -1)]
    def valid(d, g):
        return (s >= d) if g == 1 else (s + d <= NZ - 1)
    def zof(d, g): return s - d * g
    def src_own(a, h, zz, k):
        return ins[a].at[h] if k == 0 else outs[a].at[y, x, c, zz, h]
    def zcopy(a, h, zz, k, g):
        kk = 1 + 2 * (k_dist(k)) + (0 if g == 1 else 1)
        return rc(src_own(a, h, zz, k), outs[a].at[y, x, c, zz, h], zs.at[a, h, kk], zr.at[a, h, kk], dev(y, x, c, s + g))
    def k_dist(k): return steps[k][0]
    def plane(a, h, zz, k, which):
        return rc(src_own(a, h, zz, k), outs[a].at[y, x, c, zz, h], ps.at[a, k, h, which], pr.at[a, k, h, which], X if which == 0 else Y)
    def plane_recv(a, h, zz, k, which):
        d = outs[a].at[y, 1 - x, c, zz, h] if which == 0 else outs[a].at[1 - y, x, c, zz, h]
        return rc(d, d, ps.at[a, k, h, which], pr.at[a, k, h, which], X if which == 0 else Y)
    def diag(a, h, zz, k):
        d = outs[a].at[y, 1 - x, c, zz, h] if h == 0 else outs[a].at[1 - y, x, c, zz, h]
        return rc(d, d, ps.at[a, k, h, 2], pr.at[a, k, h, 2], Y if h == 0 else X)
    def diag_recv(a, h, zz, k):
        d = outs[a].at[1 - y, 1 - x, c, zz, h]
        return rc(d, d, ps.at[a, k, h, 2], pr.at[a, k, h, 2], Y if h == 0 else X)
    def core(a, zz, k, part):
        d = outs[a].at[:, :, c, zz]
        return rc(d, d, cs.at[a, k], cr.at[a, k], C)
    def core_recv(a, zz, k):
        d = outs[a].at[:, :, 1 - c, zz]
        return rc(d, d, cs.at[a, k], cr.at[a, k], C)
    def loc(a):
        return pltpu.make_async_copy(ins[a], outs[a].at[y, x, c, s], loc_sem.at[a])

    def when(k, f):
        d, g = steps[k]
        if k == 0: f()
        else: pl.when(valid(d, g))(f)

    def stage_a(k):
        d, g = steps[k]
        def go():
            zz = zof(d, g)
            for a in A:
                for h in range(2):
                    if k:
                        kk = k
                        dref = outs[a].at[y, x, c, zz, h]
                        rc(dref, dref, zs.at[a, h, kk], zr.at[a, h, kk], X).wait_recv()
                    for gg in ((1, -1) if k == 0 else (g,)):
                        okc = (s < NZ - 1) if gg == 1 else (s > 0)
                        if d + 1 < NZ:
                            @pl.when(okc)
                            def _(): zcopy(a, h, zz, k, gg).start()
                    plane(a, h, zz, k, 0).start()
                    plane(a, h, zz, k, 1).start()
        when(k, go)
    def stage_b(k):
        d, g = steps[k]
        def go():
            zz = zof(d, g)
            for a in A:
                plane_recv(a, 0, zz, k, 0).wait_recv()
                diag(a, 0, zz, k).start()
                plane_recv(a, 1, zz, k, 1).wait_recv()
                diag(a, 1, zz, k).start()
        when(k, go)
    def stage_c(k):
        d, g = steps[k]
        def go():
            zz = zof(d, g)
            for a in A:
                if k == 0: loc(a).wait()
                plane_recv(a, 1, zz, k, 0).wait_recv()
                plane_recv(a, 0, zz, k, 1).wait_recv()
                diag_recv(a, 0, zz, k).wait_recv()
                diag_recv(a, 1, zz, k).wait_recv()
                core(a, zz, k, 0).start()
        when(k, go)
    for a in A: loc(a).start()
    n = len(steps)
    for i in range(n + 2):
        if i < n: stage_a(i)
        if 0 <= i - 1 < n: stage_b(i - 1)
        if 0 <= i - 2 < n: stage_c(i - 2)
    for k in range(n):
        d, g = steps[k]
        def go():
            zz = zof(d, g)
            for a in A:
                core_recv(a, zz, k).wait_recv()
                core(a, zz, k, 0).wait_send()
                for h in range(2):
                    for gg in ((1, -1) if k == 0 else (g,)):
                        okc = (s < NZ - 1) if gg == 1 else (s > 0)
                        if d + 1 < NZ:
                            @pl.when(okc)
                            def _(): zcopy(a, h, zz, k, gg).wait_send()
                    plane(a, h, zz, k, 0).wait_send()
                    plane(a, h, zz, k, 1).wait_send()
                    diag(a, h, zz, k).wait_send()
        when(k, go)

def ag32(arrs, cid):
    ins = [a.reshape(2, a.shape[0] // 2, a.shape[1]) for a in arrs]
    n = len(ins); nk = 7
    outs = pl.pallas_call(
        functools.partial(ag_kernel, n),
        out_shape=[jax.ShapeDtypeStruct((2, 2, 2, NZ) + a.shape, a.dtype) for a in ins],
        in_specs=[pl.BlockSpec(memory_space=pltpu.VMEM)] * n,
        out_specs=[pl.BlockSpec(memory_space=pl.ANY)] * n,
        scratch_shapes=[pltpu.SemaphoreType.DMA((n,)),
            pltpu.SemaphoreType.DMA((n, 2, 9)), pltpu.SemaphoreType.DMA((n, 2, 9)),
            pltpu.SemaphoreType.DMA((n, nk, 2, 3)), pltpu.SemaphoreType.DMA((n, nk, 2, 3)),
            pltpu.SemaphoreType.DMA((n, nk)), pltpu.SemaphoreType.DMA((n, nk))],
        compiler_params=pltpu.CompilerParams(collective_id=cid, has_side_effects=True, vmem_limit_bytes=8 << 20),
        name="gather_all",
    )(*ins)
    return [o.reshape(32, a.shape[0], a.shape[1]) for o, a in zip(outs, arrs)]

ZORDER = (0, 3, 1, 2)

def rs_kernel(n_arr, *refs):
    ins = refs[:n_arr]; outs = refs[n_arr:2 * n_arr]
    sc = refs[2 * n_arr:]
    own_b = sc[:n_arr]; r0_b = sc[n_arr:2 * n_arr]; ra_b = sc[2 * n_arr:3 * n_arr]; rb_b = sc[3 * n_arr:4 * n_arr]; zu_b = sc[4 * n_arr:5 * n_arr]; zd_b = sc[5 * n_arr:6 * n_arr]
    lsem, s0s, s0r, sas, sar, sbs, sbr, zus, zur, zds, zdr = sc[6 * n_arr:]
    y, x, c, s = place()
    barrier_all(y, x, c, s)
    X = dev(y, 1 - x, c, s); Y = dev(1 - y, x, c, s); C = dev(y, x, 1 - c, s)
    UP = dev(y, x, c, s + 1); DN = dev(y, x, c, s - 1)
    def rc(src, dst, ss, rs, d):
        return pltpu.make_async_remote_copy(src_ref=src, dst_ref=dst, send_sem=ss, recv_sem=rs, device_id=d, device_id_type=MESH)
    units = [(a, zz, h) for zz in ZORDER for a in range(n_arr) for h in range(2)]
    def jj(zz, h): return ZORDER.index(zz) * 2 + h
    def load(a, zz, h):
        j = jj(zz, h)
        return pltpu.make_async_copy(ins[a].at[:, :, c, zz, h], own_b[a].at[j], lsem.at[a, j])
    def c0(a, zz, h):
        j = jj(zz, h)
        return rc(ins[a].at[:, :, 1 - c, zz, h], r0_b[a].at[j], s0s.at[a, j], s0r.at[a, j], C)
    def ca(a, zz, h):
        j = jj(zz, h)
        if h == 0: return rc(own_b[a].at[j, :, 1 - x], ra_b[a].at[j], sas.at[a, j], sar.at[a, j], X)
        return rc(own_b[a].at[j, 1 - y], ra_b[a].at[j], sas.at[a, j], sar.at[a, j], Y)
    def cb(a, zz, h):
        j = jj(zz, h)
        if h == 0: return rc(own_b[a].at[j, 1 - y, x], rb_b[a].at[j], sbs.at[a, j], sbr.at[a, j], Y)
        return rc(own_b[a].at[j, y, 1 - x], rb_b[a].at[j], sbs.at[a, j], sbr.at[a, j], X)
    def cu(a, zz, h):
        j = jj(zz, h)
        return rc(own_b[a].at[j, y, x], zu_b[a].at[j], zus.at[a, j], zur.at[a, j], UP)
    def cd(a, zz, h):
        j = jj(zz, h)
        return rc(own_b[a].at[j, y, x], zd_b[a].at[j], zds.at[a, j], zdr.at[a, j], DN)
    def add_into(dst, other):
        rows = dst.shape[0]
        st = 16 if rows % 16 == 0 else rows
        @pl.loop(0, rows // st)
        def _(i):
            r = pl.ds(i * st, st)
            dst[r, :] = (dst[r, :].astype(jnp.float32) + other[r, :].astype(jnp.float32)).astype(dst.dtype)
    def stage0(u):
        a, zz, h = u; j = jj(zz, h)
        load(a, zz, h).wait()
        c0(a, zz, h).wait_recv()
        for yy in range(2):
            for xx in range(2):
                add_into(own_b[a].at[j, yy, xx], r0_b[a].at[j, yy, xx])
        ca(a, zz, h).start()
    def stage1(u):
        a, zz, h = u; j = jj(zz, h)
        ca(a, zz, h).wait_recv()
        for q in range(2):
            if h == 0: add_into(own_b[a].at[j, q, x], ra_b[a].at[j, q])
            else: add_into(own_b[a].at[j, y, q], ra_b[a].at[j, q])
        cb(a, zz, h).start()
    def zflow(u):
        a, zz, h = u; j = jj(zz, h)
        mine = own_b[a].at[j, y, x]
        if zz > 0:
            @pl.when(jnp.logical_and(s > 0, s <= zz))
            def _():
                cu(a, zz, h).wait_recv()
                add_into(mine, zu_b[a].at[j])
            @pl.when(s < zz)
            def _(): cu(a, zz, h).start()
        if zz < NZ - 1:
            @pl.when(jnp.logical_and(s < NZ - 1, s >= zz))
            def _():
                cd(a, zz, h).wait_recv()
                add_into(mine, zd_b[a].at[j])
            @pl.when(s > zz)
            def _(): cd(a, zz, h).start()
        @pl.when(s == zz)
        def _(): outs[a][h] = mine[...].astype(outs[a].dtype)
    def stage2(u):
        a, zz, h = u; j = jj(zz, h)
        cb(a, zz, h).wait_recv()
        add_into(own_b[a].at[j, y, x], rb_b[a].at[j])
    for u in units:
        c0(*u).start(); load(*u).start()
    n = len(units)
    L1, L2, L3 = 2, 4, 5
    for i in range(n + L3):
        if i < n: stage0(units[i])
        if 0 <= i - L1 < n: stage1(units[i - L1])
        if 0 <= i - L2 < n: stage2(units[i - L2])
        if 0 <= i - L3 < n: zflow(units[i - L3])
    for u in units:
        c0(*u).wait_send(); ca(*u).wait_send(); cb(*u).wait_send()
        zz = u[1]
        if zz > 0:
            @pl.when(s < zz)
            def _(): cu(*u).wait_send()
        if zz < NZ - 1:
            @pl.when(s > zz)
            def _(): cd(*u).wait_send()

def rs32(arrs, cid, out_dtype=jnp.float32):
    n = len(arrs)
    ins = [a.reshape(2, 2, 2, NZ, 2, a.shape[1] // 2, a.shape[2]) for a in arrs]
    hs = [i.shape[-2:] for i in ins]
    V = pltpu.VMEM; bt = jnp.bfloat16
    sems = [pltpu.SemaphoreType.DMA((n, 8))] * 11
    outs = pl.pallas_call(
        functools.partial(rs_kernel, n),
        out_shape=[jax.ShapeDtypeStruct((2,) + h, out_dtype) for h in hs],
        in_specs=[pl.BlockSpec(memory_space=pl.ANY)] * n,
        out_specs=[pl.BlockSpec(memory_space=pltpu.VMEM)] * n,
        scratch_shapes=[V((8, 2, 2) + h, bt) for h in hs] + [V((8, 2, 2) + h, bt) for h in hs] + [V((8, 2) + h, bt) for h in hs]
            + [V((8,) + h, bt) for h in hs] + [V((8,) + h, bt) for h in hs] + [V((8,) + h, bt) for h in hs] + sems,
        compiler_params=pltpu.CompilerParams(collective_id=cid, has_side_effects=True, vmem_limit_bytes=64000 * 1024),
        name="scatter_all",
    )(*ins)
    return [o.reshape(a.shape[1], a.shape[2]) for o, a in zip(outs, arrs)]

def line_gather_kernel(x_ref, o_ref, ss, rs):
    y, x, c, s = place()
    bar = pltpu.get_barrier_semaphore()
    for k in range(1, NZ):
        pl.semaphore_signal(bar, inc=1, device_id=dev(y, x, c, lax.rem(s + k, NZ)), device_id_type=MESH)
    pl.semaphore_wait(bar, NZ - 1)
    def cp(k):
        return pltpu.make_async_remote_copy(src_ref=x_ref, dst_ref=o_ref.at[s], send_sem=ss.at[k], recv_sem=rs.at[k],
            device_id=dev(y, x, c, lax.rem(s + k, NZ)), device_id_type=MESH)
    def back(k):
        t = lax.rem(s + NZ - k, NZ)
        return pltpu.make_async_remote_copy(src_ref=x_ref, dst_ref=o_ref.at[t], send_sem=ss.at[k], recv_sem=rs.at[k],
            device_id=dev(y, x, c, t), device_id_type=MESH)
    for k in (2, 1, 3): cp(k).start()
    o_ref[s] = x_ref[...]
    for k in range(1, NZ): back(k).wait_recv()
    for k in range(1, NZ): cp(k).wait_send()

def line_gather(x, cid):
    if not placed():
        return lax.all_gather(x, "shard", axis=0, tiled=True)
    sem = pltpu.SemaphoreType.DMA((NZ,))
    o = pl.pallas_call(line_gather_kernel, out_shape=jax.ShapeDtypeStruct((NZ,) + x.shape, x.dtype),
        in_specs=[pl.BlockSpec(memory_space=pltpu.VMEM)], out_specs=pl.BlockSpec(memory_space=pltpu.VMEM),
        scratch_shapes=[sem, sem], compiler_params=pltpu.CompilerParams(collective_id=cid, has_side_effects=True, vmem_limit_bytes=16 << 20),
        name="line_gather")(x)
    return o.reshape(NZ * x.shape[0], x.shape[1])

def line_scatter_kernel(p_ref, o_ref, buf, ss, rs):
    y, x, c, s = place()
    bar = pltpu.get_barrier_semaphore()
    for k in range(1, NZ):
        pl.semaphore_signal(bar, inc=1, device_id=dev(y, x, c, lax.rem(s + k, NZ)), device_id_type=MESH)
    pl.semaphore_wait(bar, NZ - 1)
    def cp(k):
        t = lax.rem(s + k, NZ)
        return pltpu.make_async_remote_copy(src_ref=p_ref.at[t], dst_ref=buf.at[k], send_sem=ss.at[k], recv_sem=rs.at[k],
            device_id=dev(y, x, c, t), device_id_type=MESH)
    for k in (2, 1, 3): cp(k).start()
    for k in (1, 3, 2): cp(k).wait_recv()
    st = 32
    @pl.loop(0, o_ref.shape[0] // st)
    def _(i):
        r = pl.ds(i * st, st)
        t = p_ref[s, r, :].astype(jnp.float32)
        for k in range(1, NZ): t = t + buf[k, r, :].astype(jnp.float32)
        o_ref[r, :] = t
    for k in range(1, NZ): cp(k).wait_send()

def line_scatter(p, cid):
    if not placed():
        return lax.psum_scatter(p, "shard", scatter_dimension=0, tiled=True).astype(jnp.float32)
    R, C = p.shape[0] // NZ, p.shape[1]
    sem = pltpu.SemaphoreType.DMA((NZ,))
    return pl.pallas_call(line_scatter_kernel, out_shape=jax.ShapeDtypeStruct((R, C), jnp.float32),
        in_specs=[pl.BlockSpec(memory_space=pltpu.VMEM)], out_specs=pl.BlockSpec(memory_space=pltpu.VMEM),
        scratch_shapes=[pltpu.VMEM((NZ, R, C), p.dtype), sem, sem], compiler_params=pltpu.CompilerParams(collective_id=cid, has_side_effects=True, vmem_limit_bytes=16 << 20),
        name="line_scatter")(p.reshape(NZ, R, C))


def dot(a, b, ca, cb):
    return lax.dot_general(a, b, (((ca,), (cb,)), ((), ())), preferred_element_type=jnp.float32)

def expert_kernel(experts, slots, SB, x_ref, cot_ref, wg_hbm, wu_hbm, wd_hbm, out_ref, gr_ref, dwg_hbm, dwu_hbm, dwd_hbm,
                  wg, wu, wd, dwg, dwu, dwd, rows, gp, wsem, osem):
    bf = jnp.bfloat16
    step = pl.program_id(0)
    nsub = x_ref.shape[0] // SB
    D = cot_ref.shape[1]
    WM = x_ref.shape[1] - D
    me = lax.axis_index(("expert", "shard"))
    loads = [pltpu.make_async_copy(h.at[0], v, wsem.at[i]) for i, (h, v) in enumerate(((wg_hbm, wg), (wu_hbm, wu), (wd_hbm, wd)))]
    @pl.when(step == 0)
    def _():
        for l in loads: l.start()
        for a in (dwg, dwu, dwd): a[...] = jnp.zeros_like(a)
    tri = (lax.broadcasted_iota(jnp.int32, (SB, SB), 1) < lax.broadcasted_iota(jnp.int32, (SB, SB), 0)).astype(bf)
    lane = lax.broadcasted_iota(jnp.int32, (SB, WM), 1)
    picks, gates = [], []
    for i in range(nsub):
        r = pl.ds(i * SB, SB)
        meta = x_ref[r, D:]
        cnt = dot(tri, meta, 1, 0)
        metaf = meta.astype(jnp.float32)
        msk = jnp.sum(jnp.where(lane == me, metaf, 0.0), axis=-1, keepdims=True)
        pos = jnp.sum(jnp.where(lane == me, cnt, 0.0), axis=-1, keepdims=True)
        gate = jnp.sum(jnp.where((lane == me + experts) | (lane == me + 2 * experts), metaf, 0.0), axis=-1, keepdims=True)
        want = jnp.where(msk > 0.0, pos, -1.0).astype(jnp.int32)
        pick = (want == lax.broadcasted_iota(jnp.int32, (SB, slots), 1)).astype(bf)
        picks.append(pick); gates.append(gate)
        rows[i * slots:(i + 1) * slots, :] = dot(pick, x_ref[r, :D], 0, 0).astype(bf)
        gcot = (gate * cot_ref[r, :].astype(jnp.float32)).astype(bf)
        gp[i * slots:(i + 1) * slots, :] = dot(pick, gcot, 0, 0).astype(bf)
    @pl.when(step == 0)
    def _():
        for l in loads: l.wait()
    ga = dot(rows[...], wg[...], 1, 0)
    ua = dot(rows[...], wu[...], 1, 0)
    sig = 1.0 / (1.0 + jnp.exp(-ga))
    act = ga * sig
    hid = (act * ua).astype(bf)
    eo = dot(hid, wd[...], 1, 0).astype(bf)
    gg = []
    for i in range(nsub):
        r = pl.ds(i * SB, SB)
        tok = dot(picks[i], eo[i * slots:(i + 1) * slots, :], 1, 0)
        out_ref[r, :] = (gates[i] * tok).astype(bf)
        gg.append(jnp.sum(tok * cot_ref[r, :].astype(jnp.float32), axis=-1, keepdims=True))
    gh = dot(gp[...], wd[...], 1, 1)
    dga = (gh * ua * (sig * (1.0 + ga * (1.0 - sig)))).astype(bf)
    dua = (gh * act).astype(bf)
    dwd[...] += dot(hid, gp[...], 0, 0)
    grow = (dot(dga, wg[...], 1, 1) + dot(dua, wu[...], 1, 1)).astype(bf)
    dwg[...] += dot(rows[...], dga, 0, 0)
    dwu[...] += dot(rows[...], dua, 0, 0)
    for i in range(nsub):
        r = pl.ds(i * SB, SB)
        gr_ref[r, :D] = dot(picks[i], grow[i * slots:(i + 1) * slots, :], 1, 0).astype(bf)
        hi = gg[i].astype(bf).astype(jnp.float32)
        lo = gg[i] - hi
        gr_ref[r, D:] = (jnp.where(lane == me, hi, 0.0) + jnp.where(lane == me + experts, lo, 0.0)).astype(bf)
    @pl.when(step == pl.num_programs(0) - 1)
    def _():
        outs = [pltpu.make_async_copy(v, h.at[0], osem.at[i]) for i, (v, h) in enumerate(((dwg, dwg_hbm), (dwu, dwu_hbm), (dwd, dwd_hbm)))]
        for o in outs: o.start()
        for o in outs: o.wait()

def experts_call(x_all, cot_all, w_gate, w_up, w_down, experts, block, capacity, TB=512, SB=256):
    T, C = x_all.shape; D = cot_all.shape[1]
    F = w_gate.shape[2]
    slots = max(SB // block, 1) * capacity
    total = TB // SB * slots
    any_ = pl.BlockSpec(memory_space=pl.ANY)
    V = pltpu.VMEM; bf = jnp.bfloat16; f32 = jnp.float32
    return pl.pallas_call(
        functools.partial(expert_kernel, experts, slots, SB),
        grid=(T // TB,),
        out_shape=[jax.ShapeDtypeStruct((T, D), bf), jax.ShapeDtypeStruct((T, C), bf), jax.ShapeDtypeStruct(w_gate.shape, f32), jax.ShapeDtypeStruct(w_up.shape, f32), jax.ShapeDtypeStruct(w_down.shape, f32)],
        in_specs=[pl.BlockSpec((TB, C), lambda i: (i, 0)), pl.BlockSpec((TB, D), lambda i: (i, 0)), any_, any_, any_],
        out_specs=[pl.BlockSpec((TB, D), lambda i: (i, 0)), pl.BlockSpec((TB, C), lambda i: (i, 0)), any_, any_, any_],
        scratch_shapes=[V((D, F), bf), V((D, F), bf), V((F, D), bf), V((D, F), f32), V((D, F), f32), V((F, D), f32), V((total, D), bf), V((total, D), bf), pltpu.SemaphoreType.DMA((3,)), pltpu.SemaphoreType.DMA((3,))],
        compiler_params=pltpu.CompilerParams(dimension_semantics=("arbitrary",), vmem_limit_bytes=65000 * 1024),
        cost_estimate=pl.CostEstimate(flops=133_000_000_000, bytes_accessed=160_000_000, transcendentals=0),
        name="experts",
    )(x_all, cot_all, w_gate, w_up, w_down)

HQ = 32
HK = 4
HD = 128
epsilon = 1e-06
theta_base = 1000000.0
BOTH = ("expert", "shard")


def matmul(left, right):
    return jnp.dot(left, right, preferred_element_type=jnp.float32)


def matmul_tn(left, right):
    return lax.dot_general(
        left, right, (((0,), (0,)), ((), ())), preferred_element_type=jnp.float32
    )


def matmul_nt(left, right):
    return lax.dot_general(
        left, right, (((1,), (1,)), ((), ())), preferred_element_type=jnp.float32
    )


def norm_rows(values, gain_vec):
    return (
        values * lax.rsqrt(jnp.mean(values * values, axis=-1, keepdims=True) + epsilon) * gain_vec
    )


def norm_back(values, gain_vec, upstream):
    scaling = lax.rsqrt(jnp.mean(values * values, axis=-1, keepdims=True) + epsilon)
    gain_grad = jnp.sum(upstream * values * scaling, axis=0)
    weighted = upstream * gain_vec
    inner_sum = jnp.mean(weighted * values, axis=-1, keepdims=True)
    return (scaling * weighted - values * (scaling * scaling * scaling) * inner_sum, gain_grad)


def rotary(values, positions):
    head_width = values.shape[-1]
    half_width = head_width // 2
    frequency = theta_base ** (-2.0 * jnp.arange(half_width, dtype=jnp.float32) / head_width)
    angles = positions.astype(jnp.float32)[:, None] * frequency[None, :]
    cosine = jnp.concatenate([jnp.cos(angles), jnp.cos(angles)], axis=-1)[:, None, :]
    sine_part = jnp.concatenate([jnp.sin(angles), jnp.sin(angles)], axis=-1)[:, None, :]
    turned = jnp.concatenate([-values[..., half_width:], values[..., :half_width]], axis=-1)
    return values * cosine + turned * sine_part


def head_prep(projected, gain_vec, positions, head_count, factor):
    shaped = projected.reshape(projected.shape[0], head_count, projected.shape[1] // head_count)
    return rotary(norm_rows(shaped, gain_vec), positions) * factor


def head_forward(query_block, key_block, value_block, allowed):
    scores = jnp.einsum("rgd,sd->rgs", query_block, key_block, preferred_element_type=jnp.float32)
    raised = jnp.where(allowed[:, None, :], jnp.exp(scores), 0.0)
    totals = jnp.sum(raised, axis=-1)
    probs_low = (raised / totals[..., None]).astype(jnp.bfloat16)
    return (
        jnp.einsum("rgs,sd->rgd", probs_low, value_block, preferred_element_type=jnp.float32),
        totals,
    )


def head_backward(query_block, key_block, value_block, totals, upstream, allowed):
    scores = jnp.einsum("rgd,sd->rgs", query_block, key_block, preferred_element_type=jnp.float32)
    raised = jnp.where(allowed[:, None, :], jnp.exp(scores), 0.0)
    probs_f = raised / totals[..., None]
    probs_low = probs_f.astype(jnp.bfloat16)
    grad_probs = jnp.einsum(
        "rgd,sd->rgs", upstream, value_block, preferred_element_type=jnp.float32
    )
    inner_sum = jnp.sum(probs_f * grad_probs, axis=-1, keepdims=True)
    grad_scores = (probs_f * (grad_probs - inner_sum)).astype(jnp.bfloat16)
    grad_query = jnp.einsum(
        "rgs,sd->rgd", grad_scores, key_block, preferred_element_type=jnp.float32
    )
    grad_key = jnp.einsum(
        "rgs,rgd->sd", grad_scores, query_block, preferred_element_type=jnp.float32
    )
    grad_value = jnp.einsum("rgs,rgd->sd", probs_low, upstream, preferred_element_type=jnp.float32)
    return (grad_query, grad_key, grad_value)


def gather_all(arrays, cid):
    if placed():
        return [o.reshape(-1, o.shape[-1]) for o in ag32(arrays, cid)]
    return [lax.all_gather(a, BOTH, axis=0, tiled=True) for a in arrays]


def scatter_all(arrays, cid, out_dtype=jnp.float32):
    if placed():
        return rs32([a.reshape(32, -1, a.shape[-1]) for a in arrays], cid, out_dtype)
    return [lax.psum_scatter(a, BOTH, scatter_dimension=0, tiled=True).astype(out_dtype) for a in arrays]


def per_device(
    hidden_in,
    g_attn,
    w_query,
    w_key,
    w_value,
    g_query,
    g_key,
    w_out,
    g_ffn,
    w_router,
    w_gate,
    w_up,
    w_down,
    routes,
    cotangent,
):
    bf, f32 = jnp.bfloat16, jnp.float32
    tok_rows, model_width = hidden_in.shape
    top_count = routes.shape[1]
    devices = lax.axis_size(BOTH)
    expert_count = devices * w_gate.shape[0]
    capacity = 2 * tok_rows * top_count // expert_count
    shard_count = lax.axis_size("shard")
    shard_pos = lax.axis_index("shard")
    seq_len = tok_rows * shard_count
    group_size = HQ // HK
    factor = HD ** (-0.5)
    q_cols, kv_cols = HQ * HD, HK * HD

    pieces = [w_router.reshape(-1), g_attn, g_ffn, g_query, g_key]
    sizes = [p.shape[0] for p in pieces]
    used = sum(sizes)
    small_rows = -(-used // (32 * 128)) * 32
    small = jnp.concatenate(pieces + [jnp.zeros((small_rows * 128 - used,), bf)]).reshape(small_rows, 128)
    wqkv = jnp.concatenate([w_query, w_key, w_value], axis=1)
    wqkv_full, small_all = gather_all([wqkv, small], 1)
    small_all = small_all.reshape(devices, small_rows * 128)
    starts = [sum(sizes[:i]) for i in range(5)]
    wr_full, attn_gain, ffn_gain, query_gain, key_gain = [small_all[:, o : o + n].reshape(-1) for o, n in zip(starts, sizes)]
    wr_full = wr_full.reshape(model_width, expert_count)
    attn_gain, ffn_gain, query_gain, key_gain = [g.astype(f32) for g in (attn_gain, ffn_gain, query_gain, key_gain)]
    wo_full = lax.all_gather(w_out, BOTH, axis=0, tiled=True)
    cot_all = lax.all_gather(cotangent, BOTH, axis=0, tiled=True)

    positions = shard_pos * tok_rows + jnp.arange(tok_rows, dtype=jnp.int32)
    inputs_f = hidden_in.astype(f32)
    normed_low = norm_rows(inputs_f, attn_gain).astype(bf)
    qkv = matmul(normed_low, wqkv_full)
    q_proj, k_proj, v_proj = qkv[:, :q_cols], qkv[:, q_cols : q_cols + kv_cols], qkv[:, q_cols + kv_cols :]
    k_rot, k_pull = jax.vjp(
        lambda projected, gain_vec: head_prep(projected, gain_vec, positions, HK, 1.0),
        k_proj,
        key_gain,
    )
    q_rot, q_pull = jax.vjp(
        lambda projected, gain_vec: head_prep(projected, gain_vec, positions, HQ, factor),
        q_proj,
        query_gain,
    )
    q_low = q_rot.astype(bf)
    kv_low = jnp.concatenate([k_rot.reshape(tok_rows, kv_cols).astype(bf), v_proj.astype(bf)], axis=1)
    allowed = jnp.arange(seq_len, dtype=jnp.int32)[None, :] <= positions[:, None]
    kv_all = line_gather(kv_low, 2)
    q_heads = q_low.reshape(tok_rows, HK, group_size, HD).transpose(1, 0, 2, 3)
    k_heads = kv_all[:, :kv_cols].reshape(seq_len, HK, HD).transpose(1, 0, 2)
    v_heads = kv_all[:, kv_cols:].reshape(seq_len, HK, HD).transpose(1, 0, 2)

    def attend(pieces):
        return head_forward(pieces[0], pieces[1], pieces[2], allowed)

    head_outs, totals = lax.map(attend, (q_heads, k_heads, v_heads))
    mix_low = head_outs.transpose(1, 0, 2, 3).reshape(tok_rows, q_cols).astype(bf)
    residual = inputs_f + matmul(mix_low, wo_full)
    ffn_low = norm_rows(residual, ffn_gain).astype(bf)

    logits = matmul(ffn_low, wr_full)
    expert_ids = jnp.arange(expert_count, dtype=jnp.int32)
    chosen = jnp.any(routes[:, :, None] == expert_ids[None, None, :], axis=1)
    raised_gate = jnp.where(chosen, jnp.exp(logits), 0.0)
    gates = raised_gate / jnp.sum(raised_gate, axis=-1, keepdims=True)
    gate_high = lax.reduce_precision(gates, 8, 7)
    gate_low = gates - gate_high
    extra = -(-3 * expert_count // 128) * 128
    payload = jnp.concatenate(
        [
            ffn_low,
            chosen.astype(bf),
            gate_high.astype(bf),
            gate_low.astype(bf),
            jnp.zeros((tok_rows, extra - 3 * expert_count), bf),
        ],
        axis=1,
    )
    (payload_all,) = gather_all([payload], 3)
    out_part, grad_part, grad_wgate, grad_wup, grad_wdown = experts_call(
        payload_all, cot_all, w_gate, w_up, w_down, expert_count, tok_rows, capacity
    )
    (grad_sum,) = scatter_all([grad_part], 4)
    (moe_out,) = scatter_all([out_part], 5)
    block_out = (residual + moe_out).astype(bf)
    upstream = cotangent.astype(f32)
    grad_ffn = grad_sum[:, :model_width]
    grad_gates = (
        grad_sum[:, model_width : model_width + expert_count]
        + grad_sum[:, model_width + expert_count : model_width + 2 * expert_count]
    )
    grad_logits = (gates * (grad_gates - jnp.sum(gates * grad_gates, axis=-1, keepdims=True))).astype(bf)
    grad_wrouter = matmul_tn(ffn_low, grad_logits)
    grad_ffn = grad_ffn + matmul_nt(grad_logits, wr_full)
    grad_second, grad_ffn_gain = norm_back(residual, ffn_gain, grad_ffn)
    grad_residual = upstream + grad_second
    grad_attn_low = grad_residual.astype(bf)
    grad_wout = matmul_tn(mix_low, grad_attn_low).astype(bf)
    grad_mix = matmul_nt(grad_attn_low, wo_full).astype(bf)
    grad_heads = grad_mix.reshape(tok_rows, HK, group_size, HD).transpose(1, 0, 2, 3)

    def attend_back(pieces):
        return head_backward(pieces[0], pieces[1], pieces[2], pieces[3], pieces[4], allowed)

    grad_qheads, grad_kheads, grad_vheads = lax.map(
        attend_back, (q_heads, k_heads, v_heads, totals, grad_heads)
    )
    grad_q_rot = grad_qheads.transpose(1, 0, 2, 3).reshape(tok_rows, HQ, HD)
    grad_kv = jnp.concatenate(
        [
            grad_kheads.transpose(1, 0, 2).reshape(seq_len, kv_cols).astype(bf),
            grad_vheads.transpose(1, 0, 2).reshape(seq_len, kv_cols).astype(bf),
        ],
        axis=1,
    )
    grad_kv = line_scatter(grad_kv, 6)
    grad_q_proj, grad_query_gain = q_pull(grad_q_rot)
    grad_k_proj, grad_key_gain = k_pull(grad_kv[:, :kv_cols].reshape(tok_rows, HK, HD))
    grad_qkv_low = jnp.concatenate(
        [grad_q_proj.astype(bf), grad_k_proj.astype(bf), grad_kv[:, kv_cols:].astype(bf)], axis=1
    )
    grad_wqkv = matmul_tn(normed_low, grad_qkv_low).astype(bf)
    grad_normed = matmul_nt(grad_qkv_low, wqkv_full)
    grad_front, grad_attn_gain = norm_back(inputs_f, attn_gain, grad_normed)
    grad_input = (grad_residual + grad_front).astype(bf)

    grads = [grad_wrouter, grad_attn_gain, grad_ffn_gain, grad_query_gain, grad_key_gain]
    packed = jnp.concatenate(
        [g.astype(bf).reshape(devices, -1) for g in grads] + [jnp.zeros((devices, small_rows * 128 - used), bf)], axis=1
    ).reshape(devices * small_rows, 128)
    (out_grad,) = scatter_all([grad_wout], 7)
    qkv_grad, small_grad = scatter_all([grad_wqkv, packed], 8)
    small_grad = small_grad.reshape(-1)
    router_g, attn_g, ffn_g, query_g, key_g = [small_grad[o : o + n] for o, n in zip(starts, sizes)]
    return (
        block_out,
        grad_input,
        attn_g,
        qkv_grad[:, :q_cols],
        qkv_grad[:, q_cols : q_cols + kv_cols],
        qkv_grad[:, q_cols + kv_cols :],
        query_g,
        key_g,
        out_grad,
        ffn_g,
        router_g.reshape(w_router.shape),
        grad_wgate,
        grad_wup,
        grad_wdown,
    )


def solution(mesh):
    row = P(BOTH, None)
    vec = P(BOTH)
    cube = P(BOTH, None, None)
    in_specs = (row, vec, row, row, row, vec, vec, row, vec, row, cube, cube, cube, row, row)
    out_specs = (row, row, vec, row, row, row, vec, vec, row, vec, row, cube, cube, cube)
    return jax.shard_map(
        per_device, mesh=mesh, in_specs=in_specs, out_specs=out_specs, check_vma=False
    )
```

time: 2910 us -> 1730 us (0.59)
  Pallas kernels: 0 us -> 1390 us
  blocking collectives: 1210 us -> 0 us
  waiting for transfers between devices: 975 us -> 1.39 us
  matrix products: 347 us -> 144 us
  local copies, waits for them, and re-layouts: 205 us -> 110 us
  other arithmetic: 134 us -> 55.5 us
    pallas_call x0 -> x9, Pallas kernels: none -> 1390 us  [the longest x4 769 us: rs32(): pl.pallas_call(functools.partial(rs_kernel, n), out_shape=[jax.ShapeDtype...]
    all_to_all x2 -> x0, blocking collectives: 734 us -> none  [the longest x1 368 us: per_device(): lax.all_to_all(grad_outgoing, ('expert', 'shard'), split_axis=0, concat_a...]
    all_gather x6 -> x0, blocking collectives: 432 us -> none  [the longest x1 369 us: per_device(): lax.all_gather(w_router, 'shard', axis=0, tiled=True)]
    reduce_scatter x11 -> x0, waiting for transfers between devices: 386 us -> none  [the longest x1 118 us: per_device(): lax.psum_scatter(grad_wout.astype(jnp.bfloat16), 'expert', scatter_dimens...]
    all_to_all x2 -> x0, waiting for transfers between devices: 372 us -> none  [the longest x1 372 us: per_device(): lax.all_to_all(grad_rows.reshape(expert_count, capacity, model_width), ('...]
    all_gather x8 -> x2, waiting for transfers between devices: 198 us -> 0.01 us  [the longest x1 0.01 us: per_device(): wo_full = lax.all_gather(w_out, BOTH, axis=0, tiled=True)]
    gather x4 -> x0, local copies, waits for them, and re-layouts: 118 us -> none  [the longest x1 35.8 us: per_device(): jnp.take(grad_padded, slot_owner, axis=0)]
    dot_general x8 -> x3, matrix products: 92.4 us -> 20.7 us  [matmul(): return jnp.dot(left, right, preferred_element_type=jnp.float32)]
  transfers between devices with their start and end apart: 22 -> 2, of which waited for: 16 -> 0; matrix products, arithmetic and copies ran while one was open for 9% -> 7% of each run, Pallas kernels for 0% -> 23%
where the time goes in v1:
time: 1730 us; the launch traced here: 1720 us
  Pallas kernels  1390 us (80%)
  matrix products  144 us (8%)
  local copies, waits for them, and re-layouts  110 us (6%)
  other arithmetic  55.5 us (3%)
    pallas_call x4, Pallas kernels, rs32(): pl.pallas_call(functools.partial(rs_kernel, n), out_shape=[jax.ShapeDtype...  769 us
    pallas_call x2, Pallas kernels, ag32(): pl.pallas_call(functools.partial(ag_kernel, n), out_shape=[jax.ShapeDtype...  310 us
    pallas_call x1, Pallas kernels, experts_call(): pl.pallas_call(functools.partial(expert_kernel, experts, slots, SB), grid...  179 us
    pallas_call x1, Pallas kernels, line_gather(): pl.pallas_call(line_gather_kernel, out_shape=jax.ShapeDtypeStruct((NZ,) +...  90.7 us
    unnamed x139, local copies, waits for them, and re-layouts  49.6 us
    pallas_call x1, Pallas kernels, line_scatter(): pl.pallas_call(line_scatter_kernel, out_shape=jax.ShapeDtypeStruct((R, C)...  45.5 us
    dot_general x3, matrix products, matmul_nt(): lax.dot_general(left, right, (((1,), (1,)), ((), ())), preferred_element_...  34.7 us
  transfers between devices with their start and end apart: 2, of which 0 were waited for; matrix products, arithmetic and copies ran while one was open for 7% of the time, Pallas kernels for 23%

profile of v1, /device:TPU:18, one launch (start us, length us, event | category | flops | bytes accessed | tf_op | source)
XLA Modules:
  0.0 1721.3 jit_solution(3101851896641568017)
XLA Ops:
  9.6 2.8 concatenate.42
  13.5 137.1 %gather_all.2 = (bf16[2,2,2,4,2,32,5120]{6,5,4,3,2,1,0:T(8,128)(2,1)S(1)}, bf16[2,2,2,4,2,16,128]{6,5,4,3,2,1,0:T(8,128)(2,1)S(1)}) custom-call(bf16[2,32,5120]{2,1,0:T(8,128)(2,1)S(1)} %bitcast.205, bf16[2,16,128]{2,1,0:T(8,128)(2,1)S(1)} %bitcast.206), custom_call_target="tpu_custom_call" | custom-call | tf_op jit(solution)/shard_map/gather_all/pallas_call | solution.py:144
  150.6 7.5 copy-done.2
  159.8 10.5 fusion.77
  181.7 90.7 %line_gather.1 = bf16[4,256,1024]{2,1,0:T(8,128)(2,1)S(1)} custom-call(bf16[256,1024]{1,0:T(8,128)(2,1)S(1)} %pad_maximum_fusion.5.x_ref), custom_call_target="tpu_custom_call" | custom-call | tf_op jit(solution)/shard_map/line_gather/pallas_call | solution.py:297
  278.7 6.6 slice_bitcast_fusion
  285.4 5.6 copy.124
  291.1 2.8 multiply_reduce_fusion.3
  295.3 2.4 slice_negate_fusion.1
  297.7 3.8 copy.127
  301.5 4.3 copy.128
  305.8 6.4 copy.180
  315.6 7.9 fusion.67
  323.5 30.0 %while.28 = (s32[]{:T(128)}, bf16[4,256,8,128]{1,3,2,0:T(8,128)(2,1)}, f32[4,256,8]{1,2,0:T(8,128)}, bf16[4,256,8,128]{3,1,2,0:T(8,128)(2,1)}, bf16[4,1024,128]{...) while((s32[]{:T(128)}, ...), condition=%wide.region_5.6_spmd.clone, body=%wide.region_3.5_spmd.clone.sunk | while | flops 1084487680 | bytes 36474508 | solution.py:589
  323.7 3.0 fusion.125
  331.2 3.0 fusion.125
  334.2 2.3 fusion.126
  338.7 3.0 fusion.125
  346.2 3.0 fusion.125
  353.5 9.7 multiply_reduce_fusion.6
  366.5 172.4 %gather_all.3 = bf16[2,2,2,4,2,128,2176]{6,5,4,3,2,1,0:T(8,128)(2,1)S(1)} custom-call(bf16[2,128,2176]{2,1,0:T(8,128)(2,1)S(1)} %bitcast.204), custom_call_target="tpu_custom_call" | custom-call | tf_op jit(solution)/shard_map/gather_all/pallas_call | solution.py:144
  538.9 11.7 copy-done
  550.7 179.2 %experts.1 = (bf16[8192,2048]{1,0:T(8,128)(2,1)}, bf16[8192,2176]{1,0:T(8,128)(2,1)}, f32[1,2048,768]{2,1,0:T(8,128)}, f32[1,2048,768]{2,1,0:T(8,128)}, f32[1,768,2048]{2,1,0:T(8,128)}) custom-call(bf16[8192,2176]{1,0:T(8,128)(2,1)} %bitcast.202, bf16[8192,2048]{1,0:T(8,128)(2,1)} %all-gather.5.cloned.1.call-done.cot_ref, bf16[1,2048,768]{2,1,0:T(8,128)(2,1)} %wg_hbm.1, ...), custom_call_target="tpu_custom_call" | custom-call | flops 133000003584 | bytes 160000000 | tf_op jit(solution)/shard_map/experts/pallas_call | solution.py:409
  729.9 238.1 %scatter_all.5 = f32[2,128,2176]{2,1,0:T(8,128)} custom-call(bf16[2,2,2,4,2,128,2176]{6,5,4,3,2,1,0:T(8,128)(2,1)} %bitcast.212), custom_call_target="tpu_custom_call" | custom-call | tf_op jit(solution)/shard_map/scatter_all/pallas_call | solution.py:263
  970.4 4.9 multiply_reduce_fusion.4
  976.3 231.4 %scatter_all.4 = f32[2,128,2048]{2,1,0:T(8,128)} custom-call(bf16[2,2,2,4,2,128,2048]{6,5,4,3,2,1,0:T(8,128)(2,1)} %bitcast.213), custom_call_target="tpu_custom_call" | custom-call | tf_op jit(solution)/shard_map/scatter_all/pallas_call | solution.py:263
  1207.7 4.5 subtract_add_fusion
  1212.2 10.6 convolution_convert_fusion.1
  1222.8 18.1 %fusion.68 = bf16[32,8,32,128]{3,1,2,0:T(8,128)(2,1)} fusion(bf16[4096,2048]{1,0:T(8,128)(2,1)} %all-gather.3.cloned.1.call-done, f32[256,2048]{1,0:T(8,128)S(1)} %get-tuple-element.361), kind=kOutput, calls=%fused_computation.104 | convolution fusion | flops 4296540160 | bytes 20971520 | tf_op jit(solution)/shard_map/dot_general | solution.py:440
  1243.9 56.1 %while.29 = (s32[]{:T(128)}, f32[4,256,8,128]{3,1,2,0:T(8,128)}, bf16[4,1024,128]{2,1,0:T(8,128)(2,1)}, bf16[4,1024,128]{2,1,0:T(8,128)(2,1)}, bf16[4,256,8,128]...) while((s32[]{:T(128)}, f32[4,256,8,128]{3,1,2,0:T(8,128)}, ...), condition=%wide.region_13.14_spmd.clone, body=%wide.region_11.13_spmd.clone.sunk | while | flops 2701391872 | bytes 85244104 | solution.py:638
  1244.4 2.4 fusion.135
  1247.7 3.0 multiply_reduce_fusion.12
  1258.3 2.3 fusion.135
  1261.6 3.0 multiply_reduce_fusion.12
  1272.2 2.3 fusion.135
  1275.5 3.0 multiply_reduce_fusion.12
  1286.2 2.3 fusion.135
  1289.4 3.0 multiply_reduce_fusion.12
  1305.3 45.5 %line_scatter.1 = f32[256,1024]{1,0:T(8,128)S(1)} custom-call(bf16[4,256,1024]{2,1,0:T(8,128)(2,1)S(1)} %pad_maximum_fusion.1.p_ref), custom_call_target="tpu_custom_call" | custom-call | tf_op jit(solution)/shard_map/line_scatter/pallas_call | solution.py:329
  1350.8 5.7 copy.145
  1356.6 2.6 bitcast_multiply_fusion
  1362.7 4.1 multiply_reduce_fusion.1
  1370.2 6.1 fusion.48
  1376.3 11.7 fusion.65
  1388.0 11.9 convolution_convert_fusion
  1402.1 167.2 %scatter_all.6 = (f32[2,32,5120]{2,1,0:T(8,128)}, f32[2,16,128]{2,1,0:T(8,128)}) custom-call(bf16[2,2,2,4,2,32,5120]{6,5,4,3,2,1,0:T(8,128)(2,1)} %bitcast.210, bf16[2,2,2,4,2,16,128]{6,5,4,3,2,1,0:T(8,128)(2,1)} %bitcast.239), custom_call_target="tpu_custom_call" | custom-call | tf_op jit(solution)/shard_map/scatter_all/pallas_call | solution.py:263
  1576.7 132.0 %scatter_all.7 = f32[2,64,2048]{2,1,0:T(8,128)} custom-call(bf16[2,2,2,4,2,64,2048]{6,5,4,3,2,1,0:T(8,128)(2,1)} %bitcast.211), custom_call_target="tpu_custom_call" | custom-call | tf_op jit(solution)/shard_map/scatter_all/pallas_call | solution.py:263
  1709.5 3.8 fusion.62
  (311 shorter events, 110.0 us)
Async XLA Ops:
  7.2 151.8 %copy-start.7 = (bf16[256,2048]{1,0:T(8,128)(2,1)S(1)}, bf16[256,2048]{1,0:T(8,128)(2,1)}, u32[]{:S(2)}) copy-start(bf16[256,2048]{1,0:T(8,128)(2,1)} %param.19) | copy-start | bytes 3145732
  7.2 346.3 %all-gather.3.cloned.1.call-start = ((), (), s32[]{:S(2)}) async-start(), calls=%async_computation | async-start | bytes 17301504 | tf_op jit(solution)/shard_map/all_gather | solution.py:560
  7.9 542.7 %all-gather.5.cloned.1.call-start = ((), (), s32[]{:S(2)}) async-start(), calls=%async_computation.1 | async-start | bytes 34603008 | tf_op jit(solution)/shard_map/all_gather | solution.py:561
  150.6 7.5 copy-start.2
  158.2 18.0 %copy-start.36 = (bf16[32,4096]{1,0:T(8,128)(2,1)}, bf16[32,4096]{1,0:T(8,128)(2,1)S(1)}, u32[]{:S(2)}) copy-start(bf16[32,4096]{1,0:T(8,128)(2,1)S(1)} %reshape_reshape_reshape.6) | copy-start | bytes 786436
  159.0 11.3 copy-start.42
  159.8 10.5 copy-start.53
  159.8 13.6 copy-start.66
  175.0 5.4 copy-start.12
  176.2 5.5 copy-start.25
  176.9 4.7 copy-start.62
  178.1 137.5 %copy-start.29 = (f32[256,128]{1,0:T(8,128)}, f32[256,128]{1,0:T(8,128)S(1)}, u32[]{:S(2)}) copy-start(f32[256,128]{1,0:T(8,128)S(1)} %copy.129) | copy-start | bytes 393220
  178.8 136.7 %copy-start.27 = (f32[256,128]{1,0:T(8,128)}, f32[256,128]{1,0:T(8,128)S(1)}, u32[]{:S(2)}) copy-start(f32[256,128]{1,0:T(8,128)S(1)} %copy.126) | copy-start | bytes 393220
  285.4 5.6 copy-start.52
  291.1 24.5 %copy-start.64 = (f32[128]{0:T(128)}, f32[128]{0:T(128)S(1)}, u32[]{:S(2)}) copy-start(f32[128]{0:T(128)S(1)} %reshape.277) | copy-start | bytes 1540
  291.1 3.5 copy-start.3
  305.8 7.2 slice-start.1
  313.0 50.9 %copy-start.48 = (f32[2048]{0:T(1024)}, f32[2048]{0:T(1024)S(1)}, u32[]{:S(2)}) copy-start(f32[2048]{0:T(1024)S(1)} %reshape.279) | copy-start | bytes 24580
  353.5 9.7 copy-start.14
  353.5 9.7 copy-start.20
  353.5 9.7 copy-start.50
  353.5 10.6 copy-start.21
  353.5 10.6 copy-start.47
  364.1 174.8 %copy-start.10 = (bf16[256,2048]{1,0:T(8,128)(2,1)}, bf16[256,2048]{1,0:T(8,128)(2,1)S(1)}, u32[]{:S(2)}) copy-start(bf16[256,2048]{1,0:T(8,128)(2,1)S(1)} %multiply_convert_fusion.1) | copy-start | bytes 3145732
  538.9 11.8 copy-start
  729.8 238.1 %copy-start.32 = (f32[256,32]{1,0:T(8,128)S(1)}, f32[256,32]{1,0:T(8,128)}, u32[]{:S(2)}) copy-start(f32[256,32]{1,0:T(8,128)} %copy-done.31) | copy-start | bytes 98308
  729.8 238.1 %copy-start.58 = (f32[256]{0:T(256)S(1)}, f32[256]{0:T(256)}, u32[]{:S(2)}) copy-start(f32[256]{0:T(256)} %copy-done.57) | copy-start | bytes 3076
  729.9 240.6 %copy-start.22 = (bf16[2048,32]{1,0:T(8,128)(2,1)S(1)}, bf16[2048,32]{1,0:T(8,128)(2,1)}, u32[]{:S(2)}) copy-start(bf16[2048,32]{1,0:T(8,128)(2,1)} %reshape_reshape.29) | copy-start | bytes 393220
  729.9 240.6 %copy-start.49 = (f32[2048]{0:T(1024)S(1)}, f32[2048]{0:T(1024)}, u32[]{:S(2)}) copy-start(f32[2048]{0:T(1024)} %copy-done.48) | copy-start | bytes 24580
  729.9 240.6 %copy-start.61 = (f32[256]{0:T(256)S(1)}, f32[256]{0:T(256)}, u32[]{:S(2)}) copy-start(f32[256]{0:T(256)} %copy-done.60) | copy-start | bytes 3076
  968.0 7.4 copy-start.11
  976.3 231.4 %copy-start.24 = (bf16[256,2048]{1,0:T(8,128)(2,1)S(1)}, bf16[256,2048]{1,0:T(8,128)(2,1)}, u32[]{:S(2)}) copy-start(bf16[256,2048]{1,0:T(8,128)(2,1)} %param.33) | copy-start | bytes 3145732
  976.3 231.4 %copy-start.68 = (f32[256]{0:T(256)S(1)}, f32[256]{0:T(256)}, u32[]{:S(2)}) copy-start(f32[256]{0:T(256)} %get-tuple-element.391) | copy-start | bytes 3076
  1212.2 10.6 copy-start.9
  1350.8 5.8 copy-start.1
  1350.8 5.8 copy-start.40
  1359.2 3.5 copy-start.5
  1359.2 3.5 copy-start.65
  1362.7 4.2 copy-start.45
  1362.7 4.2 slice-start
  1362.7 4.4 copy-start.30
  1370.1 6.1 copy-start.8
  1370.1 6.1 copy-start.43
  1370.2 6.1 copy-start.54
  1388.0 12.0 copy-start.41
  1388.0 13.1 copy-start.59
  1576.7 132.8 %copy-start.67 = (f32[256]{0:T(256)S(1)}, f32[256]{0:T(256)}, u32[]{:S(2)}) copy-start(f32[256]{0:T(256)} %get-tuple-element.389) | copy-start | bytes 3076
  1708.7 4.6 copy-start.23
  (40 other events, 78.3 us)
Sparse Core Ops, SparseCore 0:
  11.0 159.7 all-gather.2
  173.7 252.4 all-gather.4

commit v2 on v1

--- a/solution.py
+++ b/solution.py
@@ -150,17 +150,18 @@
             pltpu.SemaphoreType.DMA((n, 2, 9)), pltpu.SemaphoreType.DMA((n, 2, 9)),
             pltpu.SemaphoreType.DMA((n, nk, 2, 3)), pltpu.SemaphoreType.DMA((n, nk, 2, 3)),
             pltpu.SemaphoreType.DMA((n, nk)), pltpu.SemaphoreType.DMA((n, nk))],
-        compiler_params=pltpu.CompilerParams(collective_id=cid, has_side_effects=True, vmem_limit_bytes=8 << 20),
+        compiler_params=pltpu.CompilerParams(collective_id=cid, has_side_effects=True, vmem_limit_bytes=64000 * 1024),
         name="gather_all",
     )(*ins)
     return [o.reshape(32, a.shape[0], a.shape[1]) for o, a in zip(outs, arrs)]
 
 ZORDER = (0, 3, 1, 2)
-
-def rs_kernel(n_arr, *refs):
+LAGS = (1, 1, 1, 1)
+
+def rs_kernel(n_arr, parts, *refs):
     ins = refs[:n_arr]; outs = refs[n_arr:2 * n_arr]
     sc = refs[2 * n_arr:]
-    own_b = sc[:n_arr]; r0_b = sc[n_arr:2 * n_arr]; ra_b = sc[2 * n_arr:3 * n_arr]; rb_b = sc[3 * n_arr:4 * n_arr]; zu_b = sc[4 * n_arr:5 * n_arr]; zd_b = sc[5 * n_arr:6 * n_arr]
+    own_b, r0_b, ra_b, rb_b, zu_b, zd_b = [sc[i * n_arr:(i + 1) * n_arr] for i in range(6)]
     lsem, s0s, s0r, sas, sar, sbs, sbr, zus, zur, zds, zdr = sc[6 * n_arr:]
     y, x, c, s = place()
     barrier_all(y, x, c, s)
@@ -168,8 +169,8 @@
     UP = dev(y, x, c, s + 1); DN = dev(y, x, c, s - 1)
     def rc(src, dst, ss, rs, d):
         return pltpu.make_async_remote_copy(src_ref=src, dst_ref=dst, send_sem=ss, recv_sem=rs, device_id=d, device_id_type=MESH)
-    units = [(a, zz, h) for zz in ZORDER for a in range(n_arr) for h in range(2)]
-    def jj(zz, h): return ZORDER.index(zz) * 2 + h
+    units = [(a, zz, h) for zz in ZORDER for h in range(parts) for a in range(n_arr)]
+    def jj(zz, h): return ZORDER.index(zz) * parts + h
     def load(a, zz, h):
         j = jj(zz, h)
         return pltpu.make_async_copy(ins[a].at[:, :, c, zz, h], own_b[a].at[j], lsem.at[a, j])
@@ -178,11 +179,11 @@
         return rc(ins[a].at[:, :, 1 - c, zz, h], r0_b[a].at[j], s0s.at[a, j], s0r.at[a, j], C)
     def ca(a, zz, h):
         j = jj(zz, h)
-        if h == 0: return rc(own_b[a].at[j, :, 1 - x], ra_b[a].at[j], sas.at[a, j], sar.at[a, j], X)
+        if h % 2 == 0: return rc(own_b[a].at[j, :, 1 - x], ra_b[a].at[j], sas.at[a, j], sar.at[a, j], X)
         return rc(own_b[a].at[j, 1 - y], ra_b[a].at[j], sas.at[a, j], sar.at[a, j], Y)
     def cb(a, zz, h):
         j = jj(zz, h)
-        if h == 0: return rc(own_b[a].at[j, 1 - y, x], rb_b[a].at[j], sbs.at[a, j], sbr.at[a, j], Y)
+        if h % 2 == 0: return rc(own_b[a].at[j, 1 - y, x], rb_b[a].at[j], sbs.at[a, j], sbr.at[a, j], Y)
         return rc(own_b[a].at[j, y, 1 - x], rb_b[a].at[j], sbs.at[a, j], sbr.at[a, j], X)
     def cu(a, zz, h):
         j = jj(zz, h)
@@ -209,41 +210,51 @@
         a, zz, h = u; j = jj(zz, h)
         ca(a, zz, h).wait_recv()
         for q in range(2):
-            if h == 0: add_into(own_b[a].at[j, q, x], ra_b[a].at[j, q])
+            if h % 2 == 0: add_into(own_b[a].at[j, q, x], ra_b[a].at[j, q])
             else: add_into(own_b[a].at[j, y, q], ra_b[a].at[j, q])
         cb(a, zz, h).start()
-    def zflow(u):
-        a, zz, h = u; j = jj(zz, h)
-        mine = own_b[a].at[j, y, x]
-        if zz > 0:
-            @pl.when(jnp.logical_and(s > 0, s <= zz))
-            def _():
-                cu(a, zz, h).wait_recv()
-                add_into(mine, zu_b[a].at[j])
-            @pl.when(s < zz)
-            def _(): cu(a, zz, h).start()
-        if zz < NZ - 1:
-            @pl.when(jnp.logical_and(s < NZ - 1, s >= zz))
-            def _():
-                cd(a, zz, h).wait_recv()
-                add_into(mine, zd_b[a].at[j])
-            @pl.when(s > zz)
-            def _(): cd(a, zz, h).start()
-        @pl.when(s == zz)
-        def _(): outs[a][h] = mine[...].astype(outs[a].dtype)
     def stage2(u):
         a, zz, h = u; j = jj(zz, h)
         cb(a, zz, h).wait_recv()
         add_into(own_b[a].at[j, y, x], rb_b[a].at[j])
+    def hop(u, k):
+        a, zz, h = u; j = jj(zz, h)
+        if k < zz:
+            @pl.when(s == k)
+            def _():
+                if k > 0:
+                    cu(a, zz, h).wait_recv()
+                    add_into(own_b[a].at[j, y, x], zu_b[a].at[j])
+                cu(a, zz, h).start()
+        t = NZ - 1 - k
+        if t > zz:
+            @pl.when(s == t)
+            def _():
+                if k > 0:
+                    cd(a, zz, h).wait_recv()
+                    add_into(own_b[a].at[j, y, x], zd_b[a].at[j])
+                cd(a, zz, h).start()
+    def last(u):
+        a, zz, h = u; j = jj(zz, h)
+        @pl.when(s == zz)
+        def _():
+            if zz > 0: cu(a, zz, h).wait_recv()
+            if zz < NZ - 1: cd(a, zz, h).wait_recv()
+            t = own_b[a][j, y, x].astype(jnp.float32)
+            if zz > 0: t = t + zu_b[a][j].astype(jnp.float32)
+            if zz < NZ - 1: t = t + zd_b[a][j].astype(jnp.float32)
+            outs[a][h] = t.astype(outs[a].dtype)
     for u in units:
         c0(*u).start(); load(*u).start()
     n = len(units)
-    L1, L2, L3 = 2, 4, 5
-    for i in range(n + L3):
+    L1 = LAGS[0] * n_arr; L2 = L1 + LAGS[1] * n_arr; L3 = L2 + LAGS[2] * n_arr; dl = LAGS[3] * n_arr
+    for i in range(n + L3 + (NZ - 1) * dl):
         if i < n: stage0(units[i])
         if 0 <= i - L1 < n: stage1(units[i - L1])
         if 0 <= i - L2 < n: stage2(units[i - L2])
-        if 0 <= i - L3 < n: zflow(units[i - L3])
+        for k in range(NZ - 1):
+            if 0 <= i - L3 - k * dl < n: hop(units[i - L3 - k * dl], k)
+    for u in units: last(u)
     for u in units:
         c0(*u).wait_send(); ca(*u).wait_send(); cb(*u).wait_send()
         zz = u[1]
@@ -254,82 +265,147 @@
             @pl.when(s > zz)
             def _(): cd(*u).wait_send()
 
-def rs32(arrs, cid, out_dtype=jnp.float32):
+def rs32(arrs, cid, out_dtype=jnp.float32, parts=4):
     n = len(arrs)
-    ins = [a.reshape(2, 2, 2, NZ, 2, a.shape[1] // 2, a.shape[2]) for a in arrs]
+    if any(a.shape[1] % (parts * 16) for a in arrs): parts = 2
+    ins = [a.reshape(2, 2, 2, NZ, parts, a.shape[1] // parts, a.shape[2]) for a in arrs]
     hs = [i.shape[-2:] for i in ins]
-    V = pltpu.VMEM; bt = jnp.bfloat16
-    sems = [pltpu.SemaphoreType.DMA((n, 8))] * 11
+    V = pltpu.VMEM; bt = jnp.bfloat16; m = NZ * parts
+    sems = [pltpu.SemaphoreType.DMA((n, m))] * 11
     outs = pl.pallas_call(
-        functools.partial(rs_kernel, n),
-        out_shape=[jax.ShapeDtypeStruct((2,) + h, out_dtype) for h in hs],
+        functools.partial(rs_kernel, n, parts),
+        out_shape=[jax.ShapeDtypeStruct((parts,) + h, out_dtype) for h in hs],
         in_specs=[pl.BlockSpec(memory_space=pl.ANY)] * n,
         out_specs=[pl.BlockSpec(memory_space=pltpu.VMEM)] * n,
-        scratch_shapes=[V((8, 2, 2) + h, bt) for h in hs] + [V((8, 2, 2) + h, bt) for h in hs] + [V((8, 2) + h, bt) for h in hs]
-            + [V((8,) + h, bt) for h in hs] + [V((8,) + h, bt) for h in hs] + [V((8,) + h, bt) for h in hs] + sems,
+        scratch_shapes=[V((m, 2, 2) + h, bt) for h in hs] + [V((m, 2, 2) + h, bt) for h in hs] + [V((m, 2) + h, bt) for h in hs]
+            + [V((m,) + h, bt) for h in hs] + [V((m,) + h, bt) for h in hs] + [V((m,) + h, bt) for h in hs] + sems,
         compiler_params=pltpu.CompilerParams(collective_id=cid, has_side_effects=True, vmem_limit_bytes=64000 * 1024),
         name="scatter_all",
     )(*ins)
     return [o.reshape(a.shape[1], a.shape[2]) for o, a in zip(outs, arrs)]
 
-def line_gather_kernel(x_ref, o_ref, ss, rs):
+def line_barrier(y, x, c, s):
+    bar = pltpu.get_barrier_semaphore()
+    @pl.when(s > 0)
+    def _(): pl.semaphore_signal(bar, inc=1, device_id=dev(y, x, c, s - 1), device_id_type=MESH)
+    @pl.when(s < NZ - 1)
+    def _(): pl.semaphore_signal(bar, inc=1, device_id=dev(y, x, c, s + 1), device_id_type=MESH)
+    pl.semaphore_wait(bar, jnp.where(s > 0, 1, 0) + jnp.where(s < NZ - 1, 1, 0))
+
+def line_gather_kernel(parts, x_ref, o_ref, ss, rs):
     y, x, c, s = place()
-    bar = pltpu.get_barrier_semaphore()
-    for k in range(1, NZ):
-        pl.semaphore_signal(bar, inc=1, device_id=dev(y, x, c, lax.rem(s + k, NZ)), device_id_type=MESH)
-    pl.semaphore_wait(bar, NZ - 1)
-    def cp(k):
-        return pltpu.make_async_remote_copy(src_ref=x_ref, dst_ref=o_ref.at[s], send_sem=ss.at[k], recv_sem=rs.at[k],
-            device_id=dev(y, x, c, lax.rem(s + k, NZ)), device_id_type=MESH)
-    def back(k):
-        t = lax.rem(s + NZ - k, NZ)
-        return pltpu.make_async_remote_copy(src_ref=x_ref, dst_ref=o_ref.at[t], send_sem=ss.at[k], recv_sem=rs.at[k],
-            device_id=dev(y, x, c, t), device_id_type=MESH)
-    for k in (2, 1, 3): cp(k).start()
-    o_ref[s] = x_ref[...]
-    for k in range(1, NZ): back(k).wait_recv()
-    for k in range(1, NZ): cp(k).wait_send()
-
-def line_gather(x, cid):
+    line_barrier(y, x, c, s)
+    def cp(d, g, h):
+        src = x_ref.at[h] if d == 0 else o_ref.at[s - d * g, h]
+        k = 0 if g == 1 else 1
+        return pltpu.make_async_remote_copy(src_ref=src, dst_ref=o_ref.at[s - d * g, h], send_sem=ss.at[k, d, h], recv_sem=rs.at[k, d, h],
+            device_id=dev(y, x, c, s + g), device_id_type=MESH)
+    def arrived(d, g, h):
+        k = 0 if g == 1 else 1
+        ref = o_ref.at[s - (d + 1) * g, h]
+        return pltpu.make_async_remote_copy(src_ref=ref, dst_ref=ref, send_sem=ss.at[k, d, h], recv_sem=rs.at[k, d, h],
+            device_id=dev(y, x, c, s + g), device_id_type=MESH)
+    def sends(d, g): return (s >= d) & (s < NZ - 1) if g == 1 else (s + d <= NZ - 1) & (s > 0)
+    def gets(d, g): return s >= d + 1 if g == 1 else s + d + 1 <= NZ - 1
+    for d in range(NZ):
+        for h in range(parts):
+            for g in (1, -1):
+                if d:
+                    @pl.when(gets(d - 1, g))
+                    def _(): arrived(d - 1, g, h).wait_recv()
+                if d < NZ - 1:
+                    @pl.when(sends(d, g))
+                    def _(): cp(d, g, h).start()
+        if d == 0: o_ref[s] = x_ref[...]
+    for d in range(NZ - 1):
+        for h in range(parts):
+            for g in (1, -1):
+                @pl.when(sends(d, g))
+                def _(): cp(d, g, h).wait_send()
+
+def line_gather(x, cid, parts=4):
     if not placed():
         return lax.all_gather(x, "shard", axis=0, tiled=True)
-    sem = pltpu.SemaphoreType.DMA((NZ,))
-    o = pl.pallas_call(line_gather_kernel, out_shape=jax.ShapeDtypeStruct((NZ,) + x.shape, x.dtype),
+    R, C = x.shape
+    sem = pltpu.SemaphoreType.DMA((2, NZ, parts))
+    o = pl.pallas_call(functools.partial(line_gather_kernel, parts), out_shape=jax.ShapeDtypeStruct((NZ, parts, R // parts, C), x.dtype),
         in_specs=[pl.BlockSpec(memory_space=pltpu.VMEM)], out_specs=pl.BlockSpec(memory_space=pltpu.VMEM),
         scratch_shapes=[sem, sem], compiler_params=pltpu.CompilerParams(collective_id=cid, has_side_effects=True, vmem_limit_bytes=16 << 20),
-        name="line_gather")(x)
-    return o.reshape(NZ * x.shape[0], x.shape[1])
-
-def line_scatter_kernel(p_ref, o_ref, buf, ss, rs):
+        name="line_gather")(x.reshape(parts, R // parts, C))
+    return o.reshape(NZ * R, C)
+
+def line_scatter_kernel(parts, p_ref, o_ref, acc, zu, zd, ss_u, rs_u, ss_d, rs_d):
     y, x, c, s = place()
-    bar = pltpu.get_barrier_semaphore()
-    for k in range(1, NZ):
-        pl.semaphore_signal(bar, inc=1, device_id=dev(y, x, c, lax.rem(s + k, NZ)), device_id_type=MESH)
-    pl.semaphore_wait(bar, NZ - 1)
-    def cp(k):
-        t = lax.rem(s + k, NZ)
-        return pltpu.make_async_remote_copy(src_ref=p_ref.at[t], dst_ref=buf.at[k], send_sem=ss.at[k], recv_sem=rs.at[k],
-            device_id=dev(y, x, c, t), device_id_type=MESH)
-    for k in (2, 1, 3): cp(k).start()
-    for k in (1, 3, 2): cp(k).wait_recv()
+    line_barrier(y, x, c, s)
+    def rc(src, dst, a, b, d):
+        return pltpu.make_async_remote_copy(src_ref=src, dst_ref=dst, send_sem=a, recv_sem=b, device_id=d, device_id_type=MESH)
+    def cu(zz, h, k):
+        src = p_ref.at[zz, h] if k == 0 else acc.at[zz, h]
+        return rc(src, zu.at[zz, h], ss_u.at[zz, h], rs_u.at[zz, h], dev(y, x, c, s + 1))
+    def cd(zz, h, k):
+        src = p_ref.at[zz, h] if k == 0 else acc.at[zz, h]
+        return rc(src, zd.at[zz, h], ss_d.at[zz, h], rs_d.at[zz, h], dev(y, x, c, s - 1))
     st = 32
-    @pl.loop(0, o_ref.shape[0] // st)
-    def _(i):
-        r = pl.ds(i * st, st)
-        t = p_ref[s, r, :].astype(jnp.float32)
-        for k in range(1, NZ): t = t + buf[k, r, :].astype(jnp.float32)
-        o_ref[r, :] = t
-    for k in range(1, NZ): cp(k).wait_send()
-
-def line_scatter(p, cid):
+    def total(dst, refs):
+        @pl.loop(0, dst.shape[0] // st)
+        def _(i):
+            r = pl.ds(i * st, st)
+            t = refs[0][r, :].astype(jnp.float32)
+            for f in refs[1:]: t = t + f[r, :].astype(jnp.float32)
+            dst[r, :] = t.astype(dst.dtype)
+    ups = [(zz, h) for zz in (3, 2, 1) for h in range(parts)]
+    dns = [(zz, h) for zz in (0, 1, 2) for h in range(parts)]
+    n = len(ups)
+    for i in range(n + NZ):
+        for k in range(NZ - 1):
+            if 0 <= i - k < n:
+                zz, h = ups[i - k]
+                if k < zz:
+                    @pl.when(s == k)
+                    def _():
+                        if k:
+                            cu(zz, h, k).wait_recv()
+                            total(acc.at[zz, h], [p_ref.at[zz, h], zu.at[zz, h]])
+                        cu(zz, h, k).start()
+                zz, h = dns[i - k]
+                if NZ - 1 - k > zz:
+                    @pl.when(s == NZ - 1 - k)
+                    def _():
+                        if k:
+                            cd(zz, h, k).wait_recv()
+                            total(acc.at[zz, h], [p_ref.at[zz, h], zd.at[zz, h]])
+                        cd(zz, h, k).start()
+    for zz in range(NZ):
+        @pl.when(s == zz)
+        def _():
+            for h in range(parts):
+                refs = [p_ref.at[zz, h]]
+                if zz > 0:
+                    cu(zz, h, 1).wait_recv()
+                    refs.append(zu.at[zz, h])
+                if zz < NZ - 1:
+                    cd(zz, h, 1).wait_recv()
+                    refs.append(zd.at[zz, h])
+                total(o_ref.at[h], refs)
+    for zz, h in ups:
+        @pl.when(s < zz)
+        def _(): cu(zz, h, 1).wait_send()
+    for zz, h in dns:
+        @pl.when(s > zz)
+        def _(): cd(zz, h, 1).wait_send()
+
+def line_scatter(p, cid, parts=4):
     if not placed():
         return lax.psum_scatter(p, "shard", scatter_dimension=0, tiled=True).astype(jnp.float32)
     R, C = p.shape[0] // NZ, p.shape[1]
-    sem = pltpu.SemaphoreType.DMA((NZ,))
-    return pl.pallas_call(line_scatter_kernel, out_shape=jax.ShapeDtypeStruct((R, C), jnp.float32),
+    sem = pltpu.SemaphoreType.DMA((NZ, parts))
+    shape = (NZ, parts, R // parts, C)
+    buf = pltpu.VMEM(shape, p.dtype)
+    o = pl.pallas_call(functools.partial(line_scatter_kernel, parts), out_shape=jax.ShapeDtypeStruct(shape[1:], jnp.float32),
         in_specs=[pl.BlockSpec(memory_space=pltpu.VMEM)], out_specs=pl.BlockSpec(memory_space=pltpu.VMEM),
-        scratch_shapes=[pltpu.VMEM((NZ, R, C), p.dtype), sem, sem], compiler_params=pltpu.CompilerParams(collective_id=cid, has_side_effects=True, vmem_limit_bytes=16 << 20),
-        name="line_scatter")(p.reshape(NZ, R, C))
+        scratch_shapes=[buf, buf, buf, sem, sem, sem, sem], compiler_params=pltpu.CompilerParams(collective_id=cid, has_side_effects=True, vmem_limit_bytes=24 << 20),
+        name="line_scatter")(p.reshape(shape))
+    return o.reshape(R, C)
 
 
 def dot(a, b, ca, cb):
@@ -548,7 +624,7 @@
     pieces = [w_router.reshape(-1), g_attn, g_ffn, g_query, g_key]
     sizes = [p.shape[0] for p in pieces]
     used = sum(sizes)
-    small_rows = -(-used // (32 * 128)) * 32
+    small_rows = -(-used // (64 * 128)) * 64
     small = jnp.concatenate(pieces + [jnp.zeros((small_rows * 128 - used,), bf)]).reshape(small_rows, 128)
     wqkv = jnp.concatenate([w_query, w_key, w_value], axis=1)
     wqkv_full, small_all = gather_all([wqkv, small], 1)
@@ -557,7 +633,9 @@
     wr_full, attn_gain, ffn_gain, query_gain, key_gain = [small_all[:, o : o + n].reshape(-1) for o, n in zip(starts, sizes)]
     wr_full = wr_full.reshape(model_width, expert_count)
     attn_gain, ffn_gain, query_gain, key_gain = [g.astype(f32) for g in (attn_gain, ffn_gain, query_gain, key_gain)]
+    w_out, wqkv_full = lax.optimization_barrier((w_out, wqkv_full))
     wo_full = lax.all_gather(w_out, BOTH, axis=0, tiled=True)
+    cotangent, _ = lax.optimization_barrier((cotangent, wo_full[:8, :128]))
     cot_all = lax.all_gather(cotangent, BOTH, axis=0, tiled=True)
 
     positions = shard_pos * tok_rows + jnp.arange(tok_rows, dtype=jnp.int32)
@@ -614,7 +692,8 @@
         payload_all, cot_all, w_gate, w_up, w_down, expert_count, tok_rows, capacity
     )
     (grad_sum,) = scatter_all([grad_part], 4)
-    (moe_out,) = scatter_all([out_part], 5)
+    moe_out = lax.psum_scatter(out_part, "expert", scatter_dimension=0, tiled=True)
+    moe_out = lax.psum_scatter(moe_out, "shard", scatter_dimension=0, tiled=True).astype(f32)
     block_out = (residual + moe_out).astype(bf)
     upstream = cotangent.astype(f32)
     grad_ffn = grad_sum[:, :model_width]
@@ -661,8 +740,7 @@
     packed = jnp.concatenate(
         [g.astype(bf).reshape(devices, -1) for g in grads] + [jnp.zeros((devices, small_rows * 128 - used), bf)], axis=1
     ).reshape(devices * small_rows, 128)
-    (out_grad,) = scatter_all([grad_wout], 7)
-    qkv_grad, small_grad = scatter_all([grad_wqkv, packed], 8)
+    out_grad, qkv_grad, small_grad = scatter_all([grad_wout, grad_wqkv, packed], 8)
     small_grad = small_grad.reshape(-1)
     router_g, attn_g, ffn_g, query_g, key_g = [small_grad[o : o + n] for o, n in zip(starts, sizes)]
     return (

time: 1730 us -> 1570 us (0.908)
  Pallas kernels: 1390 us -> 1020 us
  waiting for transfers between devices: 1.39 us -> 233 us
    pallas_call x6 -> x4, Pallas kernels: 905 us -> 515 us  [the longest x2 403 us: rs32(): pl.pallas_call(functools.partial(rs_kernel, n, parts), out_shape=[jax.Sha...]
    reduce_scatter x0 -> x2, waiting for transfers between devices: none -> 233 us  [the longest x1 233 us: per_device(): lax.psum_scatter(out_part, 'expert', scatter_dimension=0, tiled=True)]
    unnamed x139 -> x121, local copies, waits for them, and re-layouts: 49.6 us -> 31.6 us
  transfers between devices with their start and end apart: 2 -> 4, of which waited for: 0 -> 1; matrix products, arithmetic and copies ran while one was open for 7% -> 8% of each run, Pallas kernels for 23% -> 33%
where the time goes in v2:
time: 1570 us; the launch traced here: 1560 us
  Pallas kernels  1020 us (65%)
  waiting for transfers between devices  233 us (15%)
  matrix products  140 us (9%)
  local copies, waits for them, and re-layouts  93.8 us (6%)
  other arithmetic  54.7 us (3%)
    pallas_call x2, Pallas kernels, rs32(): pl.pallas_call(functools.partial(rs_kernel, n, parts), out_shape=[jax.Sha...  403 us
    pallas_call x2, Pallas kernels, ag32(): pl.pallas_call(functools.partial(ag_kernel, n), out_shape=[jax.ShapeDtype...  325 us
    reduce_scatter x1, waiting for transfers between devices, per_device(): lax.psum_scatter(out_part, 'expert', scatter_dimension=0, tiled=True)  233 us
    pallas_call x1, Pallas kernels, experts_call(): pl.pallas_call(functools.partial(expert_kernel, experts, slots, SB), grid...  179 us
    pallas_call x1, Pallas kernels, line_gather(): pl.pallas_call(functools.partial(line_gather_kernel, parts), out_shape=ja...  78.7 us
    pallas_call x1, Pallas kernels, line_scatter(): pl.pallas_call(functools.partial(line_scatter_kernel, parts), out_shape=j...  33.9 us
    unnamed x121, local copies, waits for them, and re-layouts  31.6 us
  transfers between devices with their start and end apart: 4, of which 1 were waited for; matrix products, arithmetic and copies ran while one was open for 8% of the time, Pallas kernels for 33%

profile of v2, /device:TPU:18, one launch (start us, length us, event | category | flops | bytes accessed | tf_op | source)
XLA Modules:
  0.0 1557.6 jit_solution(5105751383164783270)
XLA Ops:
  10.2 3.4 concatenate.42
  13.6 98.4 %gather_all.2 = (bf16[2,2,2,4,2,32,5120]{6,5,4,3,2,1,0:T(8,128)(2,1)}, bf16[2,2,2,4,2,32,128]{6,5,4,3,2,1,0:T(8,128)(2,1)}) custom-call(bf16[2,32,5120]{2,1,0:T(8,128)(2,1)} %bitcast.224, bf16[2,32,128]{2,1,0:T(8,128)(2,1)} %bitcast.236), custom_call_target="tpu_custom_call" | custom-call | tf_op jit(solution)/shard_map/gather_all/pallas_call | solution.py:144
  115.1 9.9 fusion.76
  134.0 78.7 %line_gather.1 = bf16[4,4,64,1024]{3,2,1,0:T(8,128)(2,1)S(1)} custom-call(bf16[4,64,1024]{2,1,0:T(8,128)(2,1)S(1)} %bitcast.202), custom_call_target="tpu_custom_call" | custom-call | tf_op jit(solution)/shard_map/line_gather/pallas_call | solution.py:331
  219.2 2.4 copy.137
  221.6 6.6 slice_bitcast_fusion
  228.2 5.6 copy.124
  233.9 2.9 multiply_reduce_fusion.3
  238.4 2.4 slice_negate_fusion.1
  240.7 3.8 copy.127
  244.6 3.8 copy.128
  248.4 5.0 copy.180
  254.0 8.7 fusion.66
  262.7 33.6 %while.28 = (s32[]{:T(128)}, bf16[4,256,8,128]{1,3,2,0:T(8,128)(2,1)}, f32[4,256,8]{1,2,0:T(8,128)}, bf16[4,256,8,128]{3,1,2,0:T(8,128)(2,1)}, bf16[4,1024,128]{...) while((s32[]{:T(128)}, ...), condition=%wide.region_5.6_spmd.clone, body=%wide.region_3.5_spmd.clone.sunk | while | flops 1084487680 | bytes 36474508 | solution.py:667
  262.9 3.0 fusion.124
  265.9 3.3 fusion.125
  271.3 3.0 fusion.124
  274.3 3.3 fusion.125
  279.7 2.9 fusion.124
  282.7 3.3 fusion.125
  288.1 3.0 fusion.124
  291.1 3.3 fusion.125
  296.3 9.3 multiply_reduce_fusion.6
  310.6 226.7 %gather_all.3 = bf16[2,2,2,4,2,128,2176]{6,5,4,3,2,1,0:T(8,128)(2,1)} custom-call(bf16[2,128,2176]{2,1,0:T(8,128)(2,1)} %bitcast.220), custom_call_target="tpu_custom_call" | custom-call | tf_op jit(solution)/shard_map/gather_all/pallas_call | solution.py:144
  537.3 179.5 %experts.1 = (bf16[8192,2048]{1,0:T(8,128)(2,1)}, bf16[8192,2176]{1,0:T(8,128)(2,1)}, f32[1,2048,768]{2,1,0:T(8,128)}, f32[1,2048,768]{2,1,0:T(8,128)}, f32[1,768,2048]{2,1,0:T(8,128)}) custom-call(bf16[8192,2176]{1,0:T(8,128)(2,1)} %bitcast.207, bf16[8192,2048]{1,0:T(8,128)(2,1)} %all-gather.5.cloned.1.call-done.cot_ref, bf16[1,2048,768]{2,1,0:T(8,128)(2,1)} %wg_hbm.1, ...), custom_call_target="tpu_custom_call" | custom-call | flops 133000003584 | bytes 160000000 | tf_op jit(solution)/shard_map/experts/pallas_call | solution.py:485
  716.8 232.5 %reduce-scatter.3.cloned.1.call-done = bf16[1024,2048]{1,0:T(8,128)(2,1)} async-done(((bf16[8192,2048]{1,0:T(8,128)(2,1)}), bf16[1024,2048]{1,0:T(8,128)(2,1)}) %reduce-scatter.3.cloned.1.call-update) | async-done | bytes 4194320 | tf_op jit(solution)/shard_map/reduce_scatter | solution.py:695
  949.5 204.6 %scatter_all.2 = f32[4,64,2176]{2,1,0:T(8,128)} custom-call(bf16[2,2,2,4,4,64,2176]{6,5,4,3,2,1,0:T(8,128)(2,1)} %bitcast.206), custom_call_target="tpu_custom_call" | custom-call | tf_op jit(solution)/shard_map/scatter_all/pallas_call | solution.py:275
  1160.3 3.8 multiply_reduce_fusion.4
  1164.8 4.3 subtract_add_fusion
  1169.1 10.9 fusion.67
  1181.4 55.9 %while.29 = (s32[]{:T(128)}, f32[4,256,8,128]{3,1,2,0:T(8,128)}, bf16[4,1024,128]{2,1,0:T(8,128)(2,1)}, bf16[4,1024,128]{2,1,0:T(8,128)(2,1)}, bf16[4,256,8,128]...) while((s32[]{:T(128)}, f32[4,256,8,128]{3,1,2,0:T(8,128)}, ...), condition=%wide.region_15.16_spmd.clone, body=%wide.region_13.15_spmd.clone.sunk | while | flops 2701391872 | bytes 85244104 | solution.py:717
  1181.6 2.4 fusion.134
  1184.9 3.0 multiply_reduce_fusion.12
  1198.9 3.0 multiply_reduce_fusion.12
  1209.5 2.4 fusion.134
  1212.8 3.0 multiply_reduce_fusion.12
  1226.7 3.0 multiply_reduce_fusion.12
  1242.6 33.9 %line_scatter.1 = f32[4,64,1024]{2,1,0:T(8,128)S(1)} custom-call(bf16[4,4,64,1024]{3,2,1,0:T(8,128)(2,1)S(1)} %pad_maximum_fusion.1.p_ref), custom_call_target="tpu_custom_call" | custom-call | tf_op jit(solution)/shard_map/line_scatter/pallas_call | solution.py:404
  1276.5 5.8 copy.145
  1282.4 2.6 bitcast_multiply_fusion
  1288.4 4.0 multiply_reduce_fusion.1
  1295.8 6.2 fusion.48
  1302.0 11.8 fusion.65
  1313.7 11.8 convolution_convert_fusion
  1325.6 12.6 convolution_convert_fusion.1
  1340.0 197.9 %scatter_all.3 = (f32[4,32,2048]{2,1,0:T(8,128)}, f32[4,16,5120]{2,1,0:T(8,128)}, f32[4,16,128]{2,1,0:T(8,128)}) custom-call(bf16[2,2,2,4,4,32,2048]{6,5,4,3,2,1,0:T(8,128)(2,1)} %bitcast.205, bf16[2,2,2,4,4,16,5120]{6,5,4,3,2,1,0:T(8,128)(2,1)} %bitcast.204, bf16[2,2,2,4,4,16,128]{6,5,4,3,2,1,0:T(8,128)(2,1)} %bitcast.225), custom_call_target="tpu_custom_call" | custom-call | tf_op jit(solution)/shard_map/scatter_all/pallas_call | solution.py:275
  1537.9 2.4 slice.132
  1546.1 3.8 fusion.62
  (296 shorter events, 104.3 us)
Async XLA Ops:
  7.2 107.0 %copy-start.5 = (bf16[256,2048]{1,0:T(8,128)(2,1)S(1)}, bf16[256,2048]{1,0:T(8,128)(2,1)}, u32[]{:S(2)}) copy-start(bf16[256,2048]{1,0:T(8,128)(2,1)} %param.19) | copy-start | bytes 3145732
  7.2 289.1 %all-gather.3.cloned.1.call-start = ((), (), s32[]{:S(2)}) async-start(), calls=%async_computation.2 | async-start | bytes 17301504 | tf_op jit(solution)/shard_map/all_gather | solution.py:637
  112.0 425.3 %all-gather.5.cloned.1.call-start = ((), (), s32[]{:S(2)}) async-start(), calls=%async_computation.3 | async-start | bytes 34603008 | tf_op jit(solution)/shard_map/all_gather | solution.py:639
  112.7 836.7 %reduce-scatter.3.cloned.1.call-start = ((), (), s32[]{:S(2)}) async-start(), calls=%async_computation.4 | async-start | bytes 37748736 | tf_op jit(solution)/shard_map/reduce_scatter | solution.py:695
  114.1 15.0 copy-start.30
  114.2 10.8 copy-start.36
  115.1 9.9 copy-start.44
  115.1 12.4 copy-start.57
  127.8 4.8 copy-start.9
  129.0 4.9 copy-start.19
  129.2 4.7 copy-start.53
  130.3 123.7 %copy-start.23 = (f32[256,128]{1,0:T(8,128)}, f32[256,128]{1,0:T(8,128)S(1)}, u32[]{:S(2)}) copy-start(f32[256,128]{1,0:T(8,128)S(1)} %copy.129) | copy-start | bytes 393220
  131.1 122.9 %copy-start.21 = (f32[256,128]{1,0:T(8,128)}, f32[256,128]{1,0:T(8,128)S(1)}, u32[]{:S(2)}) copy-start(f32[256,128]{1,0:T(8,128)S(1)} %copy.126) | copy-start | bytes 393220
  233.9 20.1 %copy-start.55 = (f32[128]{0:T(128)}, f32[128]{0:T(128)S(1)}, u32[]{:S(2)}) copy-start(f32[128]{0:T(128)S(1)} %reshape.281) | copy-start | bytes 1540
  233.9 3.7 copy-start
  248.4 5.1 slice-start
  253.5 52.8 %copy-start.40 = (f32[2048]{0:T(1024)}, f32[2048]{0:T(1024)S(1)}, u32[]{:S(2)}) copy-start(f32[2048]{0:T(1024)S(1)} %reshape.283) | copy-start | bytes 24580
  253.9 53.4 %copy-start.17 = (bf16[2048,32]{1,0:T(8,128)(2,1)}, bf16[2048,32]{1,0:T(8,128)(2,1)S(1)}, u32[]{:S(2)}) copy-start(bf16[2048,32]{1,0:T(8,128)(2,1)S(1)} %reshape_reshape.26) | copy-start | bytes 393220
  296.3 9.3 copy-start.11
  296.3 9.4 copy-start.42
  306.3 4.3 copy-start.51
  716.8 448.0 %reduce-scatter.5.cloned.1.call-start = ((), (), s32[]{:S(2)}) async-start(), calls=%async_computation.5 | async-start | bytes 5242880 | tf_op jit(solution)/shard_map/reduce_scatter | solution.py:696
  949.4 204.7 %copy-start.26 = (f32[256,32]{1,0:T(8,128)S(1)}, f32[256,32]{1,0:T(8,128)}, u32[]{:S(2)}) copy-start(f32[256,32]{1,0:T(8,128)} %copy-done.25) | copy-start | bytes 98308
  949.5 204.7 %copy-start.50 = (f32[256]{0:T(256)S(1)}, f32[256]{0:T(256)}, u32[]{:S(2)}) copy-start(f32[256]{0:T(256)} %copy-done.49) | copy-start | bytes 3076
  949.5 207.2 %copy-start.8 = (bf16[256,2048]{1,0:T(8,128)(2,1)S(1)}, bf16[256,2048]{1,0:T(8,128)(2,1)}, u32[]{:S(2)}) copy-start(bf16[256,2048]{1,0:T(8,128)(2,1)} %copy-done.7) | copy-start | bytes 3145732
  949.5 210.8 %copy-start.41 = (f32[2048]{0:T(1024)S(1)}, f32[2048]{0:T(1024)}, u32[]{:S(2)}) copy-start(f32[2048]{0:T(1024)} %copy-done.40) | copy-start | bytes 24580
  949.5 210.8 %copy-start.52 = (f32[256]{0:T(256)S(1)}, f32[256]{0:T(256)}, u32[]{:S(2)}) copy-start(f32[256]{0:T(256)} %copy-done.51) | copy-start | bytes 3076
  1154.2 6.2 copy-start.4
  1157.0 7.8 copy-start.18
  1157.0 7.8 copy-start.59
  1181.6 3.3 copy-start.15
  1195.6 3.3 copy-start.15
  1209.5 3.3 copy-start.15
  1223.4 3.3 copy-start.15
  1276.5 5.8 copy-start.34
  1282.3 3.1 copy-start.32
  1282.3 3.1 copy-start.33
  1285.0 3.5 copy-start.2
  1285.0 3.5 copy-start.56
  1288.4 4.0 copy-start.39
  1288.4 4.2 copy-start.24
  1295.7 6.2 copy-start.6
  1295.7 6.2 copy-start.37
  1295.8 6.2 copy-start.45
  1325.6 13.0 copy-start.35
  1325.6 13.0 copy-start.48
  1340.0 206.1 %copy-start.58 = (f32[256]{0:T(256)S(1)}, f32[256]{0:T(256)}, u32[]{:S(2)}) copy-start(f32[256]{0:T(256)} %get-tuple-element.395) | copy-start | bytes 3076
  1537.9 12.0 copy-start.29
  (32 other events, 53.5 us)
Sparse Core Ops, SparseCore 0:
  112.1 131.2 all-gather.2
  246.3 277.8 all-gather.4
  716.9 232.4 reduce-scatter.2
  951.5 100.9 reduce-scatter.4

commit v3 on v2

--- a/solution.py
+++ b/solution.py
@@ -411,88 +411,142 @@
 def dot(a, b, ca, cb):
     return lax.dot_general(a, b, (((ca,), (cb,)), ((), ())), preferred_element_type=jnp.float32)
 
-def expert_kernel(experts, slots, SB, x_ref, cot_ref, wg_hbm, wu_hbm, wd_hbm, out_ref, gr_ref, dwg_hbm, dwu_hbm, dwd_hbm,
-                  wg, wu, wd, dwg, dwu, dwd, rows, gp, wsem, osem):
+def token_picks(meta, experts, slots, me):
+    SB, WM = meta.shape
+    bf, f32 = jnp.bfloat16, jnp.float32
+    tri = (lax.broadcasted_iota(jnp.int32, (SB, SB), 1) < lax.broadcasted_iota(jnp.int32, (SB, SB), 0)).astype(bf)
+    lane = lax.broadcasted_iota(jnp.int32, (SB, WM), 1)
+    cnt = dot(tri, meta, 1, 0)
+    metaf = meta.astype(f32)
+    msk = jnp.sum(jnp.where(lane == me, metaf, 0.0), axis=-1, keepdims=True)
+    pos = jnp.sum(jnp.where(lane == me, cnt, 0.0), axis=-1, keepdims=True)
+    gate = jnp.sum(jnp.where((lane == me + experts) | (lane == me + 2 * experts), metaf, 0.0), axis=-1, keepdims=True)
+    want = jnp.where(msk > 0.0, pos, -1.0).astype(jnp.int32)
+    pick = (want == lax.broadcasted_iota(jnp.int32, (SB, slots), 1)).astype(bf)
+    return pick, gate
+
+def forward_kernel(experts, slots, SB, x_ref, wg_hbm, wu_hbm, wd_hbm, out_ref, rows_ref, ga_ref, ua_ref, wg, wu, wd, wsem):
     bf = jnp.bfloat16
     step = pl.program_id(0)
     nsub = x_ref.shape[0] // SB
+    D = out_ref.shape[1]
+    me = lax.axis_index(("expert", "shard"))
+    loads = [pltpu.make_async_copy(h.at[0], v, wsem.at[i]) for i, (h, v) in enumerate(((wg_hbm, wg), (wu_hbm, wu), (wd_hbm, wd)))]
+    @pl.when(step == 0)
+    def _():
+        for l in loads: l.start()
+    picks, gates = [], []
+    for i in range(nsub):
+        r = pl.ds(i * SB, SB)
+        pick, gate = token_picks(x_ref[r, D:], experts, slots, me)
+        picks.append(pick); gates.append(gate)
+        rows_ref[i * slots:(i + 1) * slots, :] = dot(pick, x_ref[r, :D], 0, 0).astype(bf)
+    @pl.when(step == 0)
+    def _():
+        for l in loads: l.wait()
+    ga = dot(rows_ref[...], wg[...], 1, 0)
+    ua = dot(rows_ref[...], wu[...], 1, 0)
+    ga_ref[...] = ga
+    ua_ref[...] = ua
+    hid = (ga * (1.0 / (1.0 + jnp.exp(-ga))) * ua).astype(bf)
+    eo = dot(hid, wd[...], 1, 0).astype(bf)
+    for i in range(nsub):
+        r = pl.ds(i * SB, SB)
+        tok = dot(picks[i], eo[i * slots:(i + 1) * slots, :], 1, 0)
+        out_ref[r, :] = (gates[i] * tok).astype(bf)
+
+def backward_kernel(experts, slots, SB, meta_ref, cot_ref, rows_ref, ga_ref, ua_ref, wg_hbm, wu_hbm, wd_hbm, gr_ref, dwg_hbm, dwu_hbm, dwd_hbm,
+                  wg, wu, wd, dwg, dwu, dwd, gp, wsem, osem):
+    bf = jnp.bfloat16
+    step = pl.program_id(0)
+    nsub = cot_ref.shape[0] // SB
     D = cot_ref.shape[1]
-    WM = x_ref.shape[1] - D
+    WM = meta_ref.shape[1]
     me = lax.axis_index(("expert", "shard"))
     loads = [pltpu.make_async_copy(h.at[0], v, wsem.at[i]) for i, (h, v) in enumerate(((wg_hbm, wg), (wu_hbm, wu), (wd_hbm, wd)))]
     @pl.when(step == 0)
     def _():
         for l in loads: l.start()
         for a in (dwg, dwu, dwd): a[...] = jnp.zeros_like(a)
-    tri = (lax.broadcasted_iota(jnp.int32, (SB, SB), 1) < lax.broadcasted_iota(jnp.int32, (SB, SB), 0)).astype(bf)
-    lane = lax.broadcasted_iota(jnp.int32, (SB, WM), 1)
-    picks, gates = [], []
+    picks = []
     for i in range(nsub):
         r = pl.ds(i * SB, SB)
-        meta = x_ref[r, D:]
-        cnt = dot(tri, meta, 1, 0)
-        metaf = meta.astype(jnp.float32)
-        msk = jnp.sum(jnp.where(lane == me, metaf, 0.0), axis=-1, keepdims=True)
-        pos = jnp.sum(jnp.where(lane == me, cnt, 0.0), axis=-1, keepdims=True)
-        gate = jnp.sum(jnp.where((lane == me + experts) | (lane == me + 2 * experts), metaf, 0.0), axis=-1, keepdims=True)
-        want = jnp.where(msk > 0.0, pos, -1.0).astype(jnp.int32)
-        pick = (want == lax.broadcasted_iota(jnp.int32, (SB, slots), 1)).astype(bf)
-        picks.append(pick); gates.append(gate)
-        rows[i * slots:(i + 1) * slots, :] = dot(pick, x_ref[r, :D], 0, 0).astype(bf)
+        pick, gate = token_picks(meta_ref[r, :], experts, slots, me)
+        picks.append(pick)
         gcot = (gate * cot_ref[r, :].astype(jnp.float32)).astype(bf)
         gp[i * slots:(i + 1) * slots, :] = dot(pick, gcot, 0, 0).astype(bf)
     @pl.when(step == 0)
     def _():
         for l in loads: l.wait()
-    ga = dot(rows[...], wg[...], 1, 0)
-    ua = dot(rows[...], wu[...], 1, 0)
+    ga = ga_ref[...]
+    ua = ua_ref[...]
     sig = 1.0 / (1.0 + jnp.exp(-ga))
     act = ga * sig
-    hid = (act * ua).astype(bf)
-    eo = dot(hid, wd[...], 1, 0).astype(bf)
-    gg = []
-    for i in range(nsub):
-        r = pl.ds(i * SB, SB)
-        tok = dot(picks[i], eo[i * slots:(i + 1) * slots, :], 1, 0)
-        out_ref[r, :] = (gates[i] * tok).astype(bf)
-        gg.append(jnp.sum(tok * cot_ref[r, :].astype(jnp.float32), axis=-1, keepdims=True))
+    hidf = act * ua
+    hid = hidf.astype(bf)
     gh = dot(gp[...], wd[...], 1, 1)
+    share = jnp.sum(gh * hid.astype(jnp.float32), axis=-1, keepdims=True)
     dga = (gh * ua * (sig * (1.0 + ga * (1.0 - sig)))).astype(bf)
     dua = (gh * act).astype(bf)
     dwd[...] += dot(hid, gp[...], 0, 0)
     grow = (dot(dga, wg[...], 1, 1) + dot(dua, wu[...], 1, 1)).astype(bf)
-    dwg[...] += dot(rows[...], dga, 0, 0)
-    dwu[...] += dot(rows[...], dua, 0, 0)
+    dwg[...] += dot(rows_ref[...], dga, 0, 0)
+    dwu[...] += dot(rows_ref[...], dua, 0, 0)
+    lane = lax.broadcasted_iota(jnp.int32, (share.shape[0], WM), 1)
+    high = share.astype(bf).astype(jnp.float32)
+    tail = (jnp.where(lane == me, high, 0.0) + jnp.where(lane == me + experts, share - high, 0.0)).astype(bf)
     for i in range(nsub):
         r = pl.ds(i * SB, SB)
-        gr_ref[r, :D] = dot(picks[i], grow[i * slots:(i + 1) * slots, :], 1, 0).astype(bf)
-        hi = gg[i].astype(bf).astype(jnp.float32)
-        lo = gg[i] - hi
-        gr_ref[r, D:] = (jnp.where(lane == me, hi, 0.0) + jnp.where(lane == me + experts, lo, 0.0)).astype(bf)
+        q = slice(i * slots, (i + 1) * slots)
+        gr_ref[r, :D] = dot(picks[i], grow[q, :], 1, 0).astype(bf)
+        gr_ref[r, D:] = dot(picks[i], tail[q, :], 1, 0).astype(bf)
     @pl.when(step == pl.num_programs(0) - 1)
     def _():
         outs = [pltpu.make_async_copy(v, h.at[0], osem.at[i]) for i, (v, h) in enumerate(((dwg, dwg_hbm), (dwu, dwu_hbm), (dwd, dwd_hbm)))]
         for o in outs: o.start()
         for o in outs: o.wait()
 
-def experts_call(x_all, cot_all, w_gate, w_up, w_down, experts, block, capacity, TB=512, SB=256):
-    T, C = x_all.shape; D = cot_all.shape[1]
-    F = w_gate.shape[2]
+def experts_forward(x_all, w_gate, w_up, w_down, experts, block, capacity, TB=512, SB=256):
+    T, C = x_all.shape; D, F = w_gate.shape[1:]
     slots = max(SB // block, 1) * capacity
     total = TB // SB * slots
+    S = T // SB * slots
     any_ = pl.BlockSpec(memory_space=pl.ANY)
     V = pltpu.VMEM; bf = jnp.bfloat16; f32 = jnp.float32
+    blk = lambda r, c: pl.BlockSpec((r, c), lambda i: (i, 0))
     return pl.pallas_call(
-        functools.partial(expert_kernel, experts, slots, SB),
+        functools.partial(forward_kernel, experts, slots, SB),
         grid=(T // TB,),
-        out_shape=[jax.ShapeDtypeStruct((T, D), bf), jax.ShapeDtypeStruct((T, C), bf), jax.ShapeDtypeStruct(w_gate.shape, f32), jax.ShapeDtypeStruct(w_up.shape, f32), jax.ShapeDtypeStruct(w_down.shape, f32)],
-        in_specs=[pl.BlockSpec((TB, C), lambda i: (i, 0)), pl.BlockSpec((TB, D), lambda i: (i, 0)), any_, any_, any_],
-        out_specs=[pl.BlockSpec((TB, D), lambda i: (i, 0)), pl.BlockSpec((TB, C), lambda i: (i, 0)), any_, any_, any_],
-        scratch_shapes=[V((D, F), bf), V((D, F), bf), V((F, D), bf), V((D, F), f32), V((D, F), f32), V((F, D), f32), V((total, D), bf), V((total, D), bf), pltpu.SemaphoreType.DMA((3,)), pltpu.SemaphoreType.DMA((3,))],
+        out_shape=[jax.ShapeDtypeStruct((T, D), bf), jax.ShapeDtypeStruct((S, D), bf), jax.ShapeDtypeStruct((S, F), f32), jax.ShapeDtypeStruct((S, F), f32)],
+        in_specs=[blk(TB, C), any_, any_, any_],
+        out_specs=[blk(TB, D), blk(total, D), blk(total, F), blk(total, F)],
+        scratch_shapes=[V((D, F), bf), V((D, F), bf), V((F, D), bf), pltpu.SemaphoreType.DMA((3,))],
         compiler_params=pltpu.CompilerParams(dimension_semantics=("arbitrary",), vmem_limit_bytes=65000 * 1024),
-        cost_estimate=pl.CostEstimate(flops=133_000_000_000, bytes_accessed=160_000_000, transcendentals=0),
-        name="experts",
-    )(x_all, cot_all, w_gate, w_up, w_down)
+        cost_estimate=pl.CostEstimate(flops=48_000_000_000, bytes_accessed=130_000_000, transcendentals=0),
+        name="experts_forward",
+    )(x_all, w_gate, w_up, w_down)
+
+def experts_backward(x_all, cot_all, rows, ga, ua, w_gate, w_up, w_down, experts, block, capacity, TB=512, SB=256):
+    T, C = x_all.shape; D, F = w_gate.shape[1:]
+    slots = max(SB // block, 1) * capacity
+    total = TB // SB * slots
+    WM = C - D
+    any_ = pl.BlockSpec(memory_space=pl.ANY)
+    V = pltpu.VMEM; bf = jnp.bfloat16; f32 = jnp.float32
+    blk = lambda r, c: pl.BlockSpec((r, c), lambda i: (i, 0))
+    meta = pl.BlockSpec((TB, WM), lambda i: (i, D // WM)) if D % WM == 0 else blk(TB, WM)
+    meta_in = x_all if D % WM == 0 else x_all[:, D:]
+    return pl.pallas_call(
+        functools.partial(backward_kernel, experts, slots, SB),
+        grid=(T // TB,),
+        out_shape=[jax.ShapeDtypeStruct((T, C), bf), jax.ShapeDtypeStruct(w_gate.shape, f32), jax.ShapeDtypeStruct(w_up.shape, f32), jax.ShapeDtypeStruct(w_down.shape, f32)],
+        in_specs=[meta, blk(TB, D), blk(total, D), blk(total, F), blk(total, F), any_, any_, any_],
+        out_specs=[blk(TB, C), any_, any_, any_],
+        scratch_shapes=[V((D, F), bf), V((D, F), bf), V((F, D), bf), V((D, F), f32), V((D, F), f32), V((F, D), f32), V((total, D), bf), pltpu.SemaphoreType.DMA((3,)), pltpu.SemaphoreType.DMA((3,))],
+        compiler_params=pltpu.CompilerParams(dimension_semantics=("arbitrary",), vmem_limit_bytes=65000 * 1024),
+        cost_estimate=pl.CostEstimate(flops=85_000_000_000, bytes_accessed=150_000_000, transcendentals=0),
+        name="experts_backward",
+    )(meta_in, cot_all, rows, ga, ua, w_gate, w_up, w_down)
 
 HQ = 32
 HK = 4
@@ -627,15 +681,13 @@
     small_rows = -(-used // (64 * 128)) * 64
     small = jnp.concatenate(pieces + [jnp.zeros((small_rows * 128 - used,), bf)]).reshape(small_rows, 128)
     wqkv = jnp.concatenate([w_query, w_key, w_value], axis=1)
-    wqkv_full, small_all = gather_all([wqkv, small], 1)
+    wqkv_full, small_all, wo_full = gather_all([wqkv, small, w_out], 1)
     small_all = small_all.reshape(devices, small_rows * 128)
     starts = [sum(sizes[:i]) for i in range(5)]
     wr_full, attn_gain, ffn_gain, query_gain, key_gain = [small_all[:, o : o + n].reshape(-1) for o, n in zip(starts, sizes)]
     wr_full = wr_full.reshape(model_width, expert_count)
     attn_gain, ffn_gain, query_gain, key_gain = [g.astype(f32) for g in (attn_gain, ffn_gain, query_gain, key_gain)]
-    w_out, wqkv_full = lax.optimization_barrier((w_out, wqkv_full))
-    wo_full = lax.all_gather(w_out, BOTH, axis=0, tiled=True)
-    cotangent, _ = lax.optimization_barrier((cotangent, wo_full[:8, :128]))
+    cotangent, wo_full = lax.optimization_barrier((cotangent, wo_full))
     cot_all = lax.all_gather(cotangent, BOTH, axis=0, tiled=True)
 
     positions = shard_pos * tok_rows + jnp.arange(tok_rows, dtype=jnp.int32)
@@ -688,20 +740,21 @@
         axis=1,
     )
     (payload_all,) = gather_all([payload], 3)
-    out_part, grad_part, grad_wgate, grad_wup, grad_wdown = experts_call(
-        payload_all, cot_all, w_gate, w_up, w_down, expert_count, tok_rows, capacity
+    out_part, rows, gate_act, up_act = experts_forward(
+        payload_all, w_gate, w_up, w_down, expert_count, tok_rows, capacity
+    )
+    moe_out = lax.psum_scatter(out_part, "expert", scatter_dimension=0, tiled=True)
+    grad_part, grad_wgate, grad_wup, grad_wdown = experts_backward(
+        payload_all, cot_all, rows, gate_act, up_act, w_gate, w_up, w_down, expert_count, tok_rows, capacity
     )
     (grad_sum,) = scatter_all([grad_part], 4)
-    moe_out = lax.psum_scatter(out_part, "expert", scatter_dimension=0, tiled=True)
-    moe_out = lax.psum_scatter(moe_out, "shard", scatter_dimension=0, tiled=True).astype(f32)
-    block_out = (residual + moe_out).astype(bf)
     upstream = cotangent.astype(f32)
     grad_ffn = grad_sum[:, :model_width]
-    grad_gates = (
+    grad_shares = (
         grad_sum[:, model_width : model_width + expert_count]
         + grad_sum[:, model_width + expert_count : model_width + 2 * expert_count]
     )
-    grad_logits = (gates * (grad_gates - jnp.sum(gates * grad_gates, axis=-1, keepdims=True))).astype(bf)
+    grad_logits = (grad_shares - gates * jnp.sum(grad_shares, axis=-1, keepdims=True)).astype(bf)
     grad_wrouter = matmul_tn(ffn_low, grad_logits)
     grad_ffn = grad_ffn + matmul_nt(grad_logits, wr_full)
     grad_second, grad_ffn_gain = norm_back(residual, ffn_gain, grad_ffn)
@@ -709,6 +762,9 @@
     grad_attn_low = grad_residual.astype(bf)
     grad_wout = matmul_tn(mix_low, grad_attn_low).astype(bf)
     grad_mix = matmul_nt(grad_attn_low, wo_full).astype(bf)
+    grad_mix, grad_wout = lax.optimization_barrier((grad_mix, grad_wout))
+    out_grad = lax.psum_scatter(grad_wout, "expert", scatter_dimension=0, tiled=True)
+    out_grad = lax.psum_scatter(out_grad, "shard", scatter_dimension=0, tiled=True).astype(f32)
     grad_heads = grad_mix.reshape(tok_rows, HK, group_size, HD).transpose(1, 0, 2, 3)
 
     def attend_back(pieces):
@@ -726,6 +782,9 @@
         axis=1,
     )
     grad_kv = line_scatter(grad_kv, 6)
+    grad_kv, moe_out = lax.optimization_barrier((grad_kv, moe_out))
+    moe_out = lax.psum_scatter(moe_out, "shard", scatter_dimension=0, tiled=True).astype(f32)
+    block_out = (residual + moe_out).astype(bf)
     grad_q_proj, grad_query_gain = q_pull(grad_q_rot)
     grad_k_proj, grad_key_gain = k_pull(grad_kv[:, :kv_cols].reshape(tok_rows, HK, HD))
     grad_qkv_low = jnp.concatenate(
@@ -740,7 +799,7 @@
     packed = jnp.concatenate(
         [g.astype(bf).reshape(devices, -1) for g in grads] + [jnp.zeros((devices, small_rows * 128 - used), bf)], axis=1
     ).reshape(devices * small_rows, 128)
-    out_grad, qkv_grad, small_grad = scatter_all([grad_wout, grad_wqkv, packed], 8)
+    qkv_grad, small_grad = scatter_all([grad_wqkv, packed], 8)
     small_grad = small_grad.reshape(-1)
     router_g, attn_g, ffn_g, query_g, key_g = [small_grad[o : o + n] for o, n in zip(starts, sizes)]
     return (

time: 1570 us -> 1360 us (0.87)
  waiting for transfers between devices: 233 us -> 0.14 us
  local copies, waits for them, and re-layouts: 93.8 us -> 111 us
    reduce_scatter x1, waiting for transfers between devices: 233 us -> 0.03 us  [per_device(): lax.psum_scatter(out_part, 'expert', scatter_dimension=0, tiled=True)]
    pallas_call x1 -> x2, Pallas kernels: 179 us -> 202 us  [the longest x1 128 us: experts_backward(): pl.pallas_call(functools.partial(backward_kernel, experts, slots, SB), gr...]
    pallas_call x2, Pallas kernels: 403 us -> 385 us  [rs32(): pl.pallas_call(functools.partial(rs_kernel, n, parts), out_shape=[jax.Sha...]
    unnamed x121 -> x134, local copies, waits for them, and re-layouts: 31.6 us -> 45.6 us
  transfers between devices with their start and end apart: 4 -> 5, of which waited for: 1 -> 0; matrix products, arithmetic and copies ran while one was open for 8% -> 21% of each run, Pallas kernels for 33% -> 64%
where the time goes in v3:
time: 1360 us; the launch traced here: 1350 us
  Pallas kernels  1030 us (76%)
  matrix products  146 us (11%)
  local copies, waits for them, and re-layouts  111 us (8%)
  other arithmetic  50.1 us (4%)
  between operations  17.1 us (1%)
    pallas_call x2, Pallas kernels, rs32(): pl.pallas_call(functools.partial(rs_kernel, n, parts), out_shape=[jax.Sha...  385 us
    pallas_call x2, Pallas kernels, ag32(): pl.pallas_call(functools.partial(ag_kernel, n), out_shape=[jax.ShapeDtype...  324 us
    pallas_call x1, Pallas kernels, experts_backward(): pl.pallas_call(functools.partial(backward_kernel, experts, slots, SB), gr...  128 us
    pallas_call x1, Pallas kernels, line_gather(): pl.pallas_call(functools.partial(line_gather_kernel, parts), out_shape=ja...  82.4 us
    pallas_call x1, Pallas kernels, experts_forward(): pl.pallas_call(functools.partial(forward_kernel, experts, slots, SB), gri...  74.6 us
    unnamed x134, local copies, waits for them, and re-layouts  45.6 us
    pallas_call x1, Pallas kernels, line_scatter(): pl.pallas_call(functools.partial(line_scatter_kernel, parts), out_shape=j...  34.7 us
    dot_general x3, matrix products, matmul_nt(): lax.dot_general(left, right, (((1,), (1,)), ((), ())), preferred_element_...  34.3 us
  transfers between devices with their start and end apart: 5, of which 0 were waited for; matrix products, arithmetic and copies ran while one was open for 21% of the time, Pallas kernels for 64%

profile of v3, /device:TPU:18, one launch (start us, length us, event | category | flops | bytes accessed | tf_op | source)
XLA Modules:
  0.0 1353.6 jit_solution(14425303292776619635)
XLA Ops:
  11.0 3.4 concatenate.42
  14.4 166.4 %gather_all.2 = (bf16[2,2,2,4,2,32,5120]{6,5,4,3,2,1,0:T(8,128)(2,1)}, bf16[2,2,2,4,2,32,128]{6,5,4,3,2,1,0:T(8,128)(2,1)}, bf16[2,2,2,4,2,64,2048]{6,5,4,3,2,1,0:T(8,128)(2,1)}) custom-call(bf16[2,32,5120]{2,1,0:T(8,128)(2,1)} %bitcast.225, bf16[2,32,128]{2,1,0:T(8,128)(2,1)} %bitcast.238, bf16[2,64,2048]{2,1,0:T(8,128)(2,1)} %bitcast.237), custom_call_target="tpu_custom_call" | custom-call | tf_op jit(solution)/shard_map/gather_all/pallas_call | solution.py:144
  183.2 10.4 fusion.75
  202.6 82.4 %line_gather.1 = bf16[4,4,64,1024]{3,2,1,0:T(8,128)(2,1)S(1)} custom-call(bf16[4,64,1024]{2,1,0:T(8,128)(2,1)S(1)} %bitcast.201), custom_call_target="tpu_custom_call" | custom-call | tf_op jit(solution)/shard_map/line_gather/pallas_call | solution.py:331
  286.1 13.2 copy.160
  301.0 2.5 copy.161
  303.5 2.5 copy.137
  306.0 6.6 slice_bitcast_fusion
  312.7 5.6 copy.124
  318.4 2.8 multiply_reduce_fusion.3
  325.1 3.8 copy.127
  328.9 3.8 copy.128
  332.8 5.2 copy.180
  338.6 7.7 fusion.66
  346.3 33.6 %while.28 = (s32[]{:T(128)}, bf16[4,256,8,128]{1,3,2,0:T(8,128)(2,1)}, f32[4,256,8]{1,2,0:T(8,128)}, bf16[4,256,8,128]{3,1,2,0:T(8,128)(2,1)}, bf16[4,1024,128]{...) while((s32[]{:T(128)}, ...), condition=%wide.region_5.6_spmd.clone, body=%wide.region_3.5_spmd.clone.sunk | while | flops 1084487680 | bytes 36474508 | solution.py:719
  346.5 3.0 fusion.124
  349.5 3.3 fusion.125
  354.9 2.9 fusion.124
  357.9 3.3 fusion.125
  363.3 3.0 fusion.124
  366.4 3.3 fusion.125
  371.8 2.9 fusion.124
  374.7 3.3 fusion.125
  379.9 9.8 multiply_reduce_fusion.6
  394.6 157.3 %gather_all.3 = bf16[2,2,2,4,2,128,2176]{6,5,4,3,2,1,0:T(8,128)(2,1)} custom-call(bf16[2,128,2176]{2,1,0:T(8,128)(2,1)} %bitcast.221), custom_call_target="tpu_custom_call" | custom-call | tf_op jit(solution)/shard_map/gather_all/pallas_call | solution.py:144
  552.0 74.6 %experts_forward.1 = (bf16[8192,2048]{1,0:T(8,128)(2,1)}, bf16[4096,2048]{1,0:T(8,128)(2,1)}, f32[4096,768]{1,0:T(8,128)}, f32[4096,768]{1,0:T(8,128)}) custom-call(bf16[8192,2176]{1,0:T(8,128)(2,1)} %bitcast.204, bf16[1,2048,768]{2,1,0:T(8,128)(2,1)} %wg_hbm.3, bf16[1,2048,768]{2,1,0:T(8,128)(2,1)} %wu_hbm.3, bf16[1,768,2048]{2,1,0:T(8,128)(2,1)} %wd_hbm.3), custom_call_target="tpu_custom_call" | custom-call | flops 48000000000 | bytes 130000000 | tf_op jit(solution)/shard_map/experts_forward/pallas_call | solution.py:517
  626.7 127.5 %experts_backward.1 = (bf16[8192,2176]{1,0:T(8,128)(2,1)}, f32[1,2048,768]{2,1,0:T(8,128)}, f32[1,2048,768]{2,1,0:T(8,128)}, f32[1,768,2048]{2,1,0:T(8,128)}) custom-call(bf16[8192,2176]{1,0:T(8,128)(2,1)} %bitcast.205, bf16[8192,2048]{1,0:T(8,128)(2,1)} %all-gather.2.cloned.1.call-done.cot_ref, bf16[4096,2048]{1,0:T(8,128)(2,1)} %get-tuple-element.132.rows_ref, ...), custom_call_target="tpu_custom_call" | custom-call | flops 85000003584 | bytes 150000000 | tf_op jit(solution)/shard_map/experts_backward/pallas_call | solution.py:539
  754.3 246.0 %scatter_all.2 = f32[4,64,2176]{2,1,0:T(8,128)} custom-call(bf16[2,2,2,4,4,64,2176]{6,5,4,3,2,1,0:T(8,128)(2,1)} %bitcast.206), custom_call_target="tpu_custom_call" | custom-call | tf_op jit(solution)/shard_map/scatter_all/pallas_call | solution.py:275
  1002.9 3.6 multiply_reduce_fusion.4
  1007.2 10.5 convolution_convert_fusion.1
  1017.6 18.1 %convolution_convert_fusion.2 = bf16[256,4096]{1,0:T(8,128)(2,1)} fusion(bf16[4096,2048]{1,0:T(8,128)(2,1)} %bitcast.209, f32[256,2048]{1,0:T(8,128)S(1)} %subtract_add_fusion), kind=kOutput, calls=%fused_computation.56 | convolution fusion | flops 4296540160 | bytes 20971520 | tf_op jit(solution)/shard_map/dot_general | solution.py:570
  1038.6 55.7 %while.29 = (s32[]{:T(128)}, f32[4,256,8,128]{3,1,2,0:T(8,128)}, bf16[4,1024,128]{2,1,0:T(8,128)(2,1)}, bf16[4,1024,128]{2,1,0:T(8,128)(2,1)}, bf16[4,256,8,128]...) while((s32[]{:T(128)}, f32[4,256,8,128]{3,1,2,0:T(8,128)}, ...), condition=%wide.region_13.14_spmd.clone, body=%wide.region_11.13_spmd.clone.sunk | while | flops 2701391872 | bytes 85244104 | solution.py:773
  1042.0 3.0 multiply_reduce_fusion.11
  1055.9 3.0 multiply_reduce_fusion.11
  1069.8 3.0 multiply_reduce_fusion.11
  1080.4 2.4 fusion.134
  1083.8 3.0 multiply_reduce_fusion.11
  1099.9 34.7 %line_scatter.1 = f32[4,64,1024]{2,1,0:T(8,128)S(1)} custom-call(bf16[4,4,64,1024]{3,2,1,0:T(8,128)(2,1)S(1)} %pad_maximum_fusion.1.p_ref), custom_call_target="tpu_custom_call" | custom-call | tf_op jit(solution)/shard_map/line_scatter/pallas_call | solution.py:404
  1134.8 5.5 copy.147
  1143.7 2.7 bitcast_multiply_fusion
  1150.0 3.1 multiply_reduce_fusion.1
  1153.1 2.6 fusion.48
  1155.8 12.6 fusion.65
  1178.3 11.4 convolution_convert_fusion
  1189.7 139.5 %scatter_all.3 = (f32[4,16,5120]{2,1,0:T(8,128)}, f32[4,16,128]{2,1,0:T(8,128)}) custom-call(bf16[2,2,2,4,4,16,5120]{6,5,4,3,2,1,0:T(8,128)(2,1)} %bitcast.203, bf16[2,2,2,4,4,16,128]{6,5,4,3,2,1,0:T(8,128)(2,1)} %bitcast.231), custom_call_target="tpu_custom_call" | custom-call | tf_op jit(solution)/shard_map/scatter_all/pallas_call | solution.py:275
  1329.2 2.4 slice.130
  1337.4 3.8 fusion.62
  1341.2 2.5 add_convert_fusion
  (315 shorter events, 111.9 us)
Async XLA Ops:
  8.0 174.3 %copy-start.6 = (bf16[256,2048]{1,0:T(8,128)(2,1)S(1)}, bf16[256,2048]{1,0:T(8,128)(2,1)}, u32[]{:S(2)}) copy-start(bf16[256,2048]{1,0:T(8,128)(2,1)} %param.19) | copy-start | bytes 3145732
  8.0 618.7 %all-gather.2.cloned.1.call-start = ((), (), s32[]{:S(2)}) async-start(), calls=%async_computation.4 | async-start | bytes 34603008 | tf_op jit(solution)/shard_map/all_gather | solution.py:691
  180.8 953.8 %reduce-scatter.5.cloned.1.call-start = ((), (), s32[]{:S(2)}) async-start(), calls=%async_computation.5 | async-start | bytes 37748736 | tf_op jit(solution)/shard_map/reduce_scatter | solution.py:746
  182.2 15.4 %copy-start.36 = (bf16[32,8192]{1,0:T(8,128)(2,1)}, bf16[32,8192]{1,0:T(8,128)(2,1)S(1)}, u32[]{:S(2)}) copy-start(bf16[32,8192]{1,0:T(8,128)(2,1)S(1)} %reshape_reshape_reshape.6) | copy-start | bytes 1572868
  182.3 11.3 copy-start.43
  183.2 10.4 copy-start.51
  183.2 12.9 copy-start.64
  196.4 4.8 copy-start.11
  197.6 4.9 copy-start.23
  197.8 4.7 copy-start.58
  198.9 139.6 %copy-start.27 = (f32[256,128]{1,0:T(8,128)}, f32[256,128]{1,0:T(8,128)S(1)}, u32[]{:S(2)}) copy-start(f32[256,128]{1,0:T(8,128)S(1)} %copy.129) | copy-start | bytes 393220
  199.7 138.8 %copy-start.25 = (f32[256,128]{1,0:T(8,128)}, f32[256,128]{1,0:T(8,128)S(1)}, u32[]{:S(2)}) copy-start(f32[256,128]{1,0:T(8,128)S(1)} %copy.126) | copy-start | bytes 393220
  318.4 20.2 %copy-start.60 = (f32[128]{0:T(128)}, f32[128]{0:T(128)S(1)}, u32[]{:S(2)}) copy-start(f32[128]{0:T(128)S(1)} %reshape.281) | copy-start | bytes 1540
  318.4 3.5 copy-start
  332.8 5.3 slice-start
  338.0 52.4 %copy-start.47 = (f32[2048]{0:T(1024)}, f32[2048]{0:T(1024)S(1)}, u32[]{:S(2)}) copy-start(f32[2048]{0:T(1024)S(1)} %reshape.283) | copy-start | bytes 24580
  338.4 52.9 %copy-start.20 = (bf16[2048,32]{1,0:T(8,128)(2,1)}, bf16[2048,32]{1,0:T(8,128)(2,1)S(1)}, u32[]{:S(2)}) copy-start(bf16[2048,32]{1,0:T(8,128)(2,1)S(1)} %reshape_reshape.27) | copy-start | bytes 393220
  379.9 9.8 copy-start.13
  379.9 9.8 copy-start.49
  390.4 4.2 copy-start.56
  626.6 529.1 %reduce-scatter.9.cloned.1.call-start = ((), (), s32[]{:S(2)}) async-start(), calls=%async_computation.7 | async-start | bytes 18874368 | tf_op jit(solution)/shard_map/reduce_scatter | solution.py:766
  754.2 247.4 %copy-start.31 = (f32[256,32]{1,0:T(8,128)S(1)}, f32[256,32]{1,0:T(8,128)}, u32[]{:S(2)}) copy-start(f32[256,32]{1,0:T(8,128)} %copy-done.30) | copy-start | bytes 98308
  754.2 247.4 %copy-start.63 = (f32[256]{0:T(256)S(1)}, f32[256]{0:T(256)}, u32[]{:S(2)}) copy-start(f32[256]{0:T(256)} %copy-done.62) | copy-start | bytes 3076
  754.3 248.6 %copy-start.21 = (bf16[2048,32]{1,0:T(8,128)(2,1)S(1)}, bf16[2048,32]{1,0:T(8,128)(2,1)}, u32[]{:S(2)}) copy-start(bf16[2048,32]{1,0:T(8,128)(2,1)} %copy-done.20) | copy-start | bytes 393220
  754.3 248.6 %copy-start.48 = (f32[2048]{0:T(1024)S(1)}, f32[2048]{0:T(1024)}, u32[]{:S(2)}) copy-start(f32[2048]{0:T(1024)} %copy-done.47) | copy-start | bytes 24580
  754.3 248.6 %copy-start.57 = (f32[256]{0:T(256)S(1)}, f32[256]{0:T(256)}, u32[]{:S(2)}) copy-start(f32[256]{0:T(256)} %copy-done.56) | copy-start | bytes 3076
  1000.3 6.2 copy-start.3
  1000.3 6.2 copy-start.22
  1000.3 6.2 copy-start.66
  1002.9 3.6 copy-start.37
  1007.1 10.5 copy-start.8
  1035.7 305.5 %reduce-scatter.7.cloned.1.call-start = ((), (), s32[]{:S(2)}) async-start(), calls=%async_computation.6 | async-start | bytes 5242880 | tf_op jit(solution)/shard_map/reduce_scatter | solution.py:786
  1038.7 3.3 copy-start.17
  1052.6 3.3 copy-start.17
  1066.5 3.3 copy-start.17
  1080.4 3.3 copy-start.17
  1134.6 209.1 %reduce-scatter.11.cloned.1.call-start = ((), (), s32[]{:S(2)}) async-start(), calls=%async_computation.8 | async-start | bytes 2621440 | tf_op jit(solution)/shard_map/reduce_scatter | solution.py:767
  1134.8 5.8 copy-start.28
  1143.5 12.3 copy-start.32
  1143.6 12.1 copy-start.33
  1146.4 3.5 copy-start.5
  1146.4 3.5 copy-start.61
  1155.8 12.7 copy-start.10
  1155.8 12.6 copy-start.38
  1155.8 17.8 %copy-start.55 = (bf16[2048]{0:T(1024)(128)(2,1)S(1)}, bf16[2048]{0:T(1024)(128)(2,1)}, u32[]{:S(2)}) copy-start(bf16[2048]{0:T(1024)(128)(2,1)} %get-tuple-element.329) | copy-start | bytes 12292
  1168.8 9.5 copy-start.18
  1189.7 147.7 %copy-start.65 = (f32[256]{0:T(256)S(1)}, f32[256]{0:T(256)}, u32[]{:S(2)}) copy-start(f32[256]{0:T(256)} %get-tuple-element.407) | copy-start | bytes 3076
  1329.1 12.1 copy-start.4
  (40 other events, 75.3 us)
Sparse Core Ops, SparseCore 0:
  181.0 217.4 all-gather.1
Sparse Core Ops, SparseCore 1:
  626.7 260.9 reduce-scatter.4
  1035.8 115.1 reduce-scatter.8
  1153.1 89.7 reduce-scatter.6
  1245.2 70.1 reduce-scatter.10

commit v4 on v3

--- a/solution.py
+++ b/solution.py
@@ -30,24 +30,28 @@
     def _(): sig(dev(y, x, c, s + 1))
     pl.semaphore_wait(bar, 3 + jnp.where(s > 0, 1, 0) + jnp.where(s < NZ - 1, 1, 0))
 
-def ag_kernel(n_arr, *refs):
-    ins = refs[:n_arr]; outs = refs[n_arr:2 * n_arr]
-    loc_sem, zs, zr, ps, pr, cs, cr = refs[2 * n_arr:]
+def ag_kernel(n_arr, n_line, *refs):
+    n_all = n_arr + n_line
+    ins = refs[:n_all]; outs = refs[n_all:2 * n_all]
+    loc_sem, zs, zr, ps, pr, cs, cr = refs[2 * n_all:]
     y, x, c, s = place()
     barrier_all(y, x, c, s)
     def rc(src, dst, ss, rs, d):
         return pltpu.make_async_remote_copy(src_ref=src, dst_ref=dst, send_sem=ss, recv_sem=rs, device_id=d, device_id_type=MESH)
     X = dev(y, 1 - x, c, s); Y = dev(1 - y, x, c, s); C = dev(y, x, 1 - c, s)
     A = range(n_arr)
+    every = range(n_all)
+    def home(a, zz):
+        return outs[a].at[y, x, c, zz] if a < n_arr else outs[a].at[zz]
     steps = [(0, 0)] + [(d, g) for d in range(1, NZ) for g in (1, -1)]
     def valid(d, g):
         return (s >= d) if g == 1 else (s + d <= NZ - 1)
     def zof(d, g): return s - d * g
     def src_own(a, h, zz, k):
-        return ins[a].at[h] if k == 0 else outs[a].at[y, x, c, zz, h]
+        return ins[a].at[h] if k == 0 else home(a, zz).at[h]
     def zcopy(a, h, zz, k, g):
         kk = 1 + 2 * (k_dist(k)) + (0 if g == 1 else 1)
-        return rc(src_own(a, h, zz, k), outs[a].at[y, x, c, zz, h], zs.at[a, h, kk], zr.at[a, h, kk], dev(y, x, c, s + g))
+        return rc(src_own(a, h, zz, k), home(a, zz).at[h], zs.at[a, h, kk], zr.at[a, h, kk], dev(y, x, c, s + g))
     def k_dist(k): return steps[k][0]
     def plane(a, h, zz, k, which):
         return rc(src_own(a, h, zz, k), outs[a].at[y, x, c, zz, h], ps.at[a, k, h, which], pr.at[a, k, h, which], X if which == 0 else Y)
@@ -67,7 +71,7 @@
         d = outs[a].at[:, :, 1 - c, zz]
         return rc(d, d, cs.at[a, k], cr.at[a, k], C)
     def loc(a):
-        return pltpu.make_async_copy(ins[a], outs[a].at[y, x, c, s], loc_sem.at[a])
+        return pltpu.make_async_copy(ins[a], home(a, s), loc_sem.at[a])
 
     def when(k, f):
         d, g = steps[k]
@@ -78,19 +82,20 @@
         d, g = steps[k]
         def go():
             zz = zof(d, g)
-            for a in A:
+            for a in every:
                 for h in range(2):
                     if k:
                         kk = k
-                        dref = outs[a].at[y, x, c, zz, h]
+                        dref = home(a, zz).at[h]
                         rc(dref, dref, zs.at[a, h, kk], zr.at[a, h, kk], X).wait_recv()
                     for gg in ((1, -1) if k == 0 else (g,)):
                         okc = (s < NZ - 1) if gg == 1 else (s > 0)
                         if d + 1 < NZ:
                             @pl.when(okc)
                             def _(): zcopy(a, h, zz, k, gg).start()
-                    plane(a, h, zz, k, 0).start()
-                    plane(a, h, zz, k, 1).start()
+                    if a < n_arr:
+                        plane(a, h, zz, k, 0).start()
+                        plane(a, h, zz, k, 1).start()
         when(k, go)
     def stage_b(k):
         d, g = steps[k]
@@ -114,7 +119,7 @@
                 diag_recv(a, 1, zz, k).wait_recv()
                 core(a, zz, k, 0).start()
         when(k, go)
-    for a in A: loc(a).start()
+    for a in every: loc(a).start()
     n = len(steps)
     for i in range(n + 2):
         if i < n: stage_a(i)
@@ -124,36 +129,39 @@
         d, g = steps[k]
         def go():
             zz = zof(d, g)
-            for a in A:
-                core_recv(a, zz, k).wait_recv()
-                core(a, zz, k, 0).wait_send()
+            for a in every:
+                if a < n_arr:
+                    core_recv(a, zz, k).wait_recv()
+                    core(a, zz, k, 0).wait_send()
+                elif k == 0: loc(a).wait()
                 for h in range(2):
                     for gg in ((1, -1) if k == 0 else (g,)):
                         okc = (s < NZ - 1) if gg == 1 else (s > 0)
                         if d + 1 < NZ:
                             @pl.when(okc)
                             def _(): zcopy(a, h, zz, k, gg).wait_send()
-                    plane(a, h, zz, k, 0).wait_send()
-                    plane(a, h, zz, k, 1).wait_send()
-                    diag(a, h, zz, k).wait_send()
+                    if a < n_arr:
+                        plane(a, h, zz, k, 0).wait_send()
+                        plane(a, h, zz, k, 1).wait_send()
+                        diag(a, h, zz, k).wait_send()
         when(k, go)
 
-def ag32(arrs, cid):
-    ins = [a.reshape(2, a.shape[0] // 2, a.shape[1]) for a in arrs]
-    n = len(ins); nk = 7
+def ag32(arrs, cid, line=()):
+    ins = [a.reshape(2, a.shape[0] // 2, a.shape[1]) for a in list(arrs) + list(line)]
+    n, m = len(arrs), len(line); nk = 7
     outs = pl.pallas_call(
-        functools.partial(ag_kernel, n),
-        out_shape=[jax.ShapeDtypeStruct((2, 2, 2, NZ) + a.shape, a.dtype) for a in ins],
-        in_specs=[pl.BlockSpec(memory_space=pltpu.VMEM)] * n,
-        out_specs=[pl.BlockSpec(memory_space=pl.ANY)] * n,
-        scratch_shapes=[pltpu.SemaphoreType.DMA((n,)),
-            pltpu.SemaphoreType.DMA((n, 2, 9)), pltpu.SemaphoreType.DMA((n, 2, 9)),
+        functools.partial(ag_kernel, n, m),
+        out_shape=[jax.ShapeDtypeStruct(((2, 2, 2, NZ) if i < n else (NZ,)) + a.shape, a.dtype) for i, a in enumerate(ins)],
+        in_specs=[pl.BlockSpec(memory_space=pltpu.VMEM)] * (n + m),
+        out_specs=[pl.BlockSpec(memory_space=pl.ANY)] * (n + m),
+        scratch_shapes=[pltpu.SemaphoreType.DMA((n + m,)),
+            pltpu.SemaphoreType.DMA((n + m, 2, 9)), pltpu.SemaphoreType.DMA((n + m, 2, 9)),
             pltpu.SemaphoreType.DMA((n, nk, 2, 3)), pltpu.SemaphoreType.DMA((n, nk, 2, 3)),
             pltpu.SemaphoreType.DMA((n, nk)), pltpu.SemaphoreType.DMA((n, nk))],
         compiler_params=pltpu.CompilerParams(collective_id=cid, has_side_effects=True, vmem_limit_bytes=64000 * 1024),
         name="gather_all",
     )(*ins)
-    return [o.reshape(32, a.shape[0], a.shape[1]) for o, a in zip(outs, arrs)]
+    return [o.reshape(-1, a.shape[1] * 2, a.shape[2]) for o, a in zip(outs, ins)]
 
 ZORDER = (0, 3, 1, 2)
 LAGS = (1, 1, 1, 1)
@@ -548,6 +556,108 @@
         name="experts_backward",
     )(meta_in, cot_all, rows, ga, ua, w_gate, w_up, w_down)
 
+
+def rope_tables(seq_len):
+    half = HD // 2
+    frequency = theta_base ** (-2.0 * jnp.arange(half, dtype=jnp.float32) / HD)
+    angles = jnp.arange(seq_len, dtype=jnp.float32)[:, None] * frequency[None, :]
+    return jnp.concatenate([jnp.cos(angles)] * 2, axis=-1), jnp.concatenate([-jnp.sin(angles), jnp.sin(angles)], axis=-1)
+
+def turn(u, cos, sin):
+    return u * cos + pltpu.roll(u, HD // 2, 1) * sin
+
+def scale_of(u):
+    return lax.rsqrt(jnp.mean(u * u, axis=-1, keepdims=True) + epsilon)
+
+def attention_forward_kernel(group, q_ref, k_ref, v_ref, gq_ref, gk_ref, cos_ref, sin_ref, ql_ref, kl_ref, vl_ref, mix_ref):
+    bf, f32 = jnp.bfloat16, jnp.float32
+    rows, seq = q_ref.shape[0], k_ref.shape[0]
+    first = lax.axis_index("shard") * rows
+    k = k_ref[...]
+    kl_ref[...] = turn(k * scale_of(k) * gk_ref[...], cos_ref[...], sin_ref[...]).astype(bf)
+    vl_ref[...] = v_ref[...].astype(bf)
+    cos, sin = cos_ref[pl.ds(first, rows), :], sin_ref[pl.ds(first, rows), :]
+    allowed = lax.broadcasted_iota(jnp.int32, (rows, seq), 1) <= first + lax.broadcasted_iota(jnp.int32, (rows, seq), 0)
+    for j in range(group):
+        cols = slice(j * HD, (j + 1) * HD)
+        u = q_ref[:, cols]
+        ql = (turn(u * scale_of(u) * gq_ref[...], cos, sin) * HD ** (-0.5)).astype(bf)
+        ql_ref[:, cols] = ql
+        scores = dot(ql, kl_ref[...], 1, 1)
+        raised = jnp.where(allowed, jnp.exp(scores), 0.0)
+        probs = (raised * (1.0 / jnp.sum(raised, axis=-1, keepdims=True))).astype(bf)
+        mix_ref[:, cols] = dot(probs, vl_ref[...], 1, 0).astype(bf)
+
+def attention_forward(q_proj, kv_proj, gq, gk, cos, sin):
+    rows, seq = q_proj.shape[0], kv_proj.shape[0]
+    group = HQ // HK
+    bf = jnp.bfloat16
+    whole = lambda a: pl.BlockSpec(a.shape, lambda i: (0, 0))
+    gq, gk = gq[None, :], gk[None, :]
+    return pl.pallas_call(
+        functools.partial(attention_forward_kernel, group),
+        grid=(HK,),
+        out_shape=[jax.ShapeDtypeStruct(q_proj.shape, bf), jax.ShapeDtypeStruct((seq, HK * HD), bf), jax.ShapeDtypeStruct((seq, HK * HD), bf), jax.ShapeDtypeStruct(q_proj.shape, bf)],
+        in_specs=[pl.BlockSpec((rows, group * HD), lambda i: (0, i)), pl.BlockSpec((seq, HD), lambda i: (0, i)), pl.BlockSpec((seq, HD), lambda i: (0, HK + i)), whole(gq), whole(gk), whole(cos), whole(sin)],
+        out_specs=[pl.BlockSpec((rows, group * HD), lambda i: (0, i)), pl.BlockSpec((seq, HD), lambda i: (0, i)), pl.BlockSpec((seq, HD), lambda i: (0, i)), pl.BlockSpec((rows, group * HD), lambda i: (0, i))],
+        compiler_params=pltpu.CompilerParams(dimension_semantics=("arbitrary",), vmem_limit_bytes=48 << 20),
+        cost_estimate=pl.CostEstimate(flops=4_300_000_000, bytes_accessed=20_000_000, transcendentals=8_400_000),
+        name="attention_forward",
+    )(q_proj, kv_proj, kv_proj, gq, gk, cos, sin)
+
+def attention_backward_kernel(group, u_ref, ql_ref, kl_ref, vl_ref, gm_ref, gq_ref, cos_ref, sin_ref, gu_ref, gk_ref, gv_ref, gg_ref, gk_acc, gv_acc):
+    bf, f32 = jnp.bfloat16, jnp.float32
+    rows, seq = ql_ref.shape[0], kl_ref.shape[0]
+    first = lax.axis_index("shard") * rows
+    cos, sin = cos_ref[pl.ds(first, rows), :], sin_ref[pl.ds(first, rows), :]
+    allowed = lax.broadcasted_iota(jnp.int32, (rows, seq), 1) <= first + lax.broadcasted_iota(jnp.int32, (rows, seq), 0)
+    gain_grad = jnp.zeros((1, HD), f32)
+    for j in range(group):
+        cols = slice(j * HD, (j + 1) * HD)
+        ql, gm = ql_ref[:, cols], gm_ref[:, cols]
+        raised = jnp.where(allowed, jnp.exp(dot(ql, kl_ref[...], 1, 1)), 0.0)
+        probs = raised * (1.0 / jnp.sum(raised, axis=-1, keepdims=True))
+        gp = dot(gm, vl_ref[...], 1, 1)
+        gs = (probs * (gp - jnp.sum(probs * gp, axis=-1, keepdims=True))).astype(bf)
+        gv = dot(probs.astype(bf), gm, 0, 0)
+        gk = dot(gs, ql, 0, 0)
+        if j == 0:
+            gv_acc[...] = gv
+            gk_acc[...] = gk
+        else:
+            gv_acc[...] += gv
+            gk_acc[...] += gk
+        m = dot(gs, kl_ref[...], 1, 0) * HD ** (-0.5)
+        m = m * cos + pltpu.roll(m * sin, HD // 2, 1)
+        u = u_ref[:, cols]
+        r = scale_of(u)
+        gain_grad = gain_grad + jnp.sum(m * u * r, axis=0, keepdims=True)
+        mg = m * gq_ref[...]
+        gu_ref[:, cols] = (r * mg - u * (r * r * r) * jnp.mean(mg * u, axis=-1, keepdims=True)).astype(bf)
+    gk_ref[...] = gk_acc[...].astype(bf)
+    gv_ref[...] = gv_acc[...].astype(bf)
+    gg_ref[0] = jnp.broadcast_to(gain_grad, (8, HD))
+
+def attention_backward(q_proj, q_low, k_low, v_low, grad_mix, gq, cos, sin):
+    rows, seq = q_low.shape[0], k_low.shape[0]
+    group = HQ // HK
+    bf, f32 = jnp.bfloat16, jnp.float32
+    gq = gq[None, :]
+    whole = lambda a: pl.BlockSpec(a.shape, lambda i: (0, 0))
+    qb = pl.BlockSpec((rows, group * HD), lambda i: (0, i)); kb = pl.BlockSpec((seq, HD), lambda i: (0, i))
+    grad_q, grad_k, grad_v, gain = pl.pallas_call(
+        functools.partial(attention_backward_kernel, group),
+        grid=(HK,),
+        out_shape=[jax.ShapeDtypeStruct(q_low.shape, bf), jax.ShapeDtypeStruct(k_low.shape, bf), jax.ShapeDtypeStruct(k_low.shape, bf), jax.ShapeDtypeStruct((HK, 8, HD), f32)],
+        in_specs=[qb, qb, kb, kb, qb, whole(gq), whole(cos), whole(sin)],
+        out_specs=[qb, kb, kb, pl.BlockSpec((1, 8, HD), lambda i: (i, 0, 0))],
+        scratch_shapes=[pltpu.VMEM((seq, HD), f32), pltpu.VMEM((seq, HD), f32)],
+        compiler_params=pltpu.CompilerParams(dimension_semantics=("arbitrary",), vmem_limit_bytes=48 << 20),
+        cost_estimate=pl.CostEstimate(flops=10_700_000_000, bytes_accessed=20_000_000, transcendentals=8_400_000),
+        name="attention_backward",
+    )(q_proj, q_low, k_low, v_low, grad_mix, gq, cos, sin)
+    return grad_q, jnp.concatenate([grad_k, grad_v], axis=1), jnp.sum(gain[:, 0], axis=0)
+
 HQ = 32
 HK = 4
 HD = 128
@@ -602,41 +712,12 @@
     return rotary(norm_rows(shaped, gain_vec), positions) * factor
 
 
-def head_forward(query_block, key_block, value_block, allowed):
-    scores = jnp.einsum("rgd,sd->rgs", query_block, key_block, preferred_element_type=jnp.float32)
-    raised = jnp.where(allowed[:, None, :], jnp.exp(scores), 0.0)
-    totals = jnp.sum(raised, axis=-1)
-    probs_low = (raised / totals[..., None]).astype(jnp.bfloat16)
-    return (
-        jnp.einsum("rgs,sd->rgd", probs_low, value_block, preferred_element_type=jnp.float32),
-        totals,
-    )
-
-
-def head_backward(query_block, key_block, value_block, totals, upstream, allowed):
-    scores = jnp.einsum("rgd,sd->rgs", query_block, key_block, preferred_element_type=jnp.float32)
-    raised = jnp.where(allowed[:, None, :], jnp.exp(scores), 0.0)
-    probs_f = raised / totals[..., None]
-    probs_low = probs_f.astype(jnp.bfloat16)
-    grad_probs = jnp.einsum(
-        "rgd,sd->rgs", upstream, value_block, preferred_element_type=jnp.float32
-    )
-    inner_sum = jnp.sum(probs_f * grad_probs, axis=-1, keepdims=True)
-    grad_scores = (probs_f * (grad_probs - inner_sum)).astype(jnp.bfloat16)
-    grad_query = jnp.einsum(
-        "rgs,sd->rgd", grad_scores, key_block, preferred_element_type=jnp.float32
-    )
-    grad_key = jnp.einsum(
-        "rgs,rgd->sd", grad_scores, query_block, preferred_element_type=jnp.float32
-    )
-    grad_value = jnp.einsum("rgs,rgd->sd", probs_low, upstream, preferred_element_type=jnp.float32)
-    return (grad_query, grad_key, grad_value)
-
-
-def gather_all(arrays, cid):
+def gather_all(arrays, cid, line=()):
     if placed():
-        return [o.reshape(-1, o.shape[-1]) for o in ag32(arrays, cid)]
-    return [lax.all_gather(a, BOTH, axis=0, tiled=True) for a in arrays]
+        return [o.reshape(-1, o.shape[-1]) for o in ag32(arrays, cid, line)]
+    return [lax.all_gather(a, BOTH, axis=0, tiled=True) for a in arrays] + [
+        lax.all_gather(a, "shard", axis=0, tiled=True) for a in line
+    ]
 
 
 def scatter_all(arrays, cid, out_dtype=jnp.float32):
@@ -671,8 +752,6 @@
     shard_count = lax.axis_size("shard")
     shard_pos = lax.axis_index("shard")
     seq_len = tok_rows * shard_count
-    group_size = HQ // HK
-    factor = HD ** (-0.5)
     q_cols, kv_cols = HQ * HD, HK * HD
 
     pieces = [w_router.reshape(-1), g_attn, g_ffn, g_query, g_key]
@@ -681,7 +760,7 @@
     small_rows = -(-used // (64 * 128)) * 64
     small = jnp.concatenate(pieces + [jnp.zeros((small_rows * 128 - used,), bf)]).reshape(small_rows, 128)
     wqkv = jnp.concatenate([w_query, w_key, w_value], axis=1)
-    wqkv_full, small_all, wo_full = gather_all([wqkv, small, w_out], 1)
+    wqkv_full, small_all, wo_full, hidden_seq = gather_all([wqkv, small, w_out], 1, [hidden_in])
     small_all = small_all.reshape(devices, small_rows * 128)
     starts = [sum(sizes[:i]) for i in range(5)]
     wr_full, attn_gain, ffn_gain, query_gain, key_gain = [small_all[:, o : o + n].reshape(-1) for o, n in zip(starts, sizes)]
@@ -690,34 +769,13 @@
     cotangent, wo_full = lax.optimization_barrier((cotangent, wo_full))
     cot_all = lax.all_gather(cotangent, BOTH, axis=0, tiled=True)
 
-    positions = shard_pos * tok_rows + jnp.arange(tok_rows, dtype=jnp.int32)
     inputs_f = hidden_in.astype(f32)
     normed_low = norm_rows(inputs_f, attn_gain).astype(bf)
-    qkv = matmul(normed_low, wqkv_full)
-    q_proj, k_proj, v_proj = qkv[:, :q_cols], qkv[:, q_cols : q_cols + kv_cols], qkv[:, q_cols + kv_cols :]
-    k_rot, k_pull = jax.vjp(
-        lambda projected, gain_vec: head_prep(projected, gain_vec, positions, HK, 1.0),
-        k_proj,
-        key_gain,
-    )
-    q_rot, q_pull = jax.vjp(
-        lambda projected, gain_vec: head_prep(projected, gain_vec, positions, HQ, factor),
-        q_proj,
-        query_gain,
-    )
-    q_low = q_rot.astype(bf)
-    kv_low = jnp.concatenate([k_rot.reshape(tok_rows, kv_cols).astype(bf), v_proj.astype(bf)], axis=1)
-    allowed = jnp.arange(seq_len, dtype=jnp.int32)[None, :] <= positions[:, None]
-    kv_all = line_gather(kv_low, 2)
-    q_heads = q_low.reshape(tok_rows, HK, group_size, HD).transpose(1, 0, 2, 3)
-    k_heads = kv_all[:, :kv_cols].reshape(seq_len, HK, HD).transpose(1, 0, 2)
-    v_heads = kv_all[:, kv_cols:].reshape(seq_len, HK, HD).transpose(1, 0, 2)
-
-    def attend(pieces):
-        return head_forward(pieces[0], pieces[1], pieces[2], allowed)
-
-    head_outs, totals = lax.map(attend, (q_heads, k_heads, v_heads))
-    mix_low = head_outs.transpose(1, 0, 2, 3).reshape(tok_rows, q_cols).astype(bf)
+    normed_seq = norm_rows(hidden_seq.astype(f32), attn_gain).astype(bf)
+    kv_proj = matmul(normed_seq, wqkv_full[:, q_cols:])
+    q_proj = matmul(normed_low, wqkv_full[:, :q_cols])
+    cosine, sine = rope_tables(seq_len)
+    q_low, k_low, v_low, mix_low = attention_forward(q_proj, kv_proj, query_gain, key_gain, cosine, sine)
     residual = inputs_f + matmul(mix_low, wo_full)
     ffn_low = norm_rows(residual, ffn_gain).astype(bf)
 
@@ -765,30 +823,23 @@
     grad_mix, grad_wout = lax.optimization_barrier((grad_mix, grad_wout))
     out_grad = lax.psum_scatter(grad_wout, "expert", scatter_dimension=0, tiled=True)
     out_grad = lax.psum_scatter(out_grad, "shard", scatter_dimension=0, tiled=True).astype(f32)
-    grad_heads = grad_mix.reshape(tok_rows, HK, group_size, HD).transpose(1, 0, 2, 3)
-
-    def attend_back(pieces):
-        return head_backward(pieces[0], pieces[1], pieces[2], pieces[3], pieces[4], allowed)
-
-    grad_qheads, grad_kheads, grad_vheads = lax.map(
-        attend_back, (q_heads, k_heads, v_heads, totals, grad_heads)
-    )
-    grad_q_rot = grad_qheads.transpose(1, 0, 2, 3).reshape(tok_rows, HQ, HD)
-    grad_kv = jnp.concatenate(
-        [
-            grad_kheads.transpose(1, 0, 2).reshape(seq_len, kv_cols).astype(bf),
-            grad_vheads.transpose(1, 0, 2).reshape(seq_len, kv_cols).astype(bf),
-        ],
-        axis=1,
+
+    grad_q_low, grad_kv, grad_query_gain = attention_backward(
+        q_proj, q_low, k_low, v_low, grad_mix, query_gain, cosine, sine
     )
     grad_kv = line_scatter(grad_kv, 6)
     grad_kv, moe_out = lax.optimization_barrier((grad_kv, moe_out))
     moe_out = lax.psum_scatter(moe_out, "shard", scatter_dimension=0, tiled=True).astype(f32)
     block_out = (residual + moe_out).astype(bf)
-    grad_q_proj, grad_query_gain = q_pull(grad_q_rot)
+    own_rows = shard_pos * tok_rows
+    k_proj = lax.dynamic_slice(kv_proj, (own_rows, 0), (tok_rows, kv_cols))
+    positions = own_rows + jnp.arange(tok_rows, dtype=jnp.int32)
+    _, k_pull = jax.vjp(
+        lambda projected, gain_vec: head_prep(projected, gain_vec, positions, HK, 1.0), k_proj, key_gain
+    )
     grad_k_proj, grad_key_gain = k_pull(grad_kv[:, :kv_cols].reshape(tok_rows, HK, HD))
     grad_qkv_low = jnp.concatenate(
-        [grad_q_proj.astype(bf), grad_k_proj.astype(bf), grad_kv[:, kv_cols:].astype(bf)], axis=1
+        [grad_q_low, grad_k_proj.astype(bf), grad_kv[:, kv_cols:].astype(bf)], axis=1
     )
     grad_wqkv = matmul_tn(normed_low, grad_qkv_low).astype(bf)
     grad_normed = matmul_nt(grad_qkv_low, wqkv_full)

time: 1360 us -> 1300 us (0.956)
  local copies, waits for them, and re-layouts: 111 us -> 29.2 us
  Pallas kernels: 1030 us -> 1100 us
  matrix products: 146 us -> 87.5 us
  waiting for transfers between devices: 0.14 us -> 37.6 us
  other arithmetic: 50.1 us -> 23.7 us
    dot_general x28 -> x0, matrix products: 69.2 us -> none  [the longest x4 13.1 us: head_forward(): jnp.einsum('rgs,sd->rgd', probs_low, value_block, preferred_element_type=...]
    pallas_call x3 -> x4, Pallas kernels: 406 us -> 454 us  [the longest x2 389 us: ag32(): pl.pallas_call(functools.partial(ag_kernel, n, m), out_shape=[jax.ShapeDt...]
    unnamed x134 -> x89, local copies, waits for them, and re-layouts: 45.6 us -> 6.14 us
    reduce_scatter x1, waiting for transfers between devices: 0.01 us -> 37.5 us  [per_device(): lax.psum_scatter(grad_wout, 'expert', scatter_dimension=0, tiled=True)]
    pallas_call x2, Pallas kernels: 385 us -> 415 us  [rs32(): pl.pallas_call(functools.partial(rs_kernel, n, parts), out_shape=[jax.Sha...]
    dot_general x3 -> x4, matrix products: 20.7 us -> 31.8 us  [matmul(): return jnp.dot(left, right, preferred_element_type=jnp.float32)]
  transfers between devices with their start and end apart: 5 -> 5, of which waited for: 0 -> 1; matrix products, arithmetic and copies ran while one was open for 21% -> 10% of each run, Pallas kernels for 64% -> 72%
where the time goes in v4:
time: 1300 us
  Pallas kernels  1100 us (85%)
  matrix products  87.5 us (7%)
  waiting for transfers between devices  37.6 us (3%)
  local copies, waits for them, and re-layouts  29.2 us (2%)
  other arithmetic  23.7 us (2%)
  between operations  16.7 us (1%)
    pallas_call x2, Pallas kernels, rs32(): pl.pallas_call(functools.partial(rs_kernel, n, parts), out_shape=[jax.Sha...  415 us
    pallas_call x2, Pallas kernels, ag32(): pl.pallas_call(functools.partial(ag_kernel, n, m), out_shape=[jax.ShapeDt...  389 us
    pallas_call x1, Pallas kernels, experts_backward(): pl.pallas_call(functools.partial(backward_kernel, experts, slots, SB), gr...  127 us
    pallas_call x1, Pallas kernels, experts_forward(): pl.pallas_call(functools.partial(forward_kernel, experts, slots, SB), gri...  75 us
    pallas_call x1, Pallas kernels, attention_backward(): pl.pallas_call(functools.partial(attention_backward_kernel, group), grid=...  38.6 us
    reduce_scatter x1, waiting for transfers between devices, per_device(): lax.psum_scatter(grad_wout, 'expert', scatter_dimension=0, tiled=True)  37.5 us
    pallas_call x1, Pallas kernels, line_scatter(): pl.pallas_call(functools.partial(line_scatter_kernel, parts), out_shape=j...  33.7 us
    dot_general x3, matrix products, matmul_nt(): lax.dot_general(left, right, (((1,), (1,)), ((), ())), preferred_element_...  33.3 us
  transfers between devices with their start and end apart: 5, of which 1 were waited for; matrix products, arithmetic and copies ran while one was open for 10% of the time, Pallas kernels for 72%

profile of v4, /device:TPU:18, one launch (start us, length us, event | category | flops | bytes accessed | tf_op | source)
XLA Modules:
  0.0 1299.6 jit_solution(3156049645502065980)
XLA Ops:
  8.1 0.8 copy.55
  8.9 2.0 pad_maximum_fusion.4
  11.0 3.4 concatenate.31
  14.3 167.2 %gather_all.2 = (bf16[2,2,2,4,2,32,5120]{6,5,4,3,2,1,0:T(8,128)(2,1)}, bf16[2,2,2,4,2,32,128]{6,5,4,3,2,1,0:T(8,128)(2,1)}, bf16[2,2,2,4,2,64,2048]{6,5,4,3,2,1,0:T(8,128)(2,1)}, bf16[4,2,128,2048]{3,2,1,0:T(8,128)(2,1)}) custom-call(bf16[2,32,5120]{2,1,0:T(8,128)(2,1)} %bitcast.60, bf16[2,32,128]{2,1,0:T(8,128)(2,1)} %bitcast.67, ...), custom_call_target="tpu_custom_call" | custom-call | tf_op jit(solution)/shard_map/gather_all/pallas_call | solution.py:152
  182.0 1.3 reshape_reshape_reshape.6
  184.5 3.3 multiply_reduce_fusion
  188.1 1.0 fusion.3
  189.2 8.4 fusion.4
  197.5 5.6 copy.56.k_ref.v_ref
  203.1 2.0 fusion.26
  205.8 0.5 multiply_multiply_fusion.1
  206.3 12.4 fusion.q_ref.u_ref
  218.8 26.4 %attention_forward.1 = (bf16[256,4096]{1,0:T(8,128)(2,1)S(1)}, bf16[1024,512]{1,0:T(8,128)(2,1)S(1)}, bf16[1024,512]{1,0:T(8,128)(2,1)S(1)}, bf16[256,4096]{1,0:T(8,128)(2,1)}) custom-call(f32[256,4096]{1,0:T(8,128)} %fusion.q_ref.u_ref, f32[1024,1024]{1,0:T(8,128)} %copy.56.k_ref.v_ref, f32[1024,1024]{1,0:T(8,128)} %copy.56.k_ref.v_ref, ...), custom_call_target="tpu_custom_call" | custom-call | flops 4300000256 | bytes 20000000 | tf_op jit(solution)/shard_map/attention_forward/pallas_call | solution.py:597
  245.2 10.4 multiply_reduce_fusion.3
  255.7 0.6 multiply_multiply_fusion.2
  256.5 0.5 fusion.36
  257.1 0.6 copy-done.24
  257.8 2.0 concatenate.34
  259.8 222.0 %gather_all.3 = bf16[2,2,2,4,2,128,2176]{6,5,4,3,2,1,0:T(8,128)(2,1)} custom-call(bf16[2,128,2176]{2,1,0:T(8,128)(2,1)} %bitcast.59), custom_call_target="tpu_custom_call" | custom-call | tf_op jit(solution)/shard_map/gather_all/pallas_call | solution.py:152
  481.8 75.0 %experts_forward.1 = (bf16[8192,2048]{1,0:T(8,128)(2,1)}, bf16[4096,2048]{1,0:T(8,128)(2,1)}, f32[4096,768]{1,0:T(8,128)}, f32[4096,768]{1,0:T(8,128)}) custom-call(bf16[8192,2176]{1,0:T(8,128)(2,1)} %bitcast.50, bf16[1,2048,768]{2,1,0:T(8,128)(2,1)} %wg_hbm.3, bf16[1,2048,768]{2,1,0:T(8,128)(2,1)} %wu_hbm.3, bf16[1,768,2048]{2,1,0:T(8,128)(2,1)} %wd_hbm.3), custom_call_target="tpu_custom_call" | custom-call | flops 48000000000 | bytes 130000000 | tf_op jit(solution)/shard_map/experts_forward/pallas_call | solution.py:525
  556.9 127.0 %experts_backward.1 = (bf16[8192,2176]{1,0:T(8,128)(2,1)}, f32[1,2048,768]{2,1,0:T(8,128)}, f32[1,2048,768]{2,1,0:T(8,128)}, f32[1,768,2048]{2,1,0:T(8,128)}) custom-call(bf16[8192,2176]{1,0:T(8,128)(2,1)} %bitcast.51, bf16[8192,2048]{1,0:T(8,128)(2,1)} %all-gather.2.cloned.1.call-done.cot_ref, bf16[4096,2048]{1,0:T(8,128)(2,1)} %get-tuple-element.52.rows_ref, ...), custom_call_target="tpu_custom_call" | custom-call | flops 85000003584 | bytes 150000000 | tf_op jit(solution)/shard_map/experts_backward/pallas_call | solution.py:547
  684.0 272.1 %scatter_all.2 = f32[4,64,2176]{2,1,0:T(8,128)} custom-call(bf16[2,2,2,4,4,64,2176]{6,5,4,3,2,1,0:T(8,128)(2,1)} %bitcast.52), custom_call_target="tpu_custom_call" | custom-call | tf_op jit(solution)/shard_map/scatter_all/pallas_call | solution.py:283
  956.1 1.2 fusion.28
  957.3 1.1 subtract_convert_fusion
  958.5 3.1 multiply_reduce_fusion.1
  961.7 0.6 subtract_add_fusion
  962.3 10.5 convolution_convert_fusion.1
  972.8 18.0 %convolution_convert_fusion.2.gm_ref = bf16[256,4096]{1,0:T(8,128)(2,1)} fusion(bf16[4096,2048]{1,0:T(8,128)(2,1)} %bitcast.75, f32[256,2048]{1,0:T(8,128)S(1)} %subtract_add_fusion), kind=kOutput, calls=%fused_computation.8 | convolution fusion | flops 4296540160 | bytes 20971520 | tf_op jit(solution)/shard_map/dot_general | solution.py:680
  991.0 0.9 copy-done.1
  992.7 38.6 %attention_backward.1 = (bf16[256,4096]{1,0:T(8,128)(2,1)}, bf16[1024,512]{1,0:T(8,128)(2,1)S(1)}, bf16[1024,512]{1,0:T(8,128)(2,1)S(1)}, f32[4,8,128]{2,1,0:T(8,128)S(1)}) custom-call(f32[256,4096]{1,0:T(8,128)} %fusion.q_ref.u_ref, bf16[256,4096]{1,0:T(8,128)(2,1)} %copy-done.6, bf16[1024,512]{1,0:T(8,128)(2,1)S(1)} %copy-done.8, ...), custom_call_target="tpu_custom_call" | custom-call | flops 10700000256 | bytes 20000000 | tf_op jit(solution)/shard_map/attention_backward/pallas_call | solution.py:648
  1031.6 33.7 %line_scatter.1 = f32[4,64,1024]{2,1,0:T(8,128)S(1)} custom-call(bf16[4,4,64,1024]{3,2,1,0:T(8,128)(2,1)S(1)} %bitcast.46), custom_call_target="tpu_custom_call" | custom-call | tf_op jit(solution)/shard_map/line_scatter/pallas_call | solution.py:412
  1065.5 0.6 copy-done.29
  1066.2 1.1 multiply_reduce_fusion.6
  1068.7 37.5 %reduce-scatter.9.cloned.1.call-done = bf16[512,2048]{1,0:T(8,128)(2,1)} async-done(((bf16[4096,2048]{1,0:T(8,128)(2,1)}), bf16[512,2048]{1,0:T(8,128)(2,1)}) %reduce-scatter.9.cloned.1.call-update) | async-done | bytes 2097168 | tf_op jit(solution)/shard_map/reduce_scatter | solution.py:824
  1106.2 12.1 fusion.15
  1119.0 0.6 reshape.231
  1120.4 0.9 copy.69
  1121.3 11.7 convolution_convert_fusion
  1133.0 142.6 %scatter_all.3 = (f32[4,16,5120]{2,1,0:T(8,128)}, f32[4,16,128]{2,1,0:T(8,128)}) custom-call(bf16[2,2,2,4,4,16,5120]{6,5,4,3,2,1,0:T(8,128)(2,1)} %bitcast.49, bf16[2,2,2,4,4,16,128]{6,5,4,3,2,1,0:T(8,128)(2,1)} %bitcast.62), custom_call_target="tpu_custom_call" | custom-call | tf_op jit(solution)/shard_map/scatter_all/pallas_call | solution.py:283
  1275.6 0.7 slice.85
  1276.4 0.7 copy.65
  1277.0 2.4 slice.98
  1279.5 1.3 fusion.34
  1280.8 1.3 fusion.35
  1282.1 1.7 fusion.32
  1283.8 3.4 fusion.12
  1287.2 2.5 add_convert_fusion
  1289.7 2.1 convert_element_type.201
  (145 shorter events, 7.6 us)
Async XLA Ops:
  8.0 548.9 %all-gather.2.cloned.1.call-start = ((), (), s32[]{:S(2)}) async-start(), calls=%async_computation.4 | async-start | bytes 34603008 | tf_op jit(solution)/shard_map/all_gather | solution.py:770
  8.9 172.8 %copy-start.38 = (s32[256,8]{0,1:T(8,128)S(1)}, s32[256,8]{0,1:T(8,128)}, u32[]{:S(2)}) copy-start(s32[256,8]{0,1:T(8,128)} %param.28) | copy-start | bytes 24580
  181.5 883.8 %reduce-scatter.5.cloned.1.call-start = ((), (), s32[]{:S(2)}) async-start(), calls=%async_computation.5 | async-start | bytes 37748736 | tf_op jit(solution)/shard_map/reduce_scatter | solution.py:804
  183.4 0.6 copy-start.28
  183.5 35.2 %copy-start.4 = (f32[1,128]{1,0:T(1,128)}, f32[1,128]{1,0:T(1,128)S(1)}, u32[]{:S(2)}) copy-start(f32[1,128]{1,0:T(1,128)S(1)} %reshape.236.gq_ref) | copy-start | bytes 1540
  184.0 72.2 %copy-start.30 = (f32[2048]{0:T(1024)}, f32[2048]{0:T(1024)S(1)}, u32[]{:S(2)}) copy-start(f32[2048]{0:T(1024)S(1)} %reshape.238) | copy-start | bytes 24580
  184.1 22.2 %copy-start.26 = (f32[2048]{0:T(1024)}, f32[2048]{0:T(1024)S(1)}, u32[]{:S(2)}) copy-start(f32[2048]{0:T(1024)S(1)} %reshape.234) | copy-start | bytes 24580
  184.5 72.0 %copy-start.21 = (bf16[2048,32]{1,0:T(8,128)(2,1)}, bf16[2048,32]{1,0:T(8,128)(2,1)S(1)}, u32[]{:S(2)}) copy-start(bf16[2048,32]{1,0:T(8,128)(2,1)S(1)} %reshape_reshape.28) | copy-start | bytes 393220
  184.5 3.6 copy-start.20
  203.1 2.3 copy-start.41
  203.1 2.3 copy-start.14
  205.5 13.3 %copy-start = (f32[1024,128]{1,0:T(8,128)}, f32[1024,128]{1,0:T(8,128)S(1)}, u32[]{:S(2)}) copy-start(f32[1024,128]{1,0:T(8,128)S(1)} %get-tuple-element.164.cos_ref) | copy-start | bytes 1572868
  205.5 13.3 %copy-start.2 = (f32[1024,128]{1,0:T(8,128)}, f32[1024,128]{1,0:T(8,128)S(1)}, u32[]{:S(2)}) copy-start(f32[1024,128]{1,0:T(8,128)S(1)} %get-tuple-element.165.sin_ref) | copy-start | bytes 1572868
  206.3 12.4 copy-start.32
  245.2 10.5 copy-start.6
  245.2 10.5 copy-start.7
  245.2 10.5 copy-start.9
  255.7 1.4 copy-start.11
  256.2 0.8 copy-start.34
  256.5 3.3 copy-start.18
  257.0 0.7 copy-start.24
  257.1 2.8 copy-start.36
  556.8 549.3 %reduce-scatter.9.cloned.1.call-start = ((), (), s32[]{:S(2)}) async-start(), calls=%async_computation.7 | async-start | bytes 18874368 | tf_op jit(solution)/shard_map/reduce_scatter | solution.py:824
  683.9 273.3 %copy-start.25 = (f32[256,32]{1,0:T(8,128)S(1)}, f32[256,32]{1,0:T(8,128)}, u32[]{:S(2)}) copy-start(f32[256,32]{1,0:T(8,128)} %copy-done.24) | copy-start | bytes 98308
  684.0 273.3 %copy-start.37 = (f32[256]{0:T(256)S(1)}, f32[256]{0:T(256)}, u32[]{:S(2)}) copy-start(f32[256]{0:T(256)} %copy-done.36) | copy-start | bytes 3076
  684.0 274.4 %copy-start.22 = (bf16[2048,32]{1,0:T(8,128)(2,1)S(1)}, bf16[2048,32]{1,0:T(8,128)(2,1)}, u32[]{:S(2)}) copy-start(bf16[2048,32]{1,0:T(8,128)(2,1)} %copy-done.21) | copy-start | bytes 393220
  684.0 274.4 %copy-start.31 = (f32[2048]{0:T(1024)S(1)}, f32[2048]{0:T(1024)}, u32[]{:S(2)}) copy-start(f32[2048]{0:T(1024)} %copy-done.30) | copy-start | bytes 24580
  684.0 274.4 %copy-start.35 = (f32[256]{0:T(256)S(1)}, f32[256]{0:T(256)}, u32[]{:S(2)}) copy-start(f32[256]{0:T(256)} %copy-done.34) | copy-start | bytes 3076
  958.4 3.2 copy-start.12
  958.4 3.2 copy-start.23
  958.5 3.2 copy-start.40
  962.3 10.5 copy-start.16
  990.9 1.0 copy-start.1
  990.9 1.2 copy-start.3
  990.9 1.2 copy-start.5
  990.9 1.6 copy-start.8
  990.9 1.9 copy-start.10
  990.9 296.3 %reduce-scatter.7.cloned.1.call-start = ((), (), s32[]{:S(2)}) async-start(), calls=%async_computation.6 | async-start | bytes 5242880 | tf_op jit(solution)/shard_map/reduce_scatter | solution.py:832
  1065.4 0.7 copy-start.29
  1065.4 2.0 copy-start.42
  1065.4 224.3 %reduce-scatter.11.cloned.1.call-start = ((), (), s32[]{:S(2)}) async-start(), calls=%async_computation.8 | async-start | bytes 2621440 | tf_op jit(solution)/shard_map/reduce_scatter | solution.py:825
  1068.3 37.9 %copy-start.15 = (bf16[256,2048]{1,0:T(8,128)(2,1)S(1)}, bf16[256,2048]{1,0:T(8,128)(2,1)}, u32[]{:S(2)}) copy-start(bf16[256,2048]{1,0:T(8,128)(2,1)} %param.15) | copy-start | bytes 3145732
  1068.3 37.9 %copy-start.27 = (f32[2048]{0:T(1024)S(1)}, f32[2048]{0:T(1024)}, u32[]{:S(2)}) copy-start(f32[2048]{0:T(1024)} %copy-done.26) | copy-start | bytes 24580
  1068.3 37.9 %copy-start.33 = (f32[256]{0:T(256)S(1)}, f32[256]{0:T(256)}, u32[]{:S(2)}) copy-start(f32[256]{0:T(256)} %copy-done.32) | copy-start | bytes 3076
  1106.2 12.2 copy-start.19
  1275.6 8.3 copy-start.39
  1277.0 6.8 copy-start.17
  1283.8 3.4 copy-start.13
Sparse Core Ops, SparseCore 0:
  181.6 275.9 all-gather.1
Sparse Core Ops, SparseCore 1:
  556.9 311.3 reduce-scatter.4
  991.0 115.1 reduce-scatter.8
  1108.3 91.4 reduce-scatter.6
  1202.1 69.3 reduce-scatter.10

commit v5 on v4

--- a/solution.py
+++ b/solution.py
@@ -32,10 +32,14 @@
 
 def ag_kernel(n_arr, n_line, *refs):
     n_all = n_arr + n_line
-    ins = refs[:n_all]; outs = refs[n_all:2 * n_all]
-    loc_sem, zs, zr, ps, pr, cs, cr = refs[2 * n_all:]
+    for run in ag_steps(n_arr, n_line, refs[:n_all], refs[n_all:2 * n_all], refs[2 * n_all:]): run()
+
+AG_STEPS = 10
+
+def ag_steps(n_arr, n_line, ins, outs, sems):
+    n_all = n_arr + n_line
+    loc_sem, zs, zr, ps, pr, cs, cr = sems
     y, x, c, s = place()
-    barrier_all(y, x, c, s)
     def rc(src, dst, ss, rs, d):
         return pltpu.make_async_remote_copy(src_ref=src, dst_ref=dst, send_sem=ss, recv_sem=rs, device_id=d, device_id_type=MESH)
     X = dev(y, 1 - x, c, s); Y = dev(1 - y, x, c, s); C = dev(y, x, 1 - c, s)
@@ -119,45 +123,50 @@
                 diag_recv(a, 1, zz, k).wait_recv()
                 core(a, zz, k, 0).start()
         when(k, go)
-    for a in every: loc(a).start()
     n = len(steps)
-    for i in range(n + 2):
+    def advance(i):
+        if i == 0:
+            barrier_all(y, x, c, s)
+            for a in every: loc(a).start()
         if i < n: stage_a(i)
         if 0 <= i - 1 < n: stage_b(i - 1)
         if 0 <= i - 2 < n: stage_c(i - 2)
-    for k in range(n):
-        d, g = steps[k]
-        def go():
-            zz = zof(d, g)
-            for a in every:
-                if a < n_arr:
-                    core_recv(a, zz, k).wait_recv()
-                    core(a, zz, k, 0).wait_send()
-                elif k == 0: loc(a).wait()
-                for h in range(2):
-                    for gg in ((1, -1) if k == 0 else (g,)):
-                        okc = (s < NZ - 1) if gg == 1 else (s > 0)
-                        if d + 1 < NZ:
-                            @pl.when(okc)
-                            def _(): zcopy(a, h, zz, k, gg).wait_send()
+    def finish():
+        for k in range(n):
+            d, g = steps[k]
+            def go():
+                zz = zof(d, g)
+                for a in every:
                     if a < n_arr:
-                        plane(a, h, zz, k, 0).wait_send()
-                        plane(a, h, zz, k, 1).wait_send()
-                        diag(a, h, zz, k).wait_send()
-        when(k, go)
+                        core_recv(a, zz, k).wait_recv()
+                        core(a, zz, k, 0).wait_send()
+                    elif k == 0: loc(a).wait()
+                    for h in range(2):
+                        for gg in ((1, -1) if k == 0 else (g,)):
+                            okc = (s < NZ - 1) if gg == 1 else (s > 0)
+                            if d + 1 < NZ:
+                                @pl.when(okc)
+                                def _(): zcopy(a, h, zz, k, gg).wait_send()
+                        if a < n_arr:
+                            plane(a, h, zz, k, 0).wait_send()
+                            plane(a, h, zz, k, 1).wait_send()
+                            diag(a, h, zz, k).wait_send()
+            when(k, go)
+    return [functools.partial(advance, i) for i in range(n + 2)] + [finish]
+
+def ag_sems(n, m=0):
+    D = pltpu.SemaphoreType.DMA
+    return [D((n + m,)), D((n + m, 2, 9)), D((n + m, 2, 9)), D((n, 7, 2, 3)), D((n, 7, 2, 3)), D((n, 7)), D((n, 7))]
 
 def ag32(arrs, cid, line=()):
     ins = [a.reshape(2, a.shape[0] // 2, a.shape[1]) for a in list(arrs) + list(line)]
-    n, m = len(arrs), len(line); nk = 7
+    n, m = len(arrs), len(line)
     outs = pl.pallas_call(
         functools.partial(ag_kernel, n, m),
         out_shape=[jax.ShapeDtypeStruct(((2, 2, 2, NZ) if i < n else (NZ,)) + a.shape, a.dtype) for i, a in enumerate(ins)],
         in_specs=[pl.BlockSpec(memory_space=pltpu.VMEM)] * (n + m),
         out_specs=[pl.BlockSpec(memory_space=pl.ANY)] * (n + m),
-        scratch_shapes=[pltpu.SemaphoreType.DMA((n + m,)),
-            pltpu.SemaphoreType.DMA((n + m, 2, 9)), pltpu.SemaphoreType.DMA((n + m, 2, 9)),
-            pltpu.SemaphoreType.DMA((n, nk, 2, 3)), pltpu.SemaphoreType.DMA((n, nk, 2, 3)),
-            pltpu.SemaphoreType.DMA((n, nk)), pltpu.SemaphoreType.DMA((n, nk))],
+        scratch_shapes=ag_sems(n, m),
         compiler_params=pltpu.CompilerParams(collective_id=cid, has_side_effects=True, vmem_limit_bytes=64000 * 1024),
         name="gather_all",
     )(*ins)
@@ -166,11 +175,13 @@
 ZORDER = (0, 3, 1, 2)
 LAGS = (1, 1, 1, 1)
 
-def rs_kernel(n_arr, parts, *refs):
-    ins = refs[:n_arr]; outs = refs[n_arr:2 * n_arr]
-    sc = refs[2 * n_arr:]
-    own_b, r0_b, ra_b, rb_b, zu_b, zd_b = [sc[i * n_arr:(i + 1) * n_arr] for i in range(6)]
-    lsem, s0s, s0r, sas, sar, sbs, sbr, zus, zur, zds, zdr = sc[6 * n_arr:]
+def rs_kernel(n_arr, n_line, parts, *refs):
+    n_all = n_arr + n_line
+    ins = refs[:n_all]; outs = refs[n_all:2 * n_all]
+    sc = list(refs[2 * n_all:])
+    own_b = [sc.pop(0) for _ in range(n_all)]; zu_b = [sc.pop(0) for _ in range(n_all)]; zd_b = [sc.pop(0) for _ in range(n_all)]
+    r0_b, ra_b, rb_b = [[sc.pop(0) for _ in range(n_arr)] for _ in range(3)]
+    lsem, s0s, s0r, sas, sar, sbs, sbr, zus, zur, zds, zdr = sc
     y, x, c, s = place()
     barrier_all(y, x, c, s)
     X = dev(y, 1 - x, c, s); Y = dev(1 - y, x, c, s); C = dev(y, x, 1 - c, s)
@@ -178,10 +189,14 @@
     def rc(src, dst, ss, rs, d):
         return pltpu.make_async_remote_copy(src_ref=src, dst_ref=dst, send_sem=ss, recv_sem=rs, device_id=d, device_id_type=MESH)
     units = [(a, zz, h) for zz in ZORDER for h in range(parts) for a in range(n_arr)]
+    lines = [(a, zz, h) for zz in ZORDER for h in range(parts) for a in range(n_arr, n_all)]
     def jj(zz, h): return ZORDER.index(zz) * parts + h
     def load(a, zz, h):
         j = jj(zz, h)
-        return pltpu.make_async_copy(ins[a].at[:, :, c, zz, h], own_b[a].at[j], lsem.at[a, j])
+        src = ins[a].at[:, :, c, zz, h] if a < n_arr else ins[a].at[zz, h]
+        return pltpu.make_async_copy(src, own_b[a].at[j], lsem.at[a, j])
+    def mine(a, j):
+        return own_b[a].at[j, y, x] if a < n_arr else own_b[a].at[j]
     def c0(a, zz, h):
         j = jj(zz, h)
         return rc(ins[a].at[:, :, 1 - c, zz, h], r0_b[a].at[j], s0s.at[a, j], s0r.at[a, j], C)
@@ -195,10 +210,10 @@
         return rc(own_b[a].at[j, y, 1 - x], rb_b[a].at[j], sbs.at[a, j], sbr.at[a, j], X)
     def cu(a, zz, h):
         j = jj(zz, h)
-        return rc(own_b[a].at[j, y, x], zu_b[a].at[j], zus.at[a, j], zur.at[a, j], UP)
+        return rc(mine(a, j), zu_b[a].at[j], zus.at[a, j], zur.at[a, j], UP)
     def cd(a, zz, h):
         j = jj(zz, h)
-        return rc(own_b[a].at[j, y, x], zd_b[a].at[j], zds.at[a, j], zdr.at[a, j], DN)
+        return rc(mine(a, j), zd_b[a].at[j], zds.at[a, j], zdr.at[a, j], DN)
     def add_into(dst, other):
         rows = dst.shape[0]
         st = 16 if rows % 16 == 0 else rows
@@ -232,7 +247,7 @@
             def _():
                 if k > 0:
                     cu(a, zz, h).wait_recv()
-                    add_into(own_b[a].at[j, y, x], zu_b[a].at[j])
+                    add_into(mine(a, j), zu_b[a].at[j])
                 cu(a, zz, h).start()
         t = NZ - 1 - k
         if t > zz:
@@ -240,7 +255,7 @@
             def _():
                 if k > 0:
                     cd(a, zz, h).wait_recv()
-                    add_into(own_b[a].at[j, y, x], zd_b[a].at[j])
+                    add_into(mine(a, j), zd_b[a].at[j])
                 cd(a, zz, h).start()
     def last(u):
         a, zz, h = u; j = jj(zz, h)
@@ -248,24 +263,31 @@
         def _():
             if zz > 0: cu(a, zz, h).wait_recv()
             if zz < NZ - 1: cd(a, zz, h).wait_recv()
-            t = own_b[a][j, y, x].astype(jnp.float32)
+            t = mine(a, j)[...].astype(jnp.float32)
             if zz > 0: t = t + zu_b[a][j].astype(jnp.float32)
             if zz < NZ - 1: t = t + zd_b[a][j].astype(jnp.float32)
             outs[a][h] = t.astype(outs[a].dtype)
+    for u in lines: load(*u).start()
     for u in units:
         c0(*u).start(); load(*u).start()
-    n = len(units)
+    n = len(units); nl = len(lines)
     L1 = LAGS[0] * n_arr; L2 = L1 + LAGS[1] * n_arr; L3 = L2 + LAGS[2] * n_arr; dl = LAGS[3] * n_arr
     for i in range(n + L3 + (NZ - 1) * dl):
         if i < n: stage0(units[i])
         if 0 <= i - L1 < n: stage1(units[i - L1])
         if 0 <= i - L2 < n: stage2(units[i - L2])
         for k in range(NZ - 1):
+            for q in (2 * (i - k), 2 * (i - k) + 1):
+                if 0 <= q < nl:
+                    if k == 0: load(*lines[q]).wait()
+                    hop(lines[q], k)
+        for k in range(NZ - 1):
             if 0 <= i - L3 - k * dl < n: hop(units[i - L3 - k * dl], k)
-    for u in units: last(u)
-    for u in units:
-        c0(*u).wait_send(); ca(*u).wait_send(); cb(*u).wait_send()
-        zz = u[1]
+    for u in lines + units: last(u)
+    for u in lines + units:
+        a, zz, h = u
+        if a < n_arr:
+            c0(*u).wait_send(); ca(*u).wait_send(); cb(*u).wait_send()
         if zz > 0:
             @pl.when(s < zz)
             def _(): cu(*u).wait_send()
@@ -273,24 +295,25 @@
             @pl.when(s > zz)
             def _(): cd(*u).wait_send()
 
-def rs32(arrs, cid, out_dtype=jnp.float32, parts=4):
-    n = len(arrs)
-    if any(a.shape[1] % (parts * 16) for a in arrs): parts = 2
-    ins = [a.reshape(2, 2, 2, NZ, parts, a.shape[1] // parts, a.shape[2]) for a in arrs]
+def rs32(arrs, cid, out_dtype=jnp.float32, parts=4, line=()):
+    n, nl = len(arrs), len(line)
+    both = list(arrs) + list(line)
+    if any(a.shape[1] % (parts * 16) for a in both): parts = 2
+    ins = [a.reshape(((2, 2, 2) if i < n else ()) + (NZ, parts, a.shape[1] // parts, a.shape[2])) for i, a in enumerate(both)]
     hs = [i.shape[-2:] for i in ins]
     V = pltpu.VMEM; bt = jnp.bfloat16; m = NZ * parts
-    sems = [pltpu.SemaphoreType.DMA((n, m))] * 11
+    sems = [pltpu.SemaphoreType.DMA((n + nl, m))] * 11
     outs = pl.pallas_call(
-        functools.partial(rs_kernel, n, parts),
+        functools.partial(rs_kernel, n, nl, parts),
         out_shape=[jax.ShapeDtypeStruct((parts,) + h, out_dtype) for h in hs],
-        in_specs=[pl.BlockSpec(memory_space=pl.ANY)] * n,
-        out_specs=[pl.BlockSpec(memory_space=pltpu.VMEM)] * n,
-        scratch_shapes=[V((m, 2, 2) + h, bt) for h in hs] + [V((m, 2, 2) + h, bt) for h in hs] + [V((m, 2) + h, bt) for h in hs]
-            + [V((m,) + h, bt) for h in hs] + [V((m,) + h, bt) for h in hs] + [V((m,) + h, bt) for h in hs] + sems,
+        in_specs=[pl.BlockSpec(memory_space=pl.ANY)] * (n + nl),
+        out_specs=[pl.BlockSpec(memory_space=pltpu.VMEM)] * (n + nl),
+        scratch_shapes=[V((m,) + ((2, 2) if i < n else ()) + h, bt) for i, h in enumerate(hs)] + [V((m,) + h, bt) for h in hs] + [V((m,) + h, bt) for h in hs]
+            + [V((m, 2, 2) + h, bt) for h in hs[:n]] + [V((m, 2) + h, bt) for h in hs[:n]] + [V((m,) + h, bt) for h in hs[:n]] + sems,
         compiler_params=pltpu.CompilerParams(collective_id=cid, has_side_effects=True, vmem_limit_bytes=64000 * 1024),
         name="scatter_all",
     )(*ins)
-    return [o.reshape(a.shape[1], a.shape[2]) for o, a in zip(outs, arrs)]
+    return [o.reshape(a.shape[1], a.shape[2]) for o, a in zip(outs, both)]
 
 def line_barrier(y, x, c, s):
     bar = pltpu.get_barrier_semaphore()
@@ -433,9 +456,17 @@
     pick = (want == lax.broadcasted_iota(jnp.int32, (SB, slots), 1)).astype(bf)
     return pick, gate
 
-def forward_kernel(experts, slots, SB, x_ref, wg_hbm, wu_hbm, wd_hbm, out_ref, rows_ref, ga_ref, ua_ref, wg, wu, wd, wsem):
+def forward_kernel(experts, slots, SB, guest, *refs):
+    if guest:
+        cot_ref, x_ref, wg_hbm, wu_hbm, wd_hbm, cot_all, out_ref, rows_ref, ga_ref, ua_ref, wg, wu, wd, wsem = refs[:14]
+    else:
+        x_ref, wg_hbm, wu_hbm, wd_hbm, out_ref, rows_ref, ga_ref, ua_ref, wg, wu, wd, wsem = refs
     bf = jnp.bfloat16
     step = pl.program_id(0)
+    if guest:
+        runs = ag_steps(1, 0, [cot_ref], [cot_all], refs[14:])
+        for i, run in enumerate(runs[:-1]):
+            pl.when(step == GUEST_AT[i])(run)
     nsub = x_ref.shape[0] // SB
     D = out_ref.shape[1]
     me = lax.axis_index(("expert", "shard"))
@@ -462,14 +493,18 @@
         r = pl.ds(i * SB, SB)
         tok = dot(picks[i], eo[i * slots:(i + 1) * slots, :], 1, 0)
         out_ref[r, :] = (gates[i] * tok).astype(bf)
-
-def backward_kernel(experts, slots, SB, meta_ref, cot_ref, rows_ref, ga_ref, ua_ref, wg_hbm, wu_hbm, wd_hbm, gr_ref, dwg_hbm, dwu_hbm, dwd_hbm,
+    if guest: pl.when(step == pl.num_programs(0) - 1)(runs[-1])
+
+GUEST_AT = (0, 1, 3, 4, 6, 7, 9, 11, 13)
+
+def backward_kernel(experts, slots, SB, block, meta_ref, cota_ref, cotb_ref, rows_ref, ga_ref, ua_ref, wg_hbm, wu_hbm, wd_hbm, gr_ref, dwg_hbm, dwu_hbm, dwd_hbm,
                   wg, wu, wd, dwg, dwu, dwd, gp, wsem, osem):
     bf = jnp.bfloat16
     step = pl.program_id(0)
-    nsub = cot_ref.shape[0] // SB
-    D = cot_ref.shape[1]
+    nsub = meta_ref.shape[0] // SB
+    D = cota_ref.shape[1]
     WM = meta_ref.shape[1]
+    half = block // 2
     me = lax.axis_index(("expert", "shard"))
     loads = [pltpu.make_async_copy(h.at[0], v, wsem.at[i]) for i, (h, v) in enumerate(((wg_hbm, wg), (wu_hbm, wu), (wd_hbm, wd)))]
     @pl.when(step == 0)
@@ -481,7 +516,10 @@
         r = pl.ds(i * SB, SB)
         pick, gate = token_picks(meta_ref[r, :], experts, slots, me)
         picks.append(pick)
-        gcot = (gate * cot_ref[r, :].astype(jnp.float32)).astype(bf)
+        cot = []
+        for b in range(i * SB // block, (i + 1) * SB // block):
+            cot += [cota_ref[b * half:(b + 1) * half, :], cotb_ref[b * half:(b + 1) * half, :]]
+        gcot = (gate * jnp.concatenate(cot, axis=0).astype(jnp.float32)).astype(bf)
         gp[i * slots:(i + 1) * slots, :] = dot(pick, gcot, 0, 0).astype(bf)
     @pl.when(step == 0)
     def _():
@@ -514,7 +552,8 @@
         for o in outs: o.start()
         for o in outs: o.wait()
 
-def experts_forward(x_all, w_gate, w_up, w_down, experts, block, capacity, TB=512, SB=256):
+def experts_forward(x_all, w_gate, w_up, w_down, experts, block, capacity, guest, cid, TB=512, SB=256):
+    hosted = placed()
     T, C = x_all.shape; D, F = w_gate.shape[1:]
     slots = max(SB // block, 1) * capacity
     total = TB // SB * slots
@@ -522,19 +561,23 @@
     any_ = pl.BlockSpec(memory_space=pl.ANY)
     V = pltpu.VMEM; bf = jnp.bfloat16; f32 = jnp.float32
     blk = lambda r, c: pl.BlockSpec((r, c), lambda i: (i, 0))
-    return pl.pallas_call(
-        functools.partial(forward_kernel, experts, slots, SB),
+    g = guest.reshape(2, guest.shape[0] // 2, guest.shape[1])
+    res = pl.pallas_call(
+        functools.partial(forward_kernel, experts, slots, SB, hosted),
         grid=(T // TB,),
-        out_shape=[jax.ShapeDtypeStruct((T, D), bf), jax.ShapeDtypeStruct((S, D), bf), jax.ShapeDtypeStruct((S, F), f32), jax.ShapeDtypeStruct((S, F), f32)],
-        in_specs=[blk(TB, C), any_, any_, any_],
-        out_specs=[blk(TB, D), blk(total, D), blk(total, F), blk(total, F)],
-        scratch_shapes=[V((D, F), bf), V((D, F), bf), V((F, D), bf), pltpu.SemaphoreType.DMA((3,))],
-        compiler_params=pltpu.CompilerParams(dimension_semantics=("arbitrary",), vmem_limit_bytes=65000 * 1024),
+        out_shape=([jax.ShapeDtypeStruct((2, 2, 2, NZ) + g.shape, g.dtype)] if hosted else []) + [jax.ShapeDtypeStruct((T, D), bf), jax.ShapeDtypeStruct((S, D), bf), jax.ShapeDtypeStruct((S, F), f32), jax.ShapeDtypeStruct((S, F), f32)],
+        in_specs=([pl.BlockSpec(memory_space=pltpu.VMEM)] if hosted else []) + [blk(TB, C), any_, any_, any_],
+        out_specs=([any_] if hosted else []) + [blk(TB, D), blk(total, D), blk(total, F), blk(total, F)],
+        scratch_shapes=[V((D, F), bf), V((D, F), bf), V((F, D), bf), pltpu.SemaphoreType.DMA((3,))] + (ag_sems(1) if hosted else []),
+        compiler_params=pltpu.CompilerParams(dimension_semantics=("arbitrary",), vmem_limit_bytes=65000 * 1024,
+            **(dict(collective_id=cid, has_side_effects=True) if hosted else {})),
         cost_estimate=pl.CostEstimate(flops=48_000_000_000, bytes_accessed=130_000_000, transcendentals=0),
         name="experts_forward",
-    )(x_all, w_gate, w_up, w_down)
-
-def experts_backward(x_all, cot_all, rows, ga, ua, w_gate, w_up, w_down, experts, block, capacity, TB=512, SB=256):
+    )(*([g] if hosted else []), x_all, w_gate, w_up, w_down)
+    if hosted: return res[1:], res[0].reshape(-1, guest.shape[1])
+    return res, lax.all_gather(guest, BOTH, axis=0, tiled=True)
+
+def experts_backward(x_all, cot_a, cot_b, rows, ga, ua, w_gate, w_up, w_down, experts, block, capacity, TB=512, SB=256):
     T, C = x_all.shape; D, F = w_gate.shape[1:]
     slots = max(SB // block, 1) * capacity
     total = TB // SB * slots
@@ -545,16 +588,16 @@
     meta = pl.BlockSpec((TB, WM), lambda i: (i, D // WM)) if D % WM == 0 else blk(TB, WM)
     meta_in = x_all if D % WM == 0 else x_all[:, D:]
     return pl.pallas_call(
-        functools.partial(backward_kernel, experts, slots, SB),
+        functools.partial(backward_kernel, experts, slots, SB, block),
         grid=(T // TB,),
         out_shape=[jax.ShapeDtypeStruct((T, C), bf), jax.ShapeDtypeStruct(w_gate.shape, f32), jax.ShapeDtypeStruct(w_up.shape, f32), jax.ShapeDtypeStruct(w_down.shape, f32)],
-        in_specs=[meta, blk(TB, D), blk(total, D), blk(total, F), blk(total, F), any_, any_, any_],
+        in_specs=[meta, blk(TB // 2, D), blk(TB // 2, D), blk(total, D), blk(total, F), blk(total, F), any_, any_, any_],
         out_specs=[blk(TB, C), any_, any_, any_],
         scratch_shapes=[V((D, F), bf), V((D, F), bf), V((F, D), bf), V((D, F), f32), V((D, F), f32), V((F, D), f32), V((total, D), bf), pltpu.SemaphoreType.DMA((3,)), pltpu.SemaphoreType.DMA((3,))],
         compiler_params=pltpu.CompilerParams(dimension_semantics=("arbitrary",), vmem_limit_bytes=65000 * 1024),
         cost_estimate=pl.CostEstimate(flops=85_000_000_000, bytes_accessed=150_000_000, transcendentals=0),
         name="experts_backward",
-    )(meta_in, cot_all, rows, ga, ua, w_gate, w_up, w_down)
+    )(meta_in, cot_a, cot_b, rows, ga, ua, w_gate, w_up, w_down)
 
 
 def rope_tables(seq_len):
@@ -720,10 +763,14 @@
     ]
 
 
-def scatter_all(arrays, cid, out_dtype=jnp.float32):
+def scatter_all(arrays, cid, out_dtype=jnp.float32, line=()):
     if placed():
-        return rs32([a.reshape(32, -1, a.shape[-1]) for a in arrays], cid, out_dtype)
-    return [lax.psum_scatter(a, BOTH, scatter_dimension=0, tiled=True).astype(out_dtype) for a in arrays]
+        return rs32(
+            [a.reshape(32, -1, a.shape[-1]) for a in arrays], cid, out_dtype, line=[a.reshape(NZ, -1, a.shape[-1]) for a in line]
+        )
+    return [lax.psum_scatter(a, BOTH, scatter_dimension=0, tiled=True).astype(out_dtype) for a in arrays] + [
+        lax.psum_scatter(a, "shard", scatter_dimension=0, tiled=True).astype(out_dtype) for a in line
+    ]
 
 
 def per_device(
@@ -766,8 +813,9 @@
     wr_full, attn_gain, ffn_gain, query_gain, key_gain = [small_all[:, o : o + n].reshape(-1) for o, n in zip(starts, sizes)]
     wr_full = wr_full.reshape(model_width, expert_count)
     attn_gain, ffn_gain, query_gain, key_gain = [g.astype(f32) for g in (attn_gain, ffn_gain, query_gain, key_gain)]
-    cotangent, wo_full = lax.optimization_barrier((cotangent, wo_full))
-    cot_all = lax.all_gather(cotangent, BOTH, axis=0, tiled=True)
+    half = tok_rows // 2
+    cot_first, wo_full = lax.optimization_barrier((cotangent[:half], wo_full))
+    cot_a = lax.all_gather(cot_first, BOTH, axis=0, tiled=True)
 
     inputs_f = hidden_in.astype(f32)
     normed_low = norm_rows(inputs_f, attn_gain).astype(bf)
@@ -798,14 +846,15 @@
         axis=1,
     )
     (payload_all,) = gather_all([payload], 3)
-    out_part, rows, gate_act, up_act = experts_forward(
-        payload_all, w_gate, w_up, w_down, expert_count, tok_rows, capacity
+    (out_part, rows, gate_act, up_act), cot_b = experts_forward(
+        payload_all, w_gate, w_up, w_down, expert_count, tok_rows, capacity, cotangent[half:], 2
     )
     moe_out = lax.psum_scatter(out_part, "expert", scatter_dimension=0, tiled=True)
     grad_part, grad_wgate, grad_wup, grad_wdown = experts_backward(
-        payload_all, cot_all, rows, gate_act, up_act, w_gate, w_up, w_down, expert_count, tok_rows, capacity
+        payload_all, cot_a, cot_b, rows, gate_act, up_act, w_gate, w_up, w_down, expert_count, tok_rows, capacity
     )
     (grad_sum,) = scatter_all([grad_part], 4)
+    grad_sum, moe_out = lax.optimization_barrier((grad_sum, moe_out))
     upstream = cotangent.astype(f32)
     grad_ffn = grad_sum[:, :model_width]
     grad_shares = (
@@ -822,15 +871,11 @@
     grad_mix = matmul_nt(grad_attn_low, wo_full).astype(bf)
     grad_mix, grad_wout = lax.optimization_barrier((grad_mix, grad_wout))
     out_grad = lax.psum_scatter(grad_wout, "expert", scatter_dimension=0, tiled=True)
-    out_grad = lax.psum_scatter(out_grad, "shard", scatter_dimension=0, tiled=True).astype(f32)
 
     grad_q_low, grad_kv, grad_query_gain = attention_backward(
         q_proj, q_low, k_low, v_low, grad_mix, query_gain, cosine, sine
     )
     grad_kv = line_scatter(grad_kv, 6)
-    grad_kv, moe_out = lax.optimization_barrier((grad_kv, moe_out))
-    moe_out = lax.psum_scatter(moe_out, "shard", scatter_dimension=0, tiled=True).astype(f32)
-    block_out = (residual + moe_out).astype(bf)
     own_rows = shard_pos * tok_rows
     k_proj = lax.dynamic_slice(kv_proj, (own_rows, 0), (tok_rows, kv_cols))
     positions = own_rows + jnp.arange(tok_rows, dtype=jnp.int32)
@@ -850,7 +895,10 @@
     packed = jnp.concatenate(
         [g.astype(bf).reshape(devices, -1) for g in grads] + [jnp.zeros((devices, small_rows * 128 - used), bf)], axis=1
     ).reshape(devices * small_rows, 128)
-    qkv_grad, small_grad = scatter_all([grad_wqkv, packed], 8)
+    grad_wqkv, out_grad = lax.optimization_barrier((grad_wqkv, out_grad))
+    out_grad = lax.psum_scatter(out_grad, "shard", scatter_dimension=0, tiled=True).astype(f32)
+    qkv_grad, small_grad, moe_out = scatter_all([grad_wqkv, packed], 8, line=[moe_out])
+    block_out = (residual + moe_out).astype(bf)
     small_grad = small_grad.reshape(-1)
     router_g, attn_g, ffn_g, query_g, key_g = [small_grad[o : o + n] for o, n in zip(starts, sizes)]
     return (

time: 1300 us -> 1310 us (level)
    pallas_call x4, Pallas kernels: 617 us -> 667 us  [the longest x2 422 us: rs32(): pl.pallas_call(functools.partial(rs_kernel, n, nl, parts), out_shape=[jax...]
    pallas_call x2, Pallas kernels: 389 us -> 347 us  [ag32(): pl.pallas_call(functools.partial(ag_kernel, n, m), out_shape=[jax.ShapeDt...]
  transfers between devices with their start and end apart: 5 -> 4, of which waited for: 1 -> 1; matrix products, arithmetic and copies ran while one was open for 10% -> 8% of each run, Pallas kernels for 72% -> 73%
where the time goes in v5:
time: 1310 us; the launch traced here: 1300 us
  Pallas kernels  1110 us (85%)
  matrix products  88.4 us (7%)
  local copies, waits for them, and re-layouts  32.3 us (2%)
  waiting for transfers between devices  25.6 us (2%)
  other arithmetic  25.2 us (2%)
  between operations  16.6 us (1%)
    pallas_call x2, Pallas kernels, rs32(): pl.pallas_call(functools.partial(rs_kernel, n, nl, parts), out_shape=[jax...  422 us
    pallas_call x2, Pallas kernels, ag32(): pl.pallas_call(functools.partial(ag_kernel, n, m), out_shape=[jax.ShapeDt...  347 us
    pallas_call x1, Pallas kernels, experts_backward(): pl.pallas_call(functools.partial(backward_kernel, experts, slots, SB, blo...  128 us
    pallas_call x1, Pallas kernels, experts_forward(): pl.pallas_call(functools.partial(forward_kernel, experts, slots, SB, host...  117 us
    pallas_call x1, Pallas kernels, attention_backward(): pl.pallas_call(functools.partial(attention_backward_kernel, group), grid=...  38.2 us
    dot_general x3, matrix products, matmul_nt(): lax.dot_general(left, right, (((1,), (1,)), ((), ())), preferred_element_...  34 us
    pallas_call x1, Pallas kernels, line_scatter(): pl.pallas_call(functools.partial(line_scatter_kernel, parts), out_shape=j...  33.1 us
    dot_general x4, matrix products, matmul(): return jnp.dot(left, right, preferred_element_type=jnp.float32)  32.3 us
  transfers between devices with their start and end apart: 4, of which 1 were waited for; matrix products, arithmetic and copies ran while one was open for 8% of the time, Pallas kernels for 73%

profile of v5, /device:TPU:18, one launch (start us, length us, event | category | flops | bytes accessed | tf_op | source)
XLA Modules:
  0.0 1301.5 jit_solution(7182924661717046378)
XLA Ops:
  8.1 0.9 copy.55
  9.1 2.3 fusion.34
  11.4 0.9 pad_maximum_fusion.4
  12.3 0.7 concatenate.31
  13.0 167.2 %gather_all.2 = (bf16[2,2,2,4,2,32,5120]{6,5,4,3,2,1,0:T(8,128)(2,1)}, bf16[2,2,2,4,2,32,128]{6,5,4,3,2,1,0:T(8,128)(2,1)}, bf16[2,2,2,4,2,64,2048]{6,5,4,3,2,1,0:T(8,128)(2,1)}, bf16[4,2,128,2048]{3,2,1,0:T(8,128)(2,1)}) custom-call(bf16[2,32,5120]{2,1,0:T(8,128)(2,1)} %bitcast.68, bf16[2,32,128]{2,1,0:T(8,128)(2,1)} %bitcast.76, ...), custom_call_target="tpu_custom_call" | custom-call | tf_op jit(solution)/shard_map/gather_all/pallas_call | solution.py:164
  180.7 1.3 reshape_reshape_reshape.6
  183.2 3.3 multiply_reduce_fusion
  186.8 1.0 fusion.3
  187.8 8.4 fusion.4
  196.2 5.4 copy.56.k_ref.v_ref
  201.7 2.0 fusion.27
  205.0 12.5 fusion.q_ref.u_ref
  217.5 26.6 %attention_forward.1 = (bf16[256,4096]{1,0:T(8,128)(2,1)S(1)}, bf16[1024,512]{1,0:T(8,128)(2,1)S(1)}, bf16[1024,512]{1,0:T(8,128)(2,1)S(1)}, bf16[256,4096]{1,0:T(8,128)(2,1)}) custom-call(f32[256,4096]{1,0:T(8,128)} %fusion.q_ref.u_ref, f32[1024,1024]{1,0:T(8,128)} %copy.56.k_ref.v_ref, f32[1024,1024]{1,0:T(8,128)} %copy.56.k_ref.v_ref, ...), custom_call_target="tpu_custom_call" | custom-call | flops 4300000256 | bytes 20000000 | tf_op jit(solution)/shard_map/attention_forward/pallas_call | solution.py:640
  244.1 10.9 multiply_reduce_fusion.3
  257.9 2.0 concatenate.34
  259.9 180.2 %gather_all.3 = bf16[2,2,2,4,2,128,2176]{6,5,4,3,2,1,0:T(8,128)(2,1)} custom-call(bf16[2,128,2176]{2,1,0:T(8,128)(2,1)} %bitcast.66), custom_call_target="tpu_custom_call" | custom-call | tf_op jit(solution)/shard_map/gather_all/pallas_call | solution.py:164
  440.0 117.4 %experts_forward.1 = (bf16[2,2,2,4,2,64,2048]{6,5,4,3,2,1,0:T(8,128)(2,1)}, bf16[8192,2048]{1,0:T(8,128)(2,1)}, bf16[4096,2048]{1,0:T(8,128)(2,1)}, f32[4096,768]{1,0:T(8,128)}, f32[4096,768]{1,0:T(8,128)}) custom-call(bf16[2,64,2048]{2,1,0:T(8,128)(2,1)} %bitcast.75, bf16[8192,2176]{1,0:T(8,128)(2,1)} %bitcast.57, bf16[1,2048,768]{2,1,0:T(8,128)(2,1)} %wg_hbm.1, ...), custom_call_target="tpu_custom_call" | custom-call | flops 48000000000 | bytes 130000000 | tf_op jit(solution)/shard_map/experts_forward/pallas_call | solution.py:565
  557.5 128.1 %experts_backward.1 = (bf16[8192,2176]{1,0:T(8,128)(2,1)}, f32[1,2048,768]{2,1,0:T(8,128)}, f32[1,2048,768]{2,1,0:T(8,128)}, f32[1,768,2048]{2,1,0:T(8,128)}) custom-call(bf16[8192,2176]{1,0:T(8,128)(2,1)} %bitcast.58, bf16[4096,2048]{1,0:T(8,128)(2,1)} %all-gather.2.cloned.1.call-done.cota_ref, bf16[4096,2048]{1,0:T(8,128)(2,1)} %bitcast.85, ...), custom_call_target="tpu_custom_call" | custom-call | flops 85000003584 | bytes 150000000 | tf_op jit(solution)/shard_map/experts_backward/pallas_call | solution.py:590
  685.7 243.6 %scatter_all.2 = f32[4,64,2176]{2,1,0:T(8,128)} custom-call(bf16[2,2,2,4,4,64,2176]{6,5,4,3,2,1,0:T(8,128)(2,1)} %bitcast.59), custom_call_target="tpu_custom_call" | custom-call | tf_op jit(solution)/shard_map/scatter_all/pallas_call | solution.py:306
  929.3 1.2 fusion.29
  930.5 1.1 subtract_convert_fusion
  931.7 3.1 multiply_reduce_fusion.1
  935.5 18.8 %convolution_convert_fusion.2.gm_ref = bf16[256,4096]{1,0:T(8,128)(2,1)} fusion(bf16[4096,2048]{1,0:T(8,128)(2,1)} %bitcast.84, f32[256,2048]{1,0:T(8,128)S(1)} %subtract_add_fusion), kind=kOutput, calls=%fused_computation.8 | convolution fusion | flops 4296540160 | bytes 20971520 | tf_op jit(solution)/shard_map/dot_general | solution.py:723
  954.3 9.9 convolution_convert_fusion.1
  965.0 2.0 multiply_reduce_fusion.6
  967.4 0.7 pad_maximum_fusion.7
  968.1 38.2 %attention_backward.1 = (bf16[256,4096]{1,0:T(8,128)(2,1)}, bf16[1024,512]{1,0:T(8,128)(2,1)S(1)}, bf16[1024,512]{1,0:T(8,128)(2,1)S(1)}, f32[4,8,128]{2,1,0:T(8,128)S(1)}) custom-call(f32[256,4096]{1,0:T(8,128)} %fusion.q_ref.u_ref, bf16[256,4096]{1,0:T(8,128)(2,1)} %copy-done.6, bf16[1024,512]{1,0:T(8,128)(2,1)S(1)} %copy-done.8, ...), custom_call_target="tpu_custom_call" | custom-call | flops 10700000256 | bytes 20000000 | tf_op jit(solution)/shard_map/attention_backward/pallas_call | solution.py:691
  1006.7 33.1 %line_scatter.1 = f32[4,64,1024]{2,1,0:T(8,128)S(1)} custom-call(bf16[4,4,64,1024]{3,2,1,0:T(8,128)(2,1)S(1)} %bitcast.53), custom_call_target="tpu_custom_call" | custom-call | tf_op jit(solution)/shard_map/line_scatter/pallas_call | solution.py:435
  1040.7 1.2 reshape.242
  1041.9 0.7 convert_element_type.192
  1043.5 0.7 convert_element_type.194
  1044.2 11.9 convolution_convert_fusion
  1056.2 25.5 %reduce-scatter.6.cloned.1.call-done = bf16[512,2048]{1,0:T(8,128)(2,1)} async-done(((bf16[4096,2048]{1,0:T(8,128)(2,1)}), bf16[512,2048]{1,0:T(8,128)(2,1)}) %reduce-scatter.6.cloned.1.call-update) | async-done | bytes 2097168 | tf_op jit(solution)/shard_map/reduce_scatter | solution.py:873
  1081.7 12.1 fusion.15
  1093.8 0.7 convert_element_type.188
  1094.5 2.0 concatenate.39
  1096.5 2.0 copy.69
  1098.4 0.7 broadcast_multiply_fusion.1
  1099.1 3.2 fusion.14
  1102.3 178.4 %scatter_all.3 = (f32[4,16,5120]{2,1,0:T(8,128)}, f32[4,16,128]{2,1,0:T(8,128)}, f32[4,64,2048]{2,1,0:T(8,128)}) custom-call(bf16[2,2,2,4,4,16,5120]{6,5,4,3,2,1,0:T(8,128)(2,1)} %bitcast.56, bf16[2,2,2,4,4,16,128]{6,5,4,3,2,1,0:T(8,128)(2,1)} %bitcast.69, bf16[4,4,64,2048]{3,2,1,0:T(8,128)(2,1)} %bitcast.67), custom_call_target="tpu_custom_call" | custom-call | tf_op jit(solution)/shard_map/scatter_all/pallas_call | solution.py:306
  1280.7 0.8 slice.93
  1281.7 0.7 copy.65
  1282.3 2.3 slice.104
  1284.6 1.3 fusion.36
  1285.9 1.3 fusion.37
  1287.3 1.7 fusion.33
  1289.0 2.8 fusion.16
  1291.8 2.1 convert_element_type.197
  (167 shorter events, 10.2 us)
Async XLA Ops:
  8.0 3.4 copy-start.38
  8.0 3.4 copy-start.39
  8.0 3.3 copy-start.31
  8.0 4.2 copy-start.52
  8.1 4.2 copy-start.54
  8.1 4.2 copy-start.53
  8.1 4.2 copy-start.51
  8.1 549.4 %all-gather.2.cloned.1.call-start = ((), (), s32[]{:S(2)}) async-start(), calls=%async_computation.3 | async-start | bytes 17301504 | tf_op jit(solution)/shard_map/all_gather | solution.py:818
  11.4 169.1 %copy-start.46 = (s32[256,8]{0,1:T(8,128)S(1)}, s32[256,8]{0,1:T(8,128)}, u32[]{:S(2)}) copy-start(s32[256,8]{0,1:T(8,128)} %param.28) | copy-start | bytes 24580
  180.2 749.1 %reduce-scatter.4.cloned.1.call-start = ((), (), s32[]{:S(2)}) async-start(), calls=%async_computation.4 | async-start | bytes 37748736 | tf_op jit(solution)/shard_map/reduce_scatter | solution.py:852
  182.2 35.3 %copy-start.4 = (f32[1,128]{1,0:T(1,128)}, f32[1,128]{1,0:T(1,128)S(1)}, u32[]{:S(2)}) copy-start(f32[1,128]{1,0:T(1,128)S(1)} %reshape.248.gq_ref) | copy-start | bytes 1540
  182.7 72.9 %copy-start.36 = (f32[2048]{0:T(1024)}, f32[2048]{0:T(1024)S(1)}, u32[]{:S(2)}) copy-start(f32[2048]{0:T(1024)S(1)} %reshape.250) | copy-start | bytes 24580
  182.8 22.2 %copy-start.32 = (f32[2048]{0:T(1024)}, f32[2048]{0:T(1024)S(1)}, u32[]{:S(2)}) copy-start(f32[2048]{0:T(1024)S(1)} %reshape.246) | copy-start | bytes 24580
  183.2 73.4 %copy-start.22 = (bf16[2048,32]{1,0:T(8,128)(2,1)}, bf16[2048,32]{1,0:T(8,128)(2,1)S(1)}, u32[]{:S(2)}) copy-start(bf16[2048,32]{1,0:T(8,128)(2,1)S(1)} %reshape_reshape.31) | copy-start | bytes 393220
  183.2 3.6 copy-start.20
  201.7 2.3 copy-start.49
  201.7 2.3 copy-start.14
  204.1 13.4 %copy-start = (f32[1024,128]{1,0:T(8,128)}, f32[1024,128]{1,0:T(8,128)S(1)}, u32[]{:S(2)}) copy-start(f32[1024,128]{1,0:T(8,128)S(1)} %get-tuple-element.174.cos_ref) | copy-start | bytes 1572868
  204.1 13.4 %copy-start.2 = (f32[1024,128]{1,0:T(8,128)}, f32[1024,128]{1,0:T(8,128)S(1)}, u32[]{:S(2)}) copy-start(f32[1024,128]{1,0:T(8,128)S(1)} %get-tuple-element.175.sin_ref) | copy-start | bytes 1572868
  205.0 12.5 copy-start.40
  244.1 10.9 copy-start.6
  244.1 10.9 copy-start.7
  244.1 10.9 copy-start.9
  256.6 3.3 copy-start.18
  257.1 2.8 copy-start.44
  557.4 524.2 %reduce-scatter.6.cloned.1.call-start = ((), (), s32[]{:S(2)}) async-start(), calls=%async_computation.5 | async-start | bytes 18874368 | tf_op jit(solution)/shard_map/reduce_scatter | solution.py:873
  685.6 244.8 %copy-start.27 = (f32[256,32]{1,0:T(8,128)S(1)}, f32[256,32]{1,0:T(8,128)}, u32[]{:S(2)}) copy-start(f32[256,32]{1,0:T(8,128)} %copy-done.26) | copy-start | bytes 98308
  685.6 244.8 %copy-start.45 = (f32[256]{0:T(256)S(1)}, f32[256]{0:T(256)}, u32[]{:S(2)}) copy-start(f32[256]{0:T(256)} %copy-done.44) | copy-start | bytes 3076
  685.6 246.0 %copy-start.23 = (bf16[2048,32]{1,0:T(8,128)(2,1)S(1)}, bf16[2048,32]{1,0:T(8,128)(2,1)}, u32[]{:S(2)}) copy-start(bf16[2048,32]{1,0:T(8,128)(2,1)} %copy-done.22) | copy-start | bytes 393220
  685.6 246.0 %copy-start.37 = (f32[2048]{0:T(1024)S(1)}, f32[2048]{0:T(1024)}, u32[]{:S(2)}) copy-start(f32[2048]{0:T(1024)} %copy-done.36) | copy-start | bytes 24580
  685.6 246.0 %copy-start.43 = (f32[256]{0:T(256)S(1)}, f32[256]{0:T(256)}, u32[]{:S(2)}) copy-start(f32[256]{0:T(256)} %copy-done.42) | copy-start | bytes 3076
  931.7 3.2 copy-start.12
  931.7 3.2 copy-start.24
  931.7 3.2 copy-start.48
  935.5 18.8 %copy-start.16 = (f32[256,2048]{1,0:T(8,128)}, f32[256,2048]{1,0:T(8,128)S(1)}, u32[]{:S(2)}) copy-start(f32[256,2048]{1,0:T(8,128)S(1)} %subtract_add_fusion) | copy-start | bytes 6291460
  964.2 2.9 copy-start.50
  964.2 3.9 copy-start.1
  964.2 3.9 copy-start.3
  964.2 3.9 copy-start.5
  964.2 3.9 copy-start.8
  964.2 3.9 copy-start.10
  964.3 327.5 %reduce-scatter.8.cloned.1.call-start = ((), (), s32[]{:S(2)}) async-start(), calls=%async_computation.6 | async-start | bytes 2621440 | tf_op jit(solution)/shard_map/reduce_scatter | solution.py:899
  1006.7 33.3 %copy-start.19 = (bf16[256,2048]{1,0:T(8,128)(2,1)S(1)}, bf16[256,2048]{1,0:T(8,128)(2,1)}, u32[]{:S(2)}) copy-start(bf16[256,2048]{1,0:T(8,128)(2,1)} %copy-done.18) | copy-start | bytes 3145732
  1039.9 2.9 copy-start.30
  1056.2 25.5 %copy-start.25 = (bf16[256,4096]{1,0:T(8,128)(2,1)S(1)}, bf16[256,4096]{1,0:T(8,128)(2,1)}, u32[]{:S(2)}) copy-start(bf16[256,4096]{1,0:T(8,128)(2,1)} %get-tuple-element.64) | copy-start | bytes 6291460
  1093.8 5.3 copy-start.17
  1093.8 5.3 copy-start.47
  1280.7 8.2 copy-start.13
  (11 other events, 13.9 us)
Sparse Core Ops, SparseCore 0:
  180.3 144.2 all-gather.1
  1081.8 58.6 reduce-scatter.7
Sparse Core Ops, SparseCore 1:
  557.5 259.4 reduce-scatter.3
  964.3 117.2 reduce-scatter.5

commit v6 on v5

--- a/solution.py
+++ b/solution.py
@@ -365,9 +365,15 @@
         name="line_gather")(x.reshape(parts, R // parts, C))
     return o.reshape(NZ * R, C)
 
-def line_scatter_kernel(parts, p_ref, o_ref, acc, zu, zd, ss_u, rs_u, ss_d, rs_d):
+def line_scatter_kernel(parts, p_ref, o_ref, *scratch):
+    for run in line_scatter_steps(parts, p_ref, o_ref, scratch): run()
+
+LINE_PARTS = 4
+LINE_STEPS = 3 * LINE_PARTS + NZ + 1
+
+def line_scatter_steps(parts, p_ref, o_ref, scratch):
+    acc, zu, zd, ss_u, rs_u, ss_d, rs_d = scratch
     y, x, c, s = place()
-    line_barrier(y, x, c, s)
     def rc(src, dst, a, b, d):
         return pltpu.make_async_remote_copy(src_ref=src, dst_ref=dst, send_sem=a, recv_sem=b, device_id=d, device_id_type=MESH)
     def cu(zz, h, k):
@@ -387,7 +393,8 @@
     ups = [(zz, h) for zz in (3, 2, 1) for h in range(parts)]
     dns = [(zz, h) for zz in (0, 1, 2) for h in range(parts)]
     n = len(ups)
-    for i in range(n + NZ):
+    def advance(i):
+        if i == 0: line_barrier(y, x, c, s)
         for k in range(NZ - 1):
             if 0 <= i - k < n:
                 zz, h = ups[i - k]
@@ -406,35 +413,40 @@
                             cd(zz, h, k).wait_recv()
                             total(acc.at[zz, h], [p_ref.at[zz, h], zd.at[zz, h]])
                         cd(zz, h, k).start()
-    for zz in range(NZ):
-        @pl.when(s == zz)
-        def _():
-            for h in range(parts):
-                refs = [p_ref.at[zz, h]]
-                if zz > 0:
-                    cu(zz, h, 1).wait_recv()
-                    refs.append(zu.at[zz, h])
-                if zz < NZ - 1:
-                    cd(zz, h, 1).wait_recv()
-                    refs.append(zd.at[zz, h])
-                total(o_ref.at[h], refs)
-    for zz, h in ups:
-        @pl.when(s < zz)
-        def _(): cu(zz, h, 1).wait_send()
-    for zz, h in dns:
-        @pl.when(s > zz)
-        def _(): cd(zz, h, 1).wait_send()
-
-def line_scatter(p, cid, parts=4):
+    def finish():
+        for zz in range(NZ):
+            @pl.when(s == zz)
+            def _():
+                for h in range(parts):
+                    refs = [p_ref.at[zz, h]]
+                    if zz > 0:
+                        cu(zz, h, 1).wait_recv()
+                        refs.append(zu.at[zz, h])
+                    if zz < NZ - 1:
+                        cd(zz, h, 1).wait_recv()
+                        refs.append(zd.at[zz, h])
+                    total(o_ref.at[h], refs)
+        for zz, h in ups:
+            @pl.when(s < zz)
+            def _(): cu(zz, h, 1).wait_send()
+        for zz, h in dns:
+            @pl.when(s > zz)
+            def _(): cd(zz, h, 1).wait_send()
+    return [functools.partial(advance, i) for i in range(n + NZ)] + [finish]
+
+def line_scatter_scratch(parts, rows, cols, dtype):
+    sem = pltpu.SemaphoreType.DMA((NZ, parts))
+    buf = pltpu.VMEM((NZ, parts, rows // parts, cols), dtype)
+    return [buf, buf, buf, sem, sem, sem, sem]
+
+def line_scatter(p, cid, parts=LINE_PARTS):
     if not placed():
         return lax.psum_scatter(p, "shard", scatter_dimension=0, tiled=True).astype(jnp.float32)
     R, C = p.shape[0] // NZ, p.shape[1]
-    sem = pltpu.SemaphoreType.DMA((NZ, parts))
     shape = (NZ, parts, R // parts, C)
-    buf = pltpu.VMEM(shape, p.dtype)
     o = pl.pallas_call(functools.partial(line_scatter_kernel, parts), out_shape=jax.ShapeDtypeStruct(shape[1:], jnp.float32),
         in_specs=[pl.BlockSpec(memory_space=pltpu.VMEM)], out_specs=pl.BlockSpec(memory_space=pltpu.VMEM),
-        scratch_shapes=[buf, buf, buf, sem, sem, sem, sem], compiler_params=pltpu.CompilerParams(collective_id=cid, has_side_effects=True, vmem_limit_bytes=24 << 20),
+        scratch_shapes=line_scatter_scratch(parts, R, C, p.dtype), compiler_params=pltpu.CompilerParams(collective_id=cid, has_side_effects=True, vmem_limit_bytes=24 << 20),
         name="line_scatter")(p.reshape(shape))
     return o.reshape(R, C)
 
@@ -504,7 +516,7 @@
     nsub = meta_ref.shape[0] // SB
     D = cota_ref.shape[1]
     WM = meta_ref.shape[1]
-    half = block // 2
+    na, nb = [r.shape[0] * block // meta_ref.shape[0] for r in (cota_ref, cotb_ref)]
     me = lax.axis_index(("expert", "shard"))
     loads = [pltpu.make_async_copy(h.at[0], v, wsem.at[i]) for i, (h, v) in enumerate(((wg_hbm, wg), (wu_hbm, wu), (wd_hbm, wd)))]
     @pl.when(step == 0)
@@ -518,7 +530,7 @@
         picks.append(pick)
         cot = []
         for b in range(i * SB // block, (i + 1) * SB // block):
-            cot += [cota_ref[b * half:(b + 1) * half, :], cotb_ref[b * half:(b + 1) * half, :]]
+            cot += [cota_ref[b * na:(b + 1) * na, :], cotb_ref[b * nb:(b + 1) * nb, :]]
         gcot = (gate * jnp.concatenate(cot, axis=0).astype(jnp.float32)).astype(bf)
         gp[i * slots:(i + 1) * slots, :] = dot(pick, gcot, 0, 0).astype(bf)
     @pl.when(step == 0)
@@ -591,7 +603,7 @@
         functools.partial(backward_kernel, experts, slots, SB, block),
         grid=(T // TB,),
         out_shape=[jax.ShapeDtypeStruct((T, C), bf), jax.ShapeDtypeStruct(w_gate.shape, f32), jax.ShapeDtypeStruct(w_up.shape, f32), jax.ShapeDtypeStruct(w_down.shape, f32)],
-        in_specs=[meta, blk(TB // 2, D), blk(TB // 2, D), blk(total, D), blk(total, F), blk(total, F), any_, any_, any_],
+        in_specs=[meta, blk(cot_a.shape[0] * TB // T, D), blk(cot_b.shape[0] * TB // T, D), blk(total, D), blk(total, F), blk(total, F), any_, any_, any_],
         out_specs=[blk(TB, C), any_, any_, any_],
         scratch_shapes=[V((D, F), bf), V((D, F), bf), V((F, D), bf), V((D, F), f32), V((D, F), f32), V((F, D), f32), V((total, D), bf), pltpu.SemaphoreType.DMA((3,)), pltpu.SemaphoreType.DMA((3,))],
         compiler_params=pltpu.CompilerParams(dimension_semantics=("arbitrary",), vmem_limit_bytes=65000 * 1024),
@@ -648,16 +660,28 @@
         name="attention_forward",
     )(q_proj, kv_proj, kv_proj, gq, gk, cos, sin)
 
-def attention_backward_kernel(group, u_ref, ql_ref, kl_ref, vl_ref, gm_ref, gq_ref, cos_ref, sin_ref, gu_ref, gk_ref, gv_ref, gg_ref, gk_acc, gv_acc):
+def attention_backward_kernel(group, guest, *refs):
+    if guest:
+        p_ref, u_ref, ql_ref, kl_ref, vl_ref, ga_ref, wo_ref, gq_ref, cos_ref, sin_ref, po_ref, gu_ref, gk_ref, gv_ref, gg_ref, gk_acc, gv_acc = refs[:17]
+        runs = line_scatter_steps(LINE_PARTS, p_ref, po_ref, refs[17:])
+        slots = HK * group
+        at = {i * slots // (LINE_STEPS - 1): run for i, run in enumerate(runs[:-1])}
+    else:
+        u_ref, ql_ref, kl_ref, vl_ref, ga_ref, wo_ref, gq_ref, cos_ref, sin_ref, gu_ref, gk_ref, gv_ref, gg_ref, gk_acc, gv_acc = refs
+        at = {}
+    step = pl.program_id(0)
     bf, f32 = jnp.bfloat16, jnp.float32
+    gm_all = dot(ga_ref[...], wo_ref[...], 1, 1).astype(bf)
     rows, seq = ql_ref.shape[0], kl_ref.shape[0]
     first = lax.axis_index("shard") * rows
     cos, sin = cos_ref[pl.ds(first, rows), :], sin_ref[pl.ds(first, rows), :]
     allowed = lax.broadcasted_iota(jnp.int32, (rows, seq), 1) <= first + lax.broadcasted_iota(jnp.int32, (rows, seq), 0)
     gain_grad = jnp.zeros((1, HD), f32)
     for j in range(group):
+        for i in range(HK):
+            if i * group + j in at: pl.when(step == i)(at[i * group + j])
         cols = slice(j * HD, (j + 1) * HD)
-        ql, gm = ql_ref[:, cols], gm_ref[:, cols]
+        ql, gm = ql_ref[:, cols], gm_all[:, cols]
         raised = jnp.where(allowed, jnp.exp(dot(ql, kl_ref[...], 1, 1)), 0.0)
         probs = raised * (1.0 / jnp.sum(raised, axis=-1, keepdims=True))
         gp = dot(gm, vl_ref[...], 1, 1)
@@ -680,26 +704,34 @@
     gk_ref[...] = gk_acc[...].astype(bf)
     gv_ref[...] = gv_acc[...].astype(bf)
     gg_ref[0] = jnp.broadcast_to(gain_grad, (8, HD))
-
-def attention_backward(q_proj, q_low, k_low, v_low, grad_mix, gq, cos, sin):
+    if guest: pl.when(step == HK - 1)(runs[-1])
+
+def attention_backward(q_proj, q_low, k_low, v_low, grad_attn, w_out, gq, cos, sin, guest, cid):
     rows, seq = q_low.shape[0], k_low.shape[0]
     group = HQ // HK
     bf, f32 = jnp.bfloat16, jnp.float32
     gq = gq[None, :]
     whole = lambda a: pl.BlockSpec(a.shape, lambda i: (0, 0))
     qb = pl.BlockSpec((rows, group * HD), lambda i: (0, i)); kb = pl.BlockSpec((seq, HD), lambda i: (0, i))
-    grad_q, grad_k, grad_v, gain = pl.pallas_call(
-        functools.partial(attention_backward_kernel, group),
+    hosted = placed()
+    R, C = guest.shape[0] // lax.axis_size("shard"), guest.shape[1]
+    shape = (NZ, LINE_PARTS, R // LINE_PARTS, C)
+    vm = pl.BlockSpec(memory_space=pltpu.VMEM)
+    *summed, grad_q, grad_k, grad_v, gain = pl.pallas_call(
+        functools.partial(attention_backward_kernel, group, hosted),
         grid=(HK,),
-        out_shape=[jax.ShapeDtypeStruct(q_low.shape, bf), jax.ShapeDtypeStruct(k_low.shape, bf), jax.ShapeDtypeStruct(k_low.shape, bf), jax.ShapeDtypeStruct((HK, 8, HD), f32)],
-        in_specs=[qb, qb, kb, kb, qb, whole(gq), whole(cos), whole(sin)],
-        out_specs=[qb, kb, kb, pl.BlockSpec((1, 8, HD), lambda i: (i, 0, 0))],
-        scratch_shapes=[pltpu.VMEM((seq, HD), f32), pltpu.VMEM((seq, HD), f32)],
-        compiler_params=pltpu.CompilerParams(dimension_semantics=("arbitrary",), vmem_limit_bytes=48 << 20),
-        cost_estimate=pl.CostEstimate(flops=10_700_000_000, bytes_accessed=20_000_000, transcendentals=8_400_000),
+        out_shape=([jax.ShapeDtypeStruct(shape[1:], f32)] if hosted else []) + [jax.ShapeDtypeStruct(q_low.shape, bf), jax.ShapeDtypeStruct(k_low.shape, bf), jax.ShapeDtypeStruct(k_low.shape, bf), jax.ShapeDtypeStruct((HK, 8, HD), f32)],
+        in_specs=([vm] if hosted else []) + [qb, qb, kb, kb, whole(grad_attn), pl.BlockSpec((group * HD, w_out.shape[1]), lambda i: (i, 0)), whole(gq), whole(cos), whole(sin)],
+        out_specs=([vm] if hosted else []) + [qb, kb, kb, pl.BlockSpec((1, 8, HD), lambda i: (i, 0, 0))],
+        scratch_shapes=[pltpu.VMEM((seq, HD), f32), pltpu.VMEM((seq, HD), f32)] + (line_scatter_scratch(LINE_PARTS, R, C, bf) if hosted else []),
+        compiler_params=pltpu.CompilerParams(dimension_semantics=("arbitrary",), vmem_limit_bytes=60 << 20,
+            **(dict(collective_id=cid, has_side_effects=True) if hosted else {})),
+        cost_estimate=pl.CostEstimate(flops=15_000_000_000, bytes_accessed=20_000_000, transcendentals=8_400_000),
         name="attention_backward",
-    )(q_proj, q_low, k_low, v_low, grad_mix, gq, cos, sin)
-    return grad_q, jnp.concatenate([grad_k, grad_v], axis=1), jnp.sum(gain[:, 0], axis=0)
+    )(*([guest.reshape(shape)] if hosted else []), q_proj, q_low, k_low, v_low, grad_attn, w_out, gq, cos, sin)
+    if hosted: total = summed[0].reshape(R, C)
+    else: total = lax.psum_scatter(guest, "shard", scatter_dimension=0, tiled=True).astype(f32)
+    return total, grad_q, jnp.concatenate([grad_k, grad_v], axis=1), jnp.sum(gain[:, 0], axis=0)
 
 HQ = 32
 HK = 4
@@ -813,8 +845,8 @@
     wr_full, attn_gain, ffn_gain, query_gain, key_gain = [small_all[:, o : o + n].reshape(-1) for o, n in zip(starts, sizes)]
     wr_full = wr_full.reshape(model_width, expert_count)
     attn_gain, ffn_gain, query_gain, key_gain = [g.astype(f32) for g in (attn_gain, ffn_gain, query_gain, key_gain)]
-    half = tok_rows // 2
-    cot_first, wo_full = lax.optimization_barrier((cotangent[:half], wo_full))
+    first = 3 * tok_rows // 8
+    cot_first, wo_full = lax.optimization_barrier((cotangent[:first], wo_full))
     cot_a = lax.all_gather(cot_first, BOTH, axis=0, tiled=True)
 
     inputs_f = hidden_in.astype(f32)
@@ -847,7 +879,7 @@
     )
     (payload_all,) = gather_all([payload], 3)
     (out_part, rows, gate_act, up_act), cot_b = experts_forward(
-        payload_all, w_gate, w_up, w_down, expert_count, tok_rows, capacity, cotangent[half:], 2
+        payload_all, w_gate, w_up, w_down, expert_count, tok_rows, capacity, cotangent[first:], 2
     )
     moe_out = lax.psum_scatter(out_part, "expert", scatter_dimension=0, tiled=True)
     grad_part, grad_wgate, grad_wup, grad_wdown = experts_backward(
@@ -868,12 +900,13 @@
     grad_residual = upstream + grad_second
     grad_attn_low = grad_residual.astype(bf)
     grad_wout = matmul_tn(mix_low, grad_attn_low).astype(bf)
-    grad_mix = matmul_nt(grad_attn_low, wo_full).astype(bf)
-    grad_mix, grad_wout = lax.optimization_barrier((grad_mix, grad_wout))
+    grad_attn_low, grad_wout = lax.optimization_barrier((grad_attn_low, grad_wout))
     out_grad = lax.psum_scatter(grad_wout, "expert", scatter_dimension=0, tiled=True)
 
-    grad_q_low, grad_kv, grad_query_gain = attention_backward(
-        q_proj, q_low, k_low, v_low, grad_mix, query_gain, cosine, sine
+    moe_parts = moe_out.reshape(shard_count, 2, tok_rows // 2, model_width)
+    moe_a, moe_b = [moe_parts[:, i].reshape(-1, model_width) for i in range(2)]
+    moe_a, grad_q_low, grad_kv, grad_query_gain = attention_backward(
+        q_proj, q_low, k_low, v_low, grad_attn_low, wo_full, query_gain, cosine, sine, moe_a, 5
     )
     grad_kv = line_scatter(grad_kv, 6)
     own_rows = shard_pos * tok_rows
@@ -897,8 +930,8 @@
     ).reshape(devices * small_rows, 128)
     grad_wqkv, out_grad = lax.optimization_barrier((grad_wqkv, out_grad))
     out_grad = lax.psum_scatter(out_grad, "shard", scatter_dimension=0, tiled=True).astype(f32)
-    qkv_grad, small_grad, moe_out = scatter_all([grad_wqkv, packed], 8, line=[moe_out])
-    block_out = (residual + moe_out).astype(bf)
+    qkv_grad, small_grad, moe_b = scatter_all([grad_wqkv, packed], 8, line=[moe_b])
+    block_out = (residual + jnp.concatenate([moe_a, moe_b], axis=0)).astype(bf)
     small_grad = small_grad.reshape(-1)
     router_g, attn_g, ffn_g, query_g, key_g = [small_grad[o : o + n] for o, n in zip(starts, sizes)]
     return (

time: 1310 us -> 1260 us (0.962)
  waiting for transfers between devices: 25.6 us -> 0.12 us
  matrix products: 88.4 us -> 67.3 us
    pallas_call x2, Pallas kernels: 422 us -> 390 us  [rs32(): pl.pallas_call(functools.partial(rs_kernel, n, nl, parts), out_shape=[jax...]
    reduce_scatter x1, waiting for transfers between devices: 25.5 us -> 0.01 us  [per_device(): lax.psum_scatter(grad_wout, 'expert', scatter_dimension=0, tiled=True)]
    pallas_call x1, Pallas kernels: 38.2 us -> 61.8 us  [attention_backward(): pl.pallas_call(functools.partial(attention_backward_kernel, group, hosted...]
    pallas_call x1, Pallas kernels: 117 us -> 138 us  [experts_forward(): pl.pallas_call(functools.partial(forward_kernel, experts, slots, SB, host...]
    dot_general x3 -> x2, matrix products: 34 us -> 14.9 us  [matmul_nt(): lax.dot_general(left, right, (((1,), (1,)), ((), ())), preferred_element_...]
    pallas_call x2, Pallas kernels: 347 us -> 331 us  [ag32(): pl.pallas_call(functools.partial(ag_kernel, n, m), out_shape=[jax.ShapeDt...]
  transfers between devices with their start and end apart: 4 -> 4, of which waited for: 1 -> 0; matrix products, arithmetic and copies ran while one was open for 8% -> 8% of each run, Pallas kernels for 73% -> 75%
where the time goes in v6:
time: 1260 us; the launch traced here: 1250 us
  Pallas kernels  1100 us (87%)
  matrix products  67.3 us (5%)
  local copies, waits for them, and re-layouts  38.2 us (3%)
  other arithmetic  28 us (2%)
  between operations  16.5 us (1%)
    pallas_call x2, Pallas kernels, rs32(): pl.pallas_call(functools.partial(rs_kernel, n, nl, parts), out_shape=[jax...  390 us
    pallas_call x2, Pallas kernels, ag32(): pl.pallas_call(functools.partial(ag_kernel, n, m), out_shape=[jax.ShapeDt...  331 us
    pallas_call x1, Pallas kernels, experts_forward(): pl.pallas_call(functools.partial(forward_kernel, experts, slots, SB, host...  138 us
    pallas_call x1, Pallas kernels, experts_backward(): pl.pallas_call(functools.partial(backward_kernel, experts, slots, SB, blo...  128 us
    pallas_call x1, Pallas kernels, attention_backward(): pl.pallas_call(functools.partial(attention_backward_kernel, group, hosted...  61.8 us
    dot_general x4, matrix products, matmul(): return jnp.dot(left, right, preferred_element_type=jnp.float32)  31.9 us
    pallas_call x1, Pallas kernels, line_scatter(): pl.pallas_call(functools.partial(line_scatter_kernel, parts), out_shape=j...  27.9 us
    pallas_call x1, Pallas kernels, attention_forward(): pl.pallas_call(functools.partial(attention_forward_kernel, group), grid=(...  26.5 us
  transfers between devices with their start and end apart: 4, of which 0 were waited for; matrix products, arithmetic and copies ran while one was open for 8% of the time, Pallas kernels for 75%

profile of v6, /device:TPU:18, one launch (start us, length us, event | category | flops | bytes accessed | tf_op | source)
XLA Modules:
  0.0 1253.4 jit_solution(14032707994300161739)
XLA Ops:
  8.1 0.8 copy.61
  9.0 1.8 slice.82
  10.8 2.1 pad_maximum_fusion.4
  12.9 0.7 concatenate.34
  13.6 167.2 %gather_all.2 = (bf16[2,2,2,4,2,32,5120]{6,5,4,3,2,1,0:T(8,128)(2,1)}, bf16[2,2,2,4,2,32,128]{6,5,4,3,2,1,0:T(8,128)(2,1)}, bf16[2,2,2,4,2,64,2048]{6,5,4,3,2,1,0:T(8,128)(2,1)}, bf16[4,2,128,2048]{3,2,1,0:T(8,128)(2,1)}) custom-call(bf16[2,32,5120]{2,1,0:T(8,128)(2,1)} %bitcast.73, bf16[2,32,128]{2,1,0:T(8,128)(2,1)} %bitcast.84, ...), custom_call_target="tpu_custom_call" | custom-call | tf_op jit(solution)/shard_map/gather_all/pallas_call | solution.py:164
  181.2 0.9 slice.85
  183.6 3.3 multiply_reduce_fusion
  187.2 1.0 fusion.3
  188.3 8.4 fusion.4
  196.7 5.4 copy.62.k_ref.v_ref
  202.1 2.0 fusion.25
  205.4 12.4 fusion.q_ref.refs_1_
  217.9 26.5 %attention_forward.1 = (bf16[256,4096]{1,0:T(8,128)(2,1)S(1)}, bf16[1024,512]{1,0:T(8,128)(2,1)S(1)}, bf16[1024,512]{1,0:T(8,128)(2,1)S(1)}, bf16[256,4096]{1,0:T(8,128)(2,1)}) custom-call(f32[256,4096]{1,0:T(8,128)} %fusion.q_ref.refs_1_, f32[1024,1024]{1,0:T(8,128)} %copy.62.k_ref.v_ref, f32[1024,1024]{1,0:T(8,128)} %copy.62.k_ref.v_ref, ...), custom_call_target="tpu_custom_call" | custom-call | flops 4300000256 | bytes 20000000 | tf_op jit(solution)/shard_map/attention_forward/pallas_call | solution.py:652
  244.4 10.6 multiply_reduce_fusion.3
  257.8 2.0 concatenate.37
  259.8 163.8 %gather_all.3 = bf16[2,2,2,4,2,128,2176]{6,5,4,3,2,1,0:T(8,128)(2,1)} custom-call(bf16[2,128,2176]{2,1,0:T(8,128)(2,1)} %bitcast.71), custom_call_target="tpu_custom_call" | custom-call | tf_op jit(solution)/shard_map/gather_all/pallas_call | solution.py:164
  423.6 137.6 %experts_forward.1 = (bf16[2,2,2,4,2,80,2048]{6,5,4,3,2,1,0:T(8,128)(2,1)}, bf16[8192,2048]{1,0:T(8,128)(2,1)}, bf16[4096,2048]{1,0:T(8,128)(2,1)}, f32[4096,768]{1,0:T(8,128)}, f32[4096,768]{1,0:T(8,128)}) custom-call(bf16[2,80,2048]{2,1,0:T(8,128)(2,1)} %bitcast.82, bf16[8192,2176]{1,0:T(8,128)(2,1)} %bitcast.61, bf16[1,2048,768]{2,1,0:T(8,128)(2,1)} %wg_hbm.1, ...), custom_call_target="tpu_custom_call" | custom-call | flops 48000000000 | bytes 130000000 | tf_op jit(solution)/shard_map/experts_forward/pallas_call | solution.py:577
  561.3 128.1 %experts_backward.1 = (bf16[8192,2176]{1,0:T(8,128)(2,1)}, f32[1,2048,768]{2,1,0:T(8,128)}, f32[1,2048,768]{2,1,0:T(8,128)}, f32[1,768,2048]{2,1,0:T(8,128)}) custom-call(bf16[8192,2176]{1,0:T(8,128)(2,1)} %bitcast.62, bf16[3072,2048]{1,0:T(8,128)(2,1)} %all-gather.2.cloned.1.call-done.cota_ref, bf16[5120,2048]{1,0:T(8,128)(2,1)} %bitcast.93, ...), custom_call_target="tpu_custom_call" | custom-call | flops 85000003584 | bytes 150000000 | tf_op jit(solution)/shard_map/experts_backward/pallas_call | solution.py:602
  689.5 242.8 %scatter_all.2 = f32[4,64,2176]{2,1,0:T(8,128)} custom-call(bf16[2,2,2,4,4,64,2176]{6,5,4,3,2,1,0:T(8,128)(2,1)} %bitcast.63), custom_call_target="tpu_custom_call" | custom-call | tf_op jit(solution)/shard_map/scatter_all/pallas_call | solution.py:306
  932.3 1.2 fusion.27
  933.5 1.1 subtract_convert_fusion
  934.7 3.1 multiply_reduce_fusion.1
  937.9 2.0 fusion.31
  939.9 8.2 convolution_convert_fusion.1
  948.8 1.1 multiply_reduce_fusion.6
  950.3 4.9 fusion.32
  955.2 61.8 %attention_backward.1 = (f32[4,32,2048]{2,1,0:T(8,128)}, bf16[256,4096]{1,0:T(8,128)(2,1)}, bf16[1024,512]{1,0:T(8,128)(2,1)}, bf16[1024,512]{1,0:T(8,128)(2,1)}, f32[4,8,128]{2,1,0:T(8,128)}) custom-call(bf16[4,4,32,2048]{3,2,1,0:T(8,128)(2,1)} %bitcast.76, f32[256,4096]{1,0:T(8,128)} %fusion.q_ref.refs_1_, bf16[256,4096]{1,0:T(8,128)(2,1)} %copy-done.3, ...), custom_call_target="tpu_custom_call" | custom-call | flops 15000000512 | bytes 20000000 | tf_op jit(solution)/shard_map/attention_backward/pallas_call | solution.py:720
  1017.0 1.8 pad_maximum_fusion.1
  1018.9 27.9 %line_scatter.1 = f32[4,64,1024]{2,1,0:T(8,128)S(1)} custom-call(bf16[4,4,64,1024]{3,2,1,0:T(8,128)(2,1)S(1)} %bitcast.57), custom_call_target="tpu_custom_call" | custom-call | tf_op jit(solution)/shard_map/line_scatter/pallas_call | solution.py:447
  1047.5 1.2 reshape.250
  1048.7 0.7 slice_reduce_fusion
  1049.4 0.7 convert_element_type.188
  1051.0 0.7 convert_element_type.190
  1051.8 12.1 convolution_convert_fusion
  1063.9 1.6 copy-done.21
  1065.4 11.8 fusion.15
  1077.9 2.0 concatenate.42
  1079.9 2.0 copy.79
  1082.5 3.2 fusion.14
  1085.7 147.2 %scatter_all.3 = (f32[4,16,5120]{2,1,0:T(8,128)}, f32[4,16,128]{2,1,0:T(8,128)}, f32[4,32,2048]{2,1,0:T(8,128)}) custom-call(bf16[2,2,2,4,4,16,5120]{6,5,4,3,2,1,0:T(8,128)(2,1)} %bitcast.60, bf16[2,2,2,4,4,16,128]{6,5,4,3,2,1,0:T(8,128)(2,1)} %bitcast.74, bf16[4,4,32,2048]{3,2,1,0:T(8,128)(2,1)} %bitcast.69), custom_call_target="tpu_custom_call" | custom-call | tf_op jit(solution)/shard_map/scatter_all/pallas_call | solution.py:306
  1233.0 0.8 slice.101
  1233.9 0.7 copy.73
  1234.6 2.3 slice.114
  1236.8 1.3 fusion.35
  1238.2 1.3 fusion.36
  1239.5 1.7 fusion.33
  1241.2 2.4 fusion.16
  1243.6 2.1 convert_element_type.193
  (154 shorter events, 10.8 us)
Async XLA Ops:
  8.0 4.8 copy-start.45
  8.0 4.8 copy-start.47
  8.0 4.8 copy-start.46
  8.0 4.8 copy-start.44
  8.1 553.3 %all-gather.2.cloned.1.call-start = ((), (), s32[]{:S(2)}) async-start(), calls=%async_computation.3 | async-start | bytes 12976128 | tf_op jit(solution)/shard_map/all_gather | solution.py:850
  10.8 170.2 %copy-start.39 = (s32[256,8]{0,1:T(8,128)S(1)}, s32[256,8]{0,1:T(8,128)}, u32[]{:S(2)}) copy-start(s32[256,8]{0,1:T(8,128)} %param.28) | copy-start | bytes 24580
  10.8 170.4 %copy-start.18 = (bf16[256,2048]{1,0:T(8,128)(2,1)S(1)}, bf16[256,2048]{1,0:T(8,128)(2,1)}, u32[]{:S(2)}) copy-start(bf16[256,2048]{1,0:T(8,128)(2,1)} %param.29) | copy-start | bytes 3145732
  180.7 1.5 copy-start.26
  180.8 751.5 %reduce-scatter.4.cloned.1.call-start = ((), (), s32[]{:S(2)}) async-start(), calls=%async_computation.4 | async-start | bytes 37748736 | tf_op jit(solution)/shard_map/reduce_scatter | solution.py:884
  182.6 35.2 %copy-start.2 = (f32[1,128]{1,0:T(1,128)}, f32[1,128]{1,0:T(1,128)S(1)}, u32[]{:S(2)}) copy-start(f32[1,128]{1,0:T(1,128)S(1)} %reshape.256.gq_ref.refs_7_) | copy-start | bytes 1540
  183.1 72.5 %copy-start.31 = (f32[2048]{0:T(1024)}, f32[2048]{0:T(1024)S(1)}, u32[]{:S(2)}) copy-start(f32[2048]{0:T(1024)S(1)} %reshape.258) | copy-start | bytes 24580
  183.2 22.2 %copy-start.27 = (f32[2048]{0:T(1024)}, f32[2048]{0:T(1024)S(1)}, u32[]{:S(2)}) copy-start(f32[2048]{0:T(1024)S(1)} %reshape.254) | copy-start | bytes 24580
  183.6 72.9 %copy-start.15 = (bf16[2048,32]{1,0:T(8,128)(2,1)}, bf16[2048,32]{1,0:T(8,128)(2,1)S(1)}, u32[]{:S(2)}) copy-start(bf16[2048,32]{1,0:T(8,128)(2,1)S(1)} %reshape_reshape.28) | copy-start | bytes 393220
  183.6 3.6 copy-start.13
  202.1 2.3 copy-start.42
  202.1 2.3 copy-start.9
  204.5 13.4 %copy-start = (f32[1024,128]{1,0:T(8,128)}, f32[1024,128]{1,0:T(8,128)S(1)}, u32[]{:S(2)}) copy-start(f32[1024,128]{1,0:T(8,128)S(1)} %get-tuple-element.178.cos_ref.refs_8_) | copy-start | bytes 1572868
  204.5 13.4 %copy-start.1 = (f32[1024,128]{1,0:T(8,128)}, f32[1024,128]{1,0:T(8,128)S(1)}, u32[]{:S(2)}) copy-start(f32[1024,128]{1,0:T(8,128)S(1)} %get-tuple-element.179.sin_ref.refs_9_) | copy-start | bytes 1572868
  205.4 12.4 copy-start.33
  244.4 10.6 copy-start.3
  244.4 10.6 copy-start.4
  244.4 10.6 copy-start.5
  255.0 2.0 copy-start.6
  256.5 3.3 copy-start.11
  257.0 0.8 copy-start.37
  561.2 502.6 %reduce-scatter.6.cloned.1.call-start = ((), (), s32[]{:S(2)}) async-start(), calls=%async_computation.5 | async-start | bytes 18874368 | tf_op jit(solution)/shard_map/reduce_scatter | solution.py:904
  689.4 244.0 %copy-start.23 = (f32[256,32]{1,0:T(8,128)S(1)}, f32[256,32]{1,0:T(8,128)}, u32[]{:S(2)}) copy-start(f32[256,32]{1,0:T(8,128)} %copy-done.22) | copy-start | bytes 98308
  689.4 244.0 %copy-start.38 = (f32[256]{0:T(256)S(1)}, f32[256]{0:T(256)}, u32[]{:S(2)}) copy-start(f32[256]{0:T(256)} %copy-done.37) | copy-start | bytes 3076
  689.4 245.2 %copy-start.16 = (bf16[2048,32]{1,0:T(8,128)(2,1)S(1)}, bf16[2048,32]{1,0:T(8,128)(2,1)}, u32[]{:S(2)}) copy-start(bf16[2048,32]{1,0:T(8,128)(2,1)} %copy-done.15) | copy-start | bytes 393220
  689.4 245.2 %copy-start.32 = (f32[2048]{0:T(1024)S(1)}, f32[2048]{0:T(1024)}, u32[]{:S(2)}) copy-start(f32[2048]{0:T(1024)} %copy-done.31) | copy-start | bytes 24580
  689.5 245.2 %copy-start.36 = (f32[256]{0:T(256)S(1)}, f32[256]{0:T(256)}, u32[]{:S(2)}) copy-start(f32[256]{0:T(256)} %copy-done.35) | copy-start | bytes 3076
  934.6 3.2 copy-start.7
  934.7 3.2 copy-start.19
  934.7 3.2 copy-start.41
  937.9 2.0 copy-start.20
  939.9 8.2 copy-start.17
  948.0 1.9 copy-start.43
  948.0 295.6 %reduce-scatter.8.cloned.1.call-start = ((), (), s32[]{:S(2)}) async-start(), calls=%async_computation.6 | async-start | bytes 2621440 | tf_op jit(solution)/shard_map/reduce_scatter | solution.py:932
  1018.9 28.0 %copy-start.12 = (bf16[256,2048]{1,0:T(8,128)(2,1)S(1)}, bf16[256,2048]{1,0:T(8,128)(2,1)}, u32[]{:S(2)}) copy-start(bf16[256,2048]{1,0:T(8,128)(2,1)} %copy-done.11) | copy-start | bytes 3145732
  1050.5 1.3 copy-start.10
  1050.5 1.3 copy-start.28
  1050.5 1.3 copy-start.34
  1051.0 0.7 copy-start.24
  1063.8 1.6 copy-start.21
  1077.2 5.3 copy-start.14
  1077.2 5.3 copy-start.40
  1085.7 155.5 %copy-start.25 = (f32[4,32,2048]{2,1,0:T(8,128)S(1)}, f32[4,32,2048]{2,1,0:T(8,128)}, u32[]{:S(2)}) copy-start(f32[4,32,2048]{2,1,0:T(8,128)} %get-tuple-element.66) | copy-start | bytes 3145732
  1233.0 8.2 copy-start.8
  (4 other events, 2.6 us)
Sparse Core Ops, SparseCore 0:
  180.9 116.4 all-gather.1
  1064.0 63.6 reduce-scatter.7
Sparse Core Ops, SparseCore 1:
  561.3 258.7 reduce-scatter.3
  948.1 115.3 reduce-scatter.5

commit v7 on v6

--- a/solution.py
+++ b/solution.py
@@ -34,9 +34,7 @@
     n_all = n_arr + n_line
     for run in ag_steps(n_arr, n_line, refs[:n_all], refs[n_all:2 * n_all], refs[2 * n_all:]): run()
 
-AG_STEPS = 10
-
-def ag_steps(n_arr, n_line, ins, outs, sems):
+def ag_steps(n_arr, n_line, ins, outs, sems, stages=False):
     n_all = n_arr + n_line
     loc_sem, zs, zr, ps, pr, cs, cr = sems
     y, x, c, s = place()
@@ -124,11 +122,12 @@
                 core(a, zz, k, 0).start()
         when(k, go)
     n = len(steps)
+    def start():
+        barrier_all(y, x, c, s)
+        for a in every: loc(a).start()
+        stage_a(0)
     def advance(i):
-        if i == 0:
-            barrier_all(y, x, c, s)
-            for a in every: loc(a).start()
-        if i < n: stage_a(i)
+        if 0 < i < n: stage_a(i)
         if 0 <= i - 1 < n: stage_b(i - 1)
         if 0 <= i - 2 < n: stage_c(i - 2)
     def finish():
@@ -152,7 +151,8 @@
                             plane(a, h, zz, k, 1).wait_send()
                             diag(a, h, zz, k).wait_send()
             when(k, go)
-    return [functools.partial(advance, i) for i in range(n + 2)] + [finish]
+    if stages: return start, stage_a, stage_b, stage_c, finish
+    return [start] + [functools.partial(advance, i) for i in range(1, n + 2)] + [finish]
 
 def ag_sems(n, m=0):
     D = pltpu.SemaphoreType.DMA
@@ -476,9 +476,9 @@
     bf = jnp.bfloat16
     step = pl.program_id(0)
     if guest:
-        runs = ag_steps(1, 0, [cot_ref], [cot_all], refs[14:])
-        for i, run in enumerate(runs[:-1]):
-            pl.when(step == GUEST_AT[i])(run)
+        start, stage_a, stage_b, stage_c, finish = ag_steps(1, 0, [cot_ref], [cot_all], refs[14:], True)
+        pl.when(step == 0)(start)
+        for at, stage, k in GUEST_AT: pl.when(step == at)(functools.partial(stage_a if stage == 0 else stage_b if stage == 1 else stage_c, k))
     nsub = x_ref.shape[0] // SB
     D = out_ref.shape[1]
     me = lax.axis_index(("expert", "shard"))
@@ -505,9 +505,12 @@
         r = pl.ds(i * SB, SB)
         tok = dot(picks[i], eo[i * slots:(i + 1) * slots, :], 1, 0)
         out_ref[r, :] = (gates[i] * tok).astype(bf)
-    if guest: pl.when(step == pl.num_programs(0) - 1)(runs[-1])
-
-GUEST_AT = (0, 1, 3, 4, 6, 7, 9, 11, 13)
+    if guest: pl.when(step == pl.num_programs(0) - 1)(finish)
+
+GUEST_AT = (
+    (3, 0, 1), (3, 0, 2), (3, 1, 0), (5, 0, 3), (5, 0, 4), (5, 2, 0), (7, 1, 1), (7, 0, 5), (7, 0, 6), (8, 1, 2),
+    (9, 2, 1), (10, 2, 2), (11, 1, 3), (11, 1, 4), (13, 2, 3), (13, 2, 4), (14, 1, 5), (14, 1, 6), (15, 2, 5), (15, 2, 6),
+)
 
 def backward_kernel(experts, slots, SB, block, meta_ref, cota_ref, cotb_ref, rows_ref, ga_ref, ua_ref, wg_hbm, wu_hbm, wd_hbm, gr_ref, dwg_hbm, dwu_hbm, dwd_hbm,
                   wg, wu, wd, dwg, dwu, dwd, gp, wsem, osem):
@@ -624,18 +627,22 @@
 def scale_of(u):
     return lax.rsqrt(jnp.mean(u * u, axis=-1, keepdims=True) + epsilon)
 
-def attention_forward_kernel(group, q_ref, k_ref, v_ref, gq_ref, gk_ref, cos_ref, sin_ref, ql_ref, kl_ref, vl_ref, mix_ref):
+def attention_forward_kernel(group, n_ref, wq_ref, wk_ref, wv_ref, gq_ref, gk_ref, cos_ref, sin_ref, u_ref, ku_ref, ql_ref, kl_ref, vl_ref, mix_ref, k_all):
     bf, f32 = jnp.bfloat16, jnp.float32
-    rows, seq = q_ref.shape[0], k_ref.shape[0]
+    rows, seq = ql_ref.shape[0], kl_ref.shape[0]
     first = lax.axis_index("shard") * rows
-    k = k_ref[...]
+    own = pl.ds(first, rows)
+    k_all[...] = dot(n_ref[...], wk_ref[...], 1, 0)
+    ku_ref[...] = k_all[own, :]
+    k = k_all[...]
     kl_ref[...] = turn(k * scale_of(k) * gk_ref[...], cos_ref[...], sin_ref[...]).astype(bf)
-    vl_ref[...] = v_ref[...].astype(bf)
-    cos, sin = cos_ref[pl.ds(first, rows), :], sin_ref[pl.ds(first, rows), :]
+    vl_ref[...] = dot(n_ref[...], wv_ref[...], 1, 0).astype(bf)
+    u_ref[...] = dot(n_ref[own, :], wq_ref[...], 1, 0)
+    cos, sin = cos_ref[own, :], sin_ref[own, :]
     allowed = lax.broadcasted_iota(jnp.int32, (rows, seq), 1) <= first + lax.broadcasted_iota(jnp.int32, (rows, seq), 0)
     for j in range(group):
         cols = slice(j * HD, (j + 1) * HD)
-        u = q_ref[:, cols]
+        u = u_ref[:, cols]
         ql = (turn(u * scale_of(u) * gq_ref[...], cos, sin) * HD ** (-0.5)).astype(bf)
         ql_ref[:, cols] = ql
         scores = dot(ql, kl_ref[...], 1, 1)
@@ -643,22 +650,26 @@
         probs = (raised * (1.0 / jnp.sum(raised, axis=-1, keepdims=True))).astype(bf)
         mix_ref[:, cols] = dot(probs, vl_ref[...], 1, 0).astype(bf)
 
-def attention_forward(q_proj, kv_proj, gq, gk, cos, sin):
-    rows, seq = q_proj.shape[0], kv_proj.shape[0]
+def attention_forward(normed_seq, wqkv, rows, gq, gk, cos, sin):
+    seq, width = normed_seq.shape
     group = HQ // HK
-    bf = jnp.bfloat16
+    bf, f32 = jnp.bfloat16, jnp.float32
     whole = lambda a: pl.BlockSpec(a.shape, lambda i: (0, 0))
     gq, gk = gq[None, :], gk[None, :]
+    qb = pl.BlockSpec((rows, group * HD), lambda i: (0, i)); kb = pl.BlockSpec((seq, HD), lambda i: (0, i))
     return pl.pallas_call(
         functools.partial(attention_forward_kernel, group),
         grid=(HK,),
-        out_shape=[jax.ShapeDtypeStruct(q_proj.shape, bf), jax.ShapeDtypeStruct((seq, HK * HD), bf), jax.ShapeDtypeStruct((seq, HK * HD), bf), jax.ShapeDtypeStruct(q_proj.shape, bf)],
-        in_specs=[pl.BlockSpec((rows, group * HD), lambda i: (0, i)), pl.BlockSpec((seq, HD), lambda i: (0, i)), pl.BlockSpec((seq, HD), lambda i: (0, HK + i)), whole(gq), whole(gk), whole(cos), whole(sin)],
-        out_specs=[pl.BlockSpec((rows, group * HD), lambda i: (0, i)), pl.BlockSpec((seq, HD), lambda i: (0, i)), pl.BlockSpec((seq, HD), lambda i: (0, i)), pl.BlockSpec((rows, group * HD), lambda i: (0, i))],
-        compiler_params=pltpu.CompilerParams(dimension_semantics=("arbitrary",), vmem_limit_bytes=48 << 20),
-        cost_estimate=pl.CostEstimate(flops=4_300_000_000, bytes_accessed=20_000_000, transcendentals=8_400_000),
+        out_shape=[jax.ShapeDtypeStruct((rows, HQ * HD), f32), jax.ShapeDtypeStruct((rows, HK * HD), f32), jax.ShapeDtypeStruct((rows, HQ * HD), bf),
+            jax.ShapeDtypeStruct((seq, HK * HD), bf), jax.ShapeDtypeStruct((seq, HK * HD), bf), jax.ShapeDtypeStruct((rows, HQ * HD), bf)],
+        in_specs=[whole(normed_seq), pl.BlockSpec((width, group * HD), lambda i: (0, i)), pl.BlockSpec((width, HD), lambda i: (0, HQ + i)), pl.BlockSpec((width, HD), lambda i: (0, HQ + HK + i)),
+            whole(gq), whole(gk), whole(cos), whole(sin)],
+        out_specs=[qb, pl.BlockSpec((rows, HD), lambda i: (0, i)), qb, kb, kb, qb],
+        scratch_shapes=[pltpu.VMEM((seq, HD), f32)],
+        compiler_params=pltpu.CompilerParams(dimension_semantics=("arbitrary",), vmem_limit_bytes=56 << 20),
+        cost_estimate=pl.CostEstimate(flops=13_000_000_000, bytes_accessed=45_000_000, transcendentals=8_400_000),
         name="attention_forward",
-    )(q_proj, kv_proj, kv_proj, gq, gk, cos, sin)
+    )(normed_seq, wqkv, wqkv, wqkv, gq, gk, cos, sin)
 
 def attention_backward_kernel(group, guest, *refs):
     if guest:
@@ -845,17 +856,17 @@
     wr_full, attn_gain, ffn_gain, query_gain, key_gain = [small_all[:, o : o + n].reshape(-1) for o, n in zip(starts, sizes)]
     wr_full = wr_full.reshape(model_width, expert_count)
     attn_gain, ffn_gain, query_gain, key_gain = [g.astype(f32) for g in (attn_gain, ffn_gain, query_gain, key_gain)]
-    first = 3 * tok_rows // 8
+    first = tok_rows // 2
     cot_first, wo_full = lax.optimization_barrier((cotangent[:first], wo_full))
     cot_a = lax.all_gather(cot_first, BOTH, axis=0, tiled=True)
 
     inputs_f = hidden_in.astype(f32)
     normed_low = norm_rows(inputs_f, attn_gain).astype(bf)
     normed_seq = norm_rows(hidden_seq.astype(f32), attn_gain).astype(bf)
-    kv_proj = matmul(normed_seq, wqkv_full[:, q_cols:])
-    q_proj = matmul(normed_low, wqkv_full[:, :q_cols])
     cosine, sine = rope_tables(seq_len)
-    q_low, k_low, v_low, mix_low = attention_forward(q_proj, kv_proj, query_gain, key_gain, cosine, sine)
+    q_proj, k_proj, q_low, k_low, v_low, mix_low = attention_forward(
+        normed_seq, wqkv_full, tok_rows, query_gain, key_gain, cosine, sine
+    )
     residual = inputs_f + matmul(mix_low, wo_full)
     ffn_low = norm_rows(residual, ffn_gain).astype(bf)
 
@@ -910,7 +921,6 @@
     )
     grad_kv = line_scatter(grad_kv, 6)
     own_rows = shard_pos * tok_rows
-    k_proj = lax.dynamic_slice(kv_proj, (own_rows, 0), (tok_rows, kv_cols))
     positions = own_rows + jnp.arange(tok_rows, dtype=jnp.int32)
     _, k_pull = jax.vjp(
         lambda projected, gain_vec: head_prep(projected, gain_vec, positions, HK, 1.0), k_proj, key_gain
@@ -929,8 +939,7 @@
         [g.astype(bf).reshape(devices, -1) for g in grads] + [jnp.zeros((devices, small_rows * 128 - used), bf)], axis=1
     ).reshape(devices * small_rows, 128)
     grad_wqkv, out_grad = lax.optimization_barrier((grad_wqkv, out_grad))
-    out_grad = lax.psum_scatter(out_grad, "shard", scatter_dimension=0, tiled=True).astype(f32)
-    qkv_grad, small_grad, moe_b = scatter_all([grad_wqkv, packed], 8, line=[moe_b])
+    qkv_grad, small_grad, moe_b, out_grad = scatter_all([grad_wqkv, packed], 8, line=[moe_b, out_grad])
     block_out = (residual + jnp.concatenate([moe_a, moe_b], axis=0)).astype(bf)
     small_grad = small_grad.reshape(-1)
     router_g, attn_g, ffn_g, query_g, key_g = [small_grad[o : o + n] for o, n in zip(starts, sizes)]

time: 1260 us -> 1260 us (level)
  Pallas kernels: 1100 us -> 1130 us
  matrix products: 67.3 us -> 45.7 us
    pallas_call x1, Pallas kernels: 138 us -> 103 us  [experts_forward(): pl.pallas_call(functools.partial(forward_kernel, experts, slots, SB, host...]
    pallas_call x2, Pallas kernels: 331 us -> 354 us  [ag32(): pl.pallas_call(functools.partial(ag_kernel, n, m), out_shape=[jax.ShapeDt...]
    dot_general x4 -> x2, matrix products: 31.9 us -> 9.39 us  [matmul(): return jnp.dot(left, right, preferred_element_type=jnp.float32)]
    pallas_call x1, Pallas kernels: 26.5 us -> 48.9 us  [attention_forward(): pl.pallas_call(functools.partial(attention_forward_kernel, group), grid=(...]
    pallas_call x2, Pallas kernels: 390 us -> 404 us  [rs32(): pl.pallas_call(functools.partial(rs_kernel, n, nl, parts), out_shape=[jax...]
  transfers between devices with their start and end apart: 4 -> 3, of which waited for: 0 -> 0; matrix products, arithmetic and copies ran while one was open for 8% -> 6% of each run, Pallas kernels for 75% -> 64%
where the time goes in v7:
time: 1260 us; the launch traced here: 1250 us
  Pallas kernels  1130 us (90%)
  matrix products  45.7 us (4%)
  local copies, waits for them, and re-layouts  35.5 us (3%)
  other arithmetic  26.3 us (2%)
  between operations  16.4 us (1%)
    pallas_call x2, Pallas kernels, rs32(): pl.pallas_call(functools.partial(rs_kernel, n, nl, parts), out_shape=[jax...  404 us
    pallas_call x2, Pallas kernels, ag32(): pl.pallas_call(functools.partial(ag_kernel, n, m), out_shape=[jax.ShapeDt...  354 us
    pallas_call x1, Pallas kernels, experts_backward(): pl.pallas_call(functools.partial(backward_kernel, experts, slots, SB, blo...  128 us
    pallas_call x1, Pallas kernels, experts_forward(): pl.pallas_call(functools.partial(forward_kernel, experts, slots, SB, host...  103 us
    pallas_call x1, Pallas kernels, attention_backward(): pl.pallas_call(functools.partial(attention_backward_kernel, group, hosted...  60.3 us
    pallas_call x1, Pallas kernels, attention_forward(): pl.pallas_call(functools.partial(attention_forward_kernel, group), grid=(...  48.9 us
    pallas_call x1, Pallas kernels, line_scatter(): pl.pallas_call(functools.partial(line_scatter_kernel, parts), out_shape=j...  27.6 us
  transfers between devices with their start and end apart: 3, of which 0 were waited for; matrix products, arithmetic and copies ran while one was open for 6% of the time, Pallas kernels for 64%

profile of v7, /device:TPU:18, one launch (start us, length us, event | category | flops | bytes accessed | tf_op | source)
XLA Modules:
  0.0 1250.2 jit_solution(9195641343432222926)
XLA Ops:
  8.1 0.8 copy.59
  9.1 2.3 fusion.31
  11.4 0.9 pad_maximum_fusion.4
  12.3 0.7 concatenate.34
  13.0 167.2 %gather_all.2 = (bf16[2,2,2,4,2,32,5120]{6,5,4,3,2,1,0:T(8,128)(2,1)}, bf16[2,2,2,4,2,32,128]{6,5,4,3,2,1,0:T(8,128)(2,1)}, bf16[2,2,2,4,2,64,2048]{6,5,4,3,2,1,0:T(8,128)(2,1)}, bf16[4,2,128,2048]{3,2,1,0:T(8,128)(2,1)}) custom-call(bf16[2,32,5120]{2,1,0:T(8,128)(2,1)} %bitcast.73, bf16[2,32,128]{2,1,0:T(8,128)(2,1)} %bitcast.88, ...), custom_call_target="tpu_custom_call" | custom-call | tf_op jit(solution)/shard_map/gather_all/pallas_call | solution.py:164
  180.4 1.3 reshape_reshape_reshape.6
  183.8 2.0 fusion.22
  185.7 1.3 pad_maximum_fusion.5
  187.1 0.9 multiply_reduce_fusion
  188.0 3.0 fusion.1.n_ref
  191.0 48.9 %attention_forward.1 = (f32[256,4096]{1,0:T(8,128)}, f32[256,512]{1,0:T(8,128)}, bf16[256,4096]{1,0:T(8,128)(2,1)}, bf16[1024,512]{1,0:T(8,128)(2,1)}, bf16[1024...) custom-call(bf16[1024,2048]{1,0:T(8,128)(2,1)} %fusion.1.n_ref, bf16[2048,5120]{1,0:T(8,128)(2,1)} %bitcast.58, ...), custom_call_target="tpu_custom_call" | custom-call | flops 12999999488 | bytes 45000000 | tf_op jit(solution)/shard_map/attention_forward/pallas_call | solution.py:660
  239.9 8.9 multiply_reduce_fusion.3
  251.1 2.0 concatenate.37
  253.1 186.9 %gather_all.3 = bf16[2,2,2,4,2,128,2176]{6,5,4,3,2,1,0:T(8,128)(2,1)} custom-call(bf16[2,128,2176]{2,1,0:T(8,128)(2,1)} %bitcast.71), custom_call_target="tpu_custom_call" | custom-call | tf_op jit(solution)/shard_map/gather_all/pallas_call | solution.py:164
  439.9 102.8 %experts_forward.1 = (bf16[2,2,2,4,2,64,2048]{6,5,4,3,2,1,0:T(8,128)(2,1)}, bf16[8192,2048]{1,0:T(8,128)(2,1)}, bf16[4096,2048]{1,0:T(8,128)(2,1)}, f32[4096,768]{1,0:T(8,128)}, f32[4096,768]{1,0:T(8,128)}) custom-call(bf16[2,64,2048]{2,1,0:T(8,128)(2,1)} %bitcast.87, bf16[8192,2176]{1,0:T(8,128)(2,1)} %bitcast.63, bf16[1,2048,768]{2,1,0:T(8,128)(2,1)} %wg_hbm.1, ...), custom_call_target="tpu_custom_call" | custom-call | flops 48000000000 | bytes 130000000 | tf_op jit(solution)/shard_map/experts_forward/pallas_call | solution.py:580
  542.8 128.1 %experts_backward.1 = (bf16[8192,2176]{1,0:T(8,128)(2,1)}, f32[1,2048,768]{2,1,0:T(8,128)}, f32[1,2048,768]{2,1,0:T(8,128)}, f32[1,768,2048]{2,1,0:T(8,128)}) custom-call(bf16[8192,2176]{1,0:T(8,128)(2,1)} %bitcast.64, bf16[4096,2048]{1,0:T(8,128)(2,1)} %all-gather.2.cloned.1.call-done.cota_ref, bf16[4096,2048]{1,0:T(8,128)(2,1)} %bitcast.94, ...), custom_call_target="tpu_custom_call" | custom-call | flops 85000003584 | bytes 150000000 | tf_op jit(solution)/shard_map/experts_backward/pallas_call | solution.py:605
  671.0 243.5 %scatter_all.2 = f32[4,64,2176]{2,1,0:T(8,128)} custom-call(bf16[2,2,2,4,4,64,2176]{6,5,4,3,2,1,0:T(8,128)(2,1)} %bitcast.65), custom_call_target="tpu_custom_call" | custom-call | tf_op jit(solution)/shard_map/scatter_all/pallas_call | solution.py:306
  914.5 1.2 fusion.24
  915.7 1.1 subtract_convert_fusion
  916.9 3.1 multiply_reduce_fusion.1
  920.1 2.0 fusion.28
  922.2 8.3 convolution_convert_fusion.1
  933.3 4.9 fusion.29
  938.2 60.3 %attention_backward.1 = (f32[4,32,2048]{2,1,0:T(8,128)}, bf16[256,4096]{1,0:T(8,128)(2,1)}, bf16[1024,512]{1,0:T(8,128)(2,1)}, bf16[1024,512]{1,0:T(8,128)(2,1)}, f32[4,8,128]{2,1,0:T(8,128)}) custom-call(bf16[4,4,32,2048]{3,2,1,0:T(8,128)(2,1)} %bitcast.77, f32[256,4096]{1,0:T(8,128)} %get-tuple-element.64.refs_1_, ...), custom_call_target="tpu_custom_call" | custom-call | flops 15000000512 | bytes 20000000 | tf_op jit(solution)/shard_map/attention_backward/pallas_call | solution.py:731
  998.5 2.0 pad_maximum_fusion.1
  1000.4 27.6 %line_scatter.1 = f32[4,64,1024]{2,1,0:T(8,128)S(1)} custom-call(bf16[4,4,64,1024]{3,2,1,0:T(8,128)(2,1)S(1)} %bitcast.55), custom_call_target="tpu_custom_call" | custom-call | tf_op jit(solution)/shard_map/line_scatter/pallas_call | solution.py:447
  1028.9 0.9 multiply_reduce_fusion.4
  1030.1 0.7 fusion.18
  1030.9 12.9 %fusion.11 = (f32[256]{0:T(256)}, bf16[2048]{0:T(1024)(128)(2,1)S(1)}, f32[256,2048]{1,0:T(8,128)}) fusion(bf16[256,2048]{1,0:T(8,128)(2,1)S(1)} %copy-done.4, f32[2048]{0:T(1024)S(1)} %copy-done.24, f32[256]{0:T(256)S(1)} %get-tuple-element.186, bf16[2048,5120]{1,0:T(8,128)(2,1)} %bitcast.61, bf16[256,512]{1,0:T(8,128)(2,1)S(1)} %slice.127, ...), kind=kOutput, calls=%fused_computation.24 | convolution fusion | flops 5380241408 | bytes 26753024 | tf_op jit(solution)/shard_map/dot_general | solution.py:766
  1044.1 1.0 copy.68
  1045.2 2.3 reshape.253
  1047.4 0.7 convert_element_type.187
  1048.2 0.7 slice_reduce_fusion
  1048.9 0.7 convert_element_type.185
  1050.3 2.0 concatenate.42
  1052.3 2.0 copy.75
  1054.3 0.7 broadcast_multiply_fusion.1
  1055.0 3.2 fusion.10
  1058.2 11.7 convolution_convert_fusion
  1069.9 161.0 %scatter_all.3 = (f32[4,16,5120]{2,1,0:T(8,128)}, f32[4,16,128]{2,1,0:T(8,128)}, f32[4,32,2048]{2,1,0:T(8,128)}, f32[4,32,2048]{2,1,0:T(8,128)}) custom-call(bf16[2,2,2,4,4,16,5120]{6,5,4,3,2,1,0:T(8,128)(2,1)} %bitcast.62, bf16[2,2,2,4,4,16,128]{6,5,4,3,2,1,0:T(8,128)(2,1)} %bitcast.75, bf16[4,4,32,2048]{3,2,1,0:T(8,128)(2,1)} %bitcast.70, ...), custom_call_target="tpu_custom_call" | custom-call | tf_op jit(solution)/shard_map/scatter_all/pallas_call | solution.py:306
  1230.9 2.4 slice.104
  1233.3 1.7 fusion.30
  1235.0 0.7 slice.93
  1235.7 1.3 fusion.33
  1237.0 1.3 fusion.34
  1238.4 0.7 copy.70
  1239.1 2.5 fusion.12
  1241.7 1.0 copy.80
  (142 shorter events, 9.8 us)
Async XLA Ops:
  8.0 3.3 copy-start.21
  8.0 3.3 copy-start.30
  8.0 3.3 copy-start.29
  8.0 4.2 copy-start.39
  8.1 4.2 copy-start.41
  8.1 4.2 copy-start.42
  8.1 4.2 copy-start.40
  8.1 534.8 %all-gather.2.cloned.1.call-start = ((), (), s32[]{:S(2)}) async-start(), calls=%async_computation.2 | async-start | bytes 17301504 | tf_op jit(solution)/shard_map/all_gather | solution.py:861
  11.4 168.9 %copy-start.35 = (s32[256,8]{0,1:T(8,128)S(1)}, s32[256,8]{0,1:T(8,128)}, u32[]{:S(2)}) copy-start(s32[256,8]{0,1:T(8,128)} %param.28) | copy-start | bytes 24580
  180.2 734.4 %reduce-scatter.3.cloned.1.call-start = ((), (), s32[]{:S(2)}) async-start(), calls=%async_computation.3 | async-start | bytes 37748736 | tf_op jit(solution)/shard_map/reduce_scatter | solution.py:895
  181.8 6.1 copy-start.23
  181.9 5.1 copy-start.25
  183.2 66.3 %copy-start.27 = (f32[2048]{0:T(1024)}, f32[2048]{0:T(1024)S(1)}, u32[]{:S(2)}) copy-start(f32[2048]{0:T(1024)S(1)} %reshape.262) | copy-start | bytes 24580
  183.6 66.1 %copy-start.9 = (bf16[2048,32]{1,0:T(8,128)(2,1)}, bf16[2048,32]{1,0:T(8,128)(2,1)S(1)}, u32[]{:S(2)}) copy-start(bf16[2048,32]{1,0:T(8,128)(2,1)S(1)} %reshape_reshape.31) | copy-start | bytes 393220
  183.7 3.3 copy-start.37
  183.8 3.3 copy-start.7
  191.0 48.9 %copy-start.3 = (bf16[256,2048]{1,0:T(8,128)(2,1)S(1)}, bf16[256,2048]{1,0:T(8,128)(2,1)}, u32[]{:S(2)}) copy-start(bf16[256,2048]{1,0:T(8,128)(2,1)} %param.15) | copy-start | bytes 3145732
  248.8 1.5 copy-start
  249.5 0.8 copy-start.31
  249.7 3.3 copy-start.5
  250.3 0.7 copy-start.14
  250.3 0.8 copy-start.33
  542.8 527.1 %reduce-scatter.5.cloned.1.call-start = ((), (), s32[]{:S(2)}) async-start(), calls=%async_computation.4 | async-start | bytes 18874368 | tf_op jit(solution)/shard_map/reduce_scatter | solution.py:915
  671.0 244.7 %copy-start.15 = (f32[256,32]{1,0:T(8,128)S(1)}, f32[256,32]{1,0:T(8,128)}, u32[]{:S(2)}) copy-start(f32[256,32]{1,0:T(8,128)} %copy-done.14) | copy-start | bytes 98308
  671.0 244.7 %copy-start.34 = (f32[256]{0:T(256)S(1)}, f32[256]{0:T(256)}, u32[]{:S(2)}) copy-start(f32[256]{0:T(256)} %copy-done.33) | copy-start | bytes 3076
  671.0 245.9 %copy-start.10 = (bf16[2048,32]{1,0:T(8,128)(2,1)S(1)}, bf16[2048,32]{1,0:T(8,128)(2,1)}, u32[]{:S(2)}) copy-start(bf16[2048,32]{1,0:T(8,128)(2,1)} %copy-done.9) | copy-start | bytes 393220
  671.0 245.9 %copy-start.28 = (f32[2048]{0:T(1024)S(1)}, f32[2048]{0:T(1024)}, u32[]{:S(2)}) copy-start(f32[2048]{0:T(1024)} %copy-done.27) | copy-start | bytes 24580
  671.0 245.9 %copy-start.32 = (f32[256]{0:T(256)S(1)}, f32[256]{0:T(256)}, u32[]{:S(2)}) copy-start(f32[256]{0:T(256)} %copy-done.31) | copy-start | bytes 3076
  916.9 3.2 copy-start.1
  916.9 3.2 copy-start.12
  916.9 3.2 copy-start.36
  920.1 2.0 copy-start.13
  922.2 8.3 copy-start.11
  930.4 0.7 copy-start.26
  930.4 1.1 copy-start.22
  930.4 1.9 copy-start.38
  930.5 2.5 copy-start.4
  1028.1 2.7 copy-start.16
  1028.9 2.0 copy-start.24
  1030.8 12.9 %copy-start.18 = (bf16[32,8,4,128]{3,1,2,0:T(8,128)(2,1)}, bf16[32,8,4,128]{3,1,2,0:T(8,128)(2,1)S(1)}, u32[]{:S(2)}) copy-start(bf16[32,8,4,128]{3,1,2,0:T(8,128)(2,1)S(1)} %copy.77) | copy-start | bytes 786436
  1030.8 13.0 %copy-start.6 = (bf16[256,2048]{1,0:T(8,128)(2,1)S(1)}, bf16[256,2048]{1,0:T(8,128)(2,1)}, u32[]{:S(2)}) copy-start(bf16[256,2048]{1,0:T(8,128)(2,1)} %copy-done.5) | copy-start | bytes 3145732
  1044.1 10.8 copy-start.8
  1054.9 3.2 copy-start.17
  1069.9 169.2 %copy-start.19 = (f32[4,32,2048]{2,1,0:T(8,128)S(1)}, f32[4,32,2048]{2,1,0:T(8,128)}, u32[]{:S(2)}) copy-start(f32[4,32,2048]{2,1,0:T(8,128)} %get-tuple-element.70) | copy-start | bytes 3145732
  1230.9 8.3 copy-start.2
  1239.1 2.5 copy-start.20
Sparse Core Ops, SparseCore 0:
  180.3 144.1 all-gather.1
Sparse Core Ops, SparseCore 1:
  542.8 258.4 reduce-scatter.2
  930.5 116.7 reduce-scatter.4

commit v8 on v7

--- a/solution.py
+++ b/solution.py
@@ -271,13 +271,14 @@
     for u in units:
         c0(*u).start(); load(*u).start()
     n = len(units); nl = len(lines)
+    per = max(1, -(-nl // n))
     L1 = LAGS[0] * n_arr; L2 = L1 + LAGS[1] * n_arr; L3 = L2 + LAGS[2] * n_arr; dl = LAGS[3] * n_arr
     for i in range(n + L3 + (NZ - 1) * dl):
         if i < n: stage0(units[i])
         if 0 <= i - L1 < n: stage1(units[i - L1])
         if 0 <= i - L2 < n: stage2(units[i - L2])
         for k in range(NZ - 1):
-            for q in (2 * (i - k), 2 * (i - k) + 1):
+            for q in range(per * (i - k), per * (i - k) + per):
                 if 0 <= q < nl:
                     if k == 0: load(*lines[q]).wait()
                     hop(lines[q], k)
@@ -919,17 +920,19 @@
     moe_a, grad_q_low, grad_kv, grad_query_gain = attention_backward(
         q_proj, q_low, k_low, v_low, grad_attn_low, wo_full, query_gain, cosine, sine, moe_a, 5
     )
-    grad_kv = line_scatter(grad_kv, 6)
+    grad_wq = matmul_tn(normed_low, grad_q_low).astype(bf)
+    q_grad, grad_kv = scatter_all([grad_wq], 7, line=[grad_kv])
+    q_grad, out_grad = lax.optimization_barrier((q_grad, out_grad))
+    out_grad = lax.psum_scatter(out_grad, "shard", scatter_dimension=0, tiled=True).astype(f32)
     own_rows = shard_pos * tok_rows
     positions = own_rows + jnp.arange(tok_rows, dtype=jnp.int32)
     _, k_pull = jax.vjp(
         lambda projected, gain_vec: head_prep(projected, gain_vec, positions, HK, 1.0), k_proj, key_gain
     )
     grad_k_proj, grad_key_gain = k_pull(grad_kv[:, :kv_cols].reshape(tok_rows, HK, HD))
-    grad_qkv_low = jnp.concatenate(
-        [grad_q_low, grad_k_proj.astype(bf), grad_kv[:, kv_cols:].astype(bf)], axis=1
-    )
-    grad_wqkv = matmul_tn(normed_low, grad_qkv_low).astype(bf)
+    grad_kv_low = jnp.concatenate([grad_k_proj.astype(bf), grad_kv[:, kv_cols:].astype(bf)], axis=1)
+    grad_wkv = matmul_tn(normed_low, grad_kv_low).astype(bf)
+    grad_qkv_low = jnp.concatenate([grad_q_low, grad_kv_low], axis=1)
     grad_normed = matmul_nt(grad_qkv_low, wqkv_full)
     grad_front, grad_attn_gain = norm_back(inputs_f, attn_gain, grad_normed)
     grad_input = (grad_residual + grad_front).astype(bf)
@@ -938,8 +941,7 @@
     packed = jnp.concatenate(
         [g.astype(bf).reshape(devices, -1) for g in grads] + [jnp.zeros((devices, small_rows * 128 - used), bf)], axis=1
     ).reshape(devices * small_rows, 128)
-    grad_wqkv, out_grad = lax.optimization_barrier((grad_wqkv, out_grad))
-    qkv_grad, small_grad, moe_b, out_grad = scatter_all([grad_wqkv, packed], 8, line=[moe_b, out_grad])
+    kv_grad, small_grad, moe_b = scatter_all([grad_wkv, packed], 8, line=[moe_b])
     block_out = (residual + jnp.concatenate([moe_a, moe_b], axis=0)).astype(bf)
     small_grad = small_grad.reshape(-1)
     router_g, attn_g, ffn_g, query_g, key_g = [small_grad[o : o + n] for o, n in zip(starts, sizes)]
@@ -947,9 +949,9 @@
         block_out,
         grad_input,
         attn_g,
-        qkv_grad[:, :q_cols],
-        qkv_grad[:, q_cols : q_cols + kv_cols],
-        qkv_grad[:, q_cols + kv_cols :],
+        q_grad,
+        kv_grad[:, :kv_cols],
+        kv_grad[:, kv_cols:],
         query_g,
         key_g,
         out_grad,

time: 1260 us -> 1290 us (1.024)
  Pallas kernels: 1130 us -> 1160 us
    pallas_call x2 -> x3, Pallas kernels: 404 us -> 467 us  [rs32(): pl.pallas_call(functools.partial(rs_kernel, n, nl, parts), out_shape=[jax...]
    pallas_call x1 -> x0, Pallas kernels: 27.6 us -> none  [line_scatter(): pl.pallas_call(functools.partial(line_scatter_kernel, parts), out_shape=j...]
  transfers between devices with their start and end apart: 3 -> 4, of which waited for: 0 -> 0; matrix products, arithmetic and copies ran while one was open for 6% -> 6% of each run, Pallas kernels for 64% -> 77%
where the time goes in v8:
time: 1290 us; the launch traced here: 1280 us
  Pallas kernels  1160 us (90%)
  matrix products  47.4 us (4%)
  local copies, waits for them, and re-layouts  30 us (2%)
  other arithmetic  29 us (2%)
  between operations  16.6 us (1%)
    pallas_call x3, Pallas kernels, rs32(): pl.pallas_call(functools.partial(rs_kernel, n, nl, parts), out_shape=[jax...  467 us
    pallas_call x2, Pallas kernels, ag32(): pl.pallas_call(functools.partial(ag_kernel, n, m), out_shape=[jax.ShapeDt...  358 us
    pallas_call x1, Pallas kernels, experts_backward(): pl.pallas_call(functools.partial(backward_kernel, experts, slots, SB, blo...  127 us
    pallas_call x1, Pallas kernels, experts_forward(): pl.pallas_call(functools.partial(forward_kernel, experts, slots, SB, host...  106 us
    pallas_call x1, Pallas kernels, attention_backward(): pl.pallas_call(functools.partial(attention_backward_kernel, group, hosted...  60.3 us
    pallas_call x1, Pallas kernels, attention_forward(): pl.pallas_call(functools.partial(attention_forward_kernel, group), grid=(...  38.7 us
  transfers between devices with their start and end apart: 4, of which 0 were waited for; matrix products, arithmetic and copies ran while one was open for 6% of the time, Pallas kernels for 77%

profile of v8, /device:TPU:18, one launch (start us, length us, event | category | flops | bytes accessed | tf_op | source)
XLA Modules:
  0.0 1280.3 jit_solution(7922628196880605577)
XLA Ops:
  8.1 0.8 copy.59
  9.1 2.3 fusion.37
  11.4 0.9 pad_maximum_fusion.1
  12.3 0.7 concatenate.38
  13.0 167.2 %gather_all.2 = (bf16[2,2,2,4,2,32,5120]{6,5,4,3,2,1,0:T(8,128)(2,1)}, bf16[2,2,2,4,2,32,128]{6,5,4,3,2,1,0:T(8,128)(2,1)}, bf16[2,2,2,4,2,64,2048]{6,5,4,3,2,1,0:T(8,128)(2,1)}, bf16[4,2,128,2048]{3,2,1,0:T(8,128)(2,1)}) custom-call(bf16[2,32,5120]{2,1,0:T(8,128)(2,1)} %bitcast.73, bf16[2,32,128]{2,1,0:T(8,128)(2,1)} %bitcast.88, ...), custom_call_target="tpu_custom_call" | custom-call | tf_op jit(solution)/shard_map/gather_all/pallas_call | solution.py:164
  180.4 1.3 reshape_reshape_reshape.6
  181.9 0.6 reshape.256.gq_ref.refs_7_
  182.5 0.6 reshape.257.gk_ref
  183.8 2.0 fusion.29
  185.7 1.3 pad_maximum_fusion.2
  187.1 0.9 multiply_reduce_fusion
  188.0 3.0 fusion.1.n_ref
  191.0 38.7 %attention_forward.1 = (f32[256,4096]{1,0:T(8,128)}, f32[256,512]{1,0:T(8,128)}, bf16[256,4096]{1,0:T(8,128)(2,1)}, bf16[1024,512]{1,0:T(8,128)(2,1)}, bf16[1024...) custom-call(bf16[1024,2048]{1,0:T(8,128)(2,1)} %fusion.1.n_ref, bf16[2048,5120]{1,0:T(8,128)(2,1)} %bitcast.56, ...), custom_call_target="tpu_custom_call" | custom-call | flops 12999999488 | bytes 45000000 | tf_op jit(solution)/shard_map/attention_forward/pallas_call | solution.py:661
  229.7 8.9 multiply_reduce_fusion.3
  240.1 0.6 copy-done.16
  240.8 2.0 concatenate.41
  242.8 190.8 %gather_all.3 = bf16[2,2,2,4,2,128,2176]{6,5,4,3,2,1,0:T(8,128)(2,1)} custom-call(bf16[2,128,2176]{2,1,0:T(8,128)(2,1)} %bitcast.70), custom_call_target="tpu_custom_call" | custom-call | tf_op jit(solution)/shard_map/gather_all/pallas_call | solution.py:164
  433.6 105.6 %experts_forward.1 = (bf16[2,2,2,4,2,64,2048]{6,5,4,3,2,1,0:T(8,128)(2,1)}, bf16[8192,2048]{1,0:T(8,128)(2,1)}, bf16[4096,2048]{1,0:T(8,128)(2,1)}, f32[4096,768]{1,0:T(8,128)}, f32[4096,768]{1,0:T(8,128)}) custom-call(bf16[2,64,2048]{2,1,0:T(8,128)(2,1)} %bitcast.84, bf16[8192,2176]{1,0:T(8,128)(2,1)} %bitcast.61, bf16[1,2048,768]{2,1,0:T(8,128)(2,1)} %wg_hbm.1, ...), custom_call_target="tpu_custom_call" | custom-call | flops 48000000000 | bytes 130000000 | tf_op jit(solution)/shard_map/experts_forward/pallas_call | solution.py:581
  539.3 127.4 %experts_backward.1 = (bf16[8192,2176]{1,0:T(8,128)(2,1)}, f32[1,2048,768]{2,1,0:T(8,128)}, f32[1,2048,768]{2,1,0:T(8,128)}, f32[1,768,2048]{2,1,0:T(8,128)}) custom-call(bf16[8192,2176]{1,0:T(8,128)(2,1)} %bitcast.62, bf16[4096,2048]{1,0:T(8,128)(2,1)} %all-gather.2.cloned.1.call-done.cota_ref, bf16[4096,2048]{1,0:T(8,128)(2,1)} %bitcast.94, ...), custom_call_target="tpu_custom_call" | custom-call | flops 85000003584 | bytes 150000000 | tf_op jit(solution)/shard_map/experts_backward/pallas_call | solution.py:606
  666.7 246.2 %scatter_all.3 = f32[4,64,2176]{2,1,0:T(8,128)} custom-call(bf16[2,2,2,4,4,64,2176]{6,5,4,3,2,1,0:T(8,128)(2,1)} %bitcast.63), custom_call_target="tpu_custom_call" | custom-call | tf_op jit(solution)/shard_map/scatter_all/pallas_call | solution.py:307
  913.0 1.2 fusion.31
  914.1 1.1 subtract_convert_fusion
  915.4 3.7 multiply_reduce_fusion.1
  919.1 2.0 fusion.35
  921.1 8.1 convolution_convert_fusion.1
  933.4 4.9 fusion.36
  938.2 60.3 %attention_backward.1 = (f32[4,32,2048]{2,1,0:T(8,128)}, bf16[256,4096]{1,0:T(8,128)(2,1)}, bf16[1024,512]{1,0:T(8,128)(2,1)}, bf16[1024,512]{1,0:T(8,128)(2,1)}, f32[4,8,128]{2,1,0:T(8,128)}) custom-call(bf16[4,4,32,2048]{3,2,1,0:T(8,128)(2,1)} %bitcast.75, f32[256,4096]{1,0:T(8,128)} %get-tuple-element.65.refs_1_, ...), custom_call_target="tpu_custom_call" | custom-call | flops 15000000512 | bytes 20000000 | tf_op jit(solution)/shard_map/attention_backward/pallas_call | solution.py:732
  998.6 3.3 pad_maximum_fusion
  1001.8 9.9 convolution_convert_fusion
  1011.8 128.0 %scatter_all.4 = (f32[4,16,4096]{2,1,0:T(8,128)}, f32[4,64,1024]{2,1,0:T(8,128)}) custom-call(bf16[2,2,2,4,4,16,4096]{6,5,4,3,2,1,0:T(8,128)(2,1)} %bitcast.60, bf16[4,4,64,1024]{3,2,1,0:T(8,128)(2,1)} %bitcast.68), custom_call_target="tpu_custom_call" | custom-call | tf_op jit(solution)/shard_map/scatter_all/pallas_call | solution.py:307
  1139.7 1.1 slice.96
  1140.8 1.8 slice.122
  1143.6 0.9 multiply_reduce_fusion.4
  1144.9 0.7 fusion.20
  1145.8 12.5 fusion.17
  1159.6 0.7 slice_reduce_fusion
  1161.1 0.9 copy.75
  1162.0 3.4 convolution_convert_fusion.2
  1165.4 92.9 %scatter_all.5 = (f32[4,16,1024]{2,1,0:T(8,128)}, f32[4,16,128]{2,1,0:T(8,128)}, f32[4,32,2048]{2,1,0:T(8,128)}) custom-call(bf16[2,2,2,4,4,16,1024]{6,5,4,3,2,1,0:T(8,128)(2,1)} %bitcast.72, bf16[2,2,2,4,4,16,128]{6,5,4,3,2,1,0:T(8,128)(2,1)} %bitcast.76, bf16[4,4,32,2048]{3,2,1,0:T(8,128)(2,1)} %bitcast.69), custom_call_target="tpu_custom_call" | custom-call | tf_op jit(solution)/shard_map/scatter_all/pallas_call | solution.py:307
  1258.4 0.7 slice.89
  1259.1 0.7 copy.70
  1259.8 1.3 fusion.40
  1261.2 1.3 fusion.41
  1262.5 1.7 fusion.39
  1264.2 3.6 fusion.18
  1267.8 1.6 fusion.16
  1269.4 2.2 convert_element_type.197
  1271.6 1.0 copy.80
  (166 shorter events, 10.4 us)
Async XLA Ops:
  8.0 3.3 copy-start.19
  8.0 3.3 copy-start.31
  8.0 3.3 copy-start.30
  8.0 4.2 copy-start.49
  8.1 4.2 copy-start.51
  8.1 4.2 copy-start.52
  8.1 4.2 copy-start.50
  8.1 531.2 %all-gather.2.cloned.1.call-start = ((), (), s32[]{:S(2)}) async-start(), calls=%async_computation.3 | async-start | bytes 17301504 | tf_op jit(solution)/shard_map/all_gather | solution.py:862
  11.4 168.9 %copy-start.42 = (s32[256,8]{0,1:T(8,128)S(1)}, s32[256,8]{0,1:T(8,128)}, u32[]{:S(2)}) copy-start(s32[256,8]{0,1:T(8,128)} %param.28) | copy-start | bytes 24580
  180.2 732.8 %reduce-scatter.4.cloned.1.call-start = ((), (), s32[]{:S(2)}) async-start(), calls=%async_computation.4 | async-start | bytes 37748736 | tf_op jit(solution)/shard_map/reduce_scatter | solution.py:896
  181.8 6.1 copy-start.22
  181.9 5.1 copy-start.26
  183.2 56.0 %copy-start.28 = (f32[2048]{0:T(1024)}, f32[2048]{0:T(1024)S(1)}, u32[]{:S(2)}) copy-start(f32[2048]{0:T(1024)S(1)} %reshape.258) | copy-start | bytes 24580
  183.6 55.9 %copy-start.10 = (bf16[2048,32]{1,0:T(8,128)(2,1)}, bf16[2048,32]{1,0:T(8,128)(2,1)S(1)}, u32[]{:S(2)}) copy-start(bf16[2048,32]{1,0:T(8,128)(2,1)S(1)} %reshape_reshape.34) | copy-start | bytes 393220
  183.7 3.3 copy-start.46
  183.8 3.3 copy-start.6
  191.0 38.7 %copy-start.2 = (bf16[256,2048]{1,0:T(8,128)(2,1)S(1)}, bf16[256,2048]{1,0:T(8,128)(2,1)}, u32[]{:S(2)}) copy-start(bf16[256,2048]{1,0:T(8,128)(2,1)} %param.15) | copy-start | bytes 3145732
  238.6 1.4 copy-start
  239.5 3.3 copy-start.4
  539.2 606.4 %reduce-scatter.6.cloned.1.call-start = ((), (), s32[]{:S(2)}) async-start(), calls=%async_computation.5 | async-start | bytes 18874368 | tf_op jit(solution)/shard_map/reduce_scatter | solution.py:916
  666.7 247.5 %copy-start.17 = (f32[256,32]{1,0:T(8,128)S(1)}, f32[256,32]{1,0:T(8,128)}, u32[]{:S(2)}) copy-start(f32[256,32]{1,0:T(8,128)} %copy-done.16) | copy-start | bytes 98308
  666.7 247.5 %copy-start.41 = (f32[256]{0:T(256)S(1)}, f32[256]{0:T(256)}, u32[]{:S(2)}) copy-start(f32[256]{0:T(256)} %copy-done.40) | copy-start | bytes 3076
  666.7 248.6 %copy-start.11 = (bf16[2048,32]{1,0:T(8,128)(2,1)S(1)}, bf16[2048,32]{1,0:T(8,128)(2,1)}, u32[]{:S(2)}) copy-start(bf16[2048,32]{1,0:T(8,128)(2,1)} %copy-done.10) | copy-start | bytes 393220
  666.7 248.6 %copy-start.29 = (f32[2048]{0:T(1024)S(1)}, f32[2048]{0:T(1024)}, u32[]{:S(2)}) copy-start(f32[2048]{0:T(1024)} %copy-done.28) | copy-start | bytes 24580
  666.7 248.6 %copy-start.39 = (f32[256]{0:T(256)S(1)}, f32[256]{0:T(256)}, u32[]{:S(2)}) copy-start(f32[256]{0:T(256)} %copy-done.38) | copy-start | bytes 3076
  915.3 3.8 copy-start.1
  915.3 3.8 copy-start.13
  915.3 3.8 copy-start.45
  919.1 2.0 copy-start.14
  921.1 8.2 copy-start.12
  929.3 1.3 copy-start.20
  929.3 2.6 copy-start.47
  929.3 3.2 copy-start.3
  929.3 340.1 %reduce-scatter.8.cloned.1.call-start = ((), (), s32[]{:S(2)}) async-start(), calls=%async_computation.6 | async-start | bytes 2621440 | tf_op jit(solution)/shard_map/reduce_scatter | solution.py:926
  930.8 7.4 copy-start.8
  933.4 68.5 %copy-start.34 = (f32[256]{0:T(256)}, f32[256]{0:T(256)S(1)}, u32[]{:S(2)}) copy-start(f32[256]{0:T(256)S(1)} %get-tuple-element.188) | copy-start | bytes 3076
  998.6 3.3 copy-start.23
  1142.6 1.0 copy-start.43
  1143.3 1.3 copy-start.33
  1145.8 12.6 copy-start.5
  1158.3 2.2 copy-start.37
  1165.4 94.4 %copy-start.48 = (f32[256]{0:T(256)S(1)}, f32[256]{0:T(256)}, u32[]{:S(2)}) copy-start(f32[256]{0:T(256)} %get-tuple-element.160) | copy-start | bytes 3076
  1264.2 3.6 copy-start.7
  1264.2 3.6 copy-start.15
  1264.2 3.6 copy-start.25
  1264.2 3.6 copy-start.36
  1264.2 3.6 copy-start.44
  1269.4 2.2 copy-start.18
  (9 other events, 7.4 us)
Sparse Core Ops, SparseCore 0:
  180.3 156.1 all-gather.1
  1145.8 65.4 reduce-scatter.7
Sparse Core Ops, SparseCore 1:
  539.3 264.2 reduce-scatter.3
  929.4 134.2 reduce-scatter.5

commit v9 on v7

--- a/solution.py
+++ b/solution.py
@@ -271,13 +271,14 @@
     for u in units:
         c0(*u).start(); load(*u).start()
     n = len(units); nl = len(lines)
+    per = max(1, -(-nl // n))
     L1 = LAGS[0] * n_arr; L2 = L1 + LAGS[1] * n_arr; L3 = L2 + LAGS[2] * n_arr; dl = LAGS[3] * n_arr
     for i in range(n + L3 + (NZ - 1) * dl):
         if i < n: stage0(units[i])
         if 0 <= i - L1 < n: stage1(units[i - L1])
         if 0 <= i - L2 < n: stage2(units[i - L2])
         for k in range(NZ - 1):
-            for q in (2 * (i - k), 2 * (i - k) + 1):
+            for q in range(per * (i - k), per * (i - k) + per):
                 if 0 <= q < nl:
                     if k == 0: load(*lines[q]).wait()
                     hop(lines[q], k)
@@ -478,7 +479,14 @@
     if guest:
         start, stage_a, stage_b, stage_c, finish = ag_steps(1, 0, [cot_ref], [cot_all], refs[14:], True)
         pl.when(step == 0)(start)
-        for at, stage, k in GUEST_AT: pl.when(step == at)(functools.partial(stage_a if stage == 0 else stage_b if stage == 1 else stage_c, k))
+        shard = lax.axis_index("shard")
+        for at in range(1, 16):
+            for z in range(NZ):
+                now = guest_stages(z, at)
+                if now:
+                    @pl.when((step == at) & (shard == z))
+                    def _():
+                        for stage, k in now: (stage_a, stage_b, stage_c)[stage](k)
     nsub = x_ref.shape[0] // SB
     D = out_ref.shape[1]
     me = lax.axis_index(("expert", "shard"))
@@ -507,10 +515,15 @@
         out_ref[r, :] = (gates[i] * tok).astype(bf)
     if guest: pl.when(step == pl.num_programs(0) - 1)(finish)
 
-GUEST_AT = (
-    (3, 0, 1), (3, 0, 2), (3, 1, 0), (5, 0, 3), (5, 0, 4), (5, 2, 0), (7, 1, 1), (7, 0, 5), (7, 0, 6), (8, 1, 2),
-    (9, 2, 1), (10, 2, 2), (11, 1, 3), (11, 1, 4), (13, 2, 3), (13, 2, 4), (14, 1, 5), (14, 1, 6), (15, 2, 5), (15, 2, 6),
-)
+GUEST_HOP = (0, 3, 5, 8)
+GUEST_NEAR = (3, 7, 11, 14)
+GUEST_FAR = (5, 9, 12, 15)
+
+def guest_stages(z, at):
+    order = [(0, 0)] + [(d, 2 * d - 1 + up) for d in range(1, NZ) for up in range(2) if (z - d >= 0, z + d < NZ)[up]]
+    return ([(0, k) for d, k in order if k and GUEST_HOP[d] == at]
+        + [(1, k) for i, (d, k) in enumerate(order) if GUEST_NEAR[i] == at]
+        + [(2, k) for i, (d, k) in enumerate(order) if GUEST_FAR[i] == at])
 
 def backward_kernel(experts, slots, SB, block, meta_ref, cota_ref, cotb_ref, rows_ref, ga_ref, ua_ref, wg_hbm, wu_hbm, wd_hbm, gr_ref, dwg_hbm, dwu_hbm, dwd_hbm,
                   wg, wu, wd, dwg, dwu, dwd, gp, wsem, osem):
@@ -939,7 +952,8 @@
         [g.astype(bf).reshape(devices, -1) for g in grads] + [jnp.zeros((devices, small_rows * 128 - used), bf)], axis=1
     ).reshape(devices * small_rows, 128)
     grad_wqkv, out_grad = lax.optimization_barrier((grad_wqkv, out_grad))
-    qkv_grad, small_grad, moe_b, out_grad = scatter_all([grad_wqkv, packed], 8, line=[moe_b, out_grad])
+    out_grad = lax.psum_scatter(out_grad, "shard", scatter_dimension=0, tiled=True).astype(f32)
+    qkv_grad, small_grad, moe_b = scatter_all([grad_wqkv, packed], 8, line=[moe_b])
     block_out = (residual + jnp.concatenate([moe_a, moe_b], axis=0)).astype(bf)
     small_grad = small_grad.reshape(-1)
     router_g, attn_g, ffn_g, query_g, key_g = [small_grad[o : o + n] for o, n in zip(starts, sizes)]

time: 1260 us -> 1240 us (0.984)
  Pallas kernels: 1130 us -> 1110 us
    pallas_call x2, Pallas kernels: 404 us -> 368 us  [rs32(): pl.pallas_call(functools.partial(rs_kernel, n, nl, parts), out_shape=[jax...]
  transfers between devices with their start and end apart: 3 -> 4, of which waited for: 0 -> 1; matrix products, arithmetic and copies ran while one was open for 6% -> 7% of each run, Pallas kernels for 64% -> 76%
where the time goes in v9:
time: 1240 us; the launch traced here: 1230 us
  Pallas kernels  1110 us (90%)
  matrix products  45.8 us (4%)
  local copies, waits for them, and re-layouts  34.4 us (3%)
  other arithmetic  28.1 us (2%)
  between operations  16.5 us (1%)
    pallas_call x2, Pallas kernels, rs32(): pl.pallas_call(functools.partial(rs_kernel, n, nl, parts), out_shape=[jax...  368 us
    pallas_call x2, Pallas kernels, ag32(): pl.pallas_call(functools.partial(ag_kernel, n, m), out_shape=[jax.ShapeDt...  358 us
    pallas_call x1, Pallas kernels, experts_backward(): pl.pallas_call(functools.partial(backward_kernel, experts, slots, SB, blo...  140 us
    pallas_call x1, Pallas kernels, experts_forward(): pl.pallas_call(functools.partial(forward_kernel, experts, slots, SB, host...  114 us
    pallas_call x1, Pallas kernels, attention_backward(): pl.pallas_call(functools.partial(attention_backward_kernel, group, hosted...  61.2 us
    pallas_call x1, Pallas kernels, attention_forward(): pl.pallas_call(functools.partial(attention_forward_kernel, group), grid=(...  38.4 us
    pallas_call x1, Pallas kernels, line_scatter(): pl.pallas_call(functools.partial(line_scatter_kernel, parts), out_shape=j...  27.5 us
  transfers between devices with their start and end apart: 4, of which 1 were waited for; matrix products, arithmetic and copies ran while one was open for 7% of the time, Pallas kernels for 76%

profile of v9, /device:TPU:18, one launch (start us, length us, event | category | flops | bytes accessed | tf_op | source)
XLA Modules:
  0.0 1233.8 jit_solution(3812464687122779959)
XLA Ops:
  8.1 0.8 copy.59
  9.1 2.3 fusion.31
  11.4 0.9 pad_maximum_fusion.4
  12.3 0.7 concatenate.34
  13.0 167.2 %gather_all.2 = (bf16[2,2,2,4,2,32,5120]{6,5,4,3,2,1,0:T(8,128)(2,1)}, bf16[2,2,2,4,2,32,128]{6,5,4,3,2,1,0:T(8,128)(2,1)}, bf16[2,2,2,4,2,64,2048]{6,5,4,3,2,1,0:T(8,128)(2,1)}, bf16[4,2,128,2048]{3,2,1,0:T(8,128)(2,1)}) custom-call(bf16[2,32,5120]{2,1,0:T(8,128)(2,1)} %bitcast.71, bf16[2,32,128]{2,1,0:T(8,128)(2,1)} %bitcast.84, ...), custom_call_target="tpu_custom_call" | custom-call | tf_op jit(solution)/shard_map/gather_all/pallas_call | solution.py:164
  180.4 1.3 reshape_reshape_reshape.6
  183.8 2.0 fusion.22
  185.7 1.3 pad_maximum_fusion.5
  187.1 0.9 multiply_reduce_fusion
  188.0 3.0 fusion.1.n_ref
  191.0 38.4 %attention_forward.1 = (f32[256,4096]{1,0:T(8,128)}, f32[256,512]{1,0:T(8,128)}, bf16[256,4096]{1,0:T(8,128)(2,1)}, bf16[1024,512]{1,0:T(8,128)(2,1)}, bf16[1024...) custom-call(bf16[1024,2048]{1,0:T(8,128)(2,1)} %fusion.1.n_ref, bf16[2048,5120]{1,0:T(8,128)(2,1)} %bitcast.56, ...), custom_call_target="tpu_custom_call" | custom-call | flops 12999999488 | bytes 45000000 | tf_op jit(solution)/shard_map/attention_forward/pallas_call | solution.py:673
  229.4 8.9 multiply_reduce_fusion.3
  240.6 2.0 concatenate.37
  242.6 190.7 %gather_all.3 = bf16[2,2,2,4,2,128,2176]{6,5,4,3,2,1,0:T(8,128)(2,1)} custom-call(bf16[2,128,2176]{2,1,0:T(8,128)(2,1)} %bitcast.69), custom_call_target="tpu_custom_call" | custom-call | tf_op jit(solution)/shard_map/gather_all/pallas_call | solution.py:164
  433.3 113.7 %experts_forward.1 = (bf16[2,2,2,4,2,64,2048]{6,5,4,3,2,1,0:T(8,128)(2,1)}, bf16[8192,2048]{1,0:T(8,128)(2,1)}, bf16[4096,2048]{1,0:T(8,128)(2,1)}, f32[4096,768]{1,0:T(8,128)}, f32[4096,768]{1,0:T(8,128)}) custom-call(bf16[2,64,2048]{2,1,0:T(8,128)(2,1)} %bitcast.83, bf16[8192,2176]{1,0:T(8,128)(2,1)} %bitcast.61, bf16[1,2048,768]{2,1,0:T(8,128)(2,1)} %wg_hbm.1, ...), custom_call_target="tpu_custom_call" | custom-call | flops 48000000000 | bytes 130000000 | tf_op jit(solution)/shard_map/experts_forward/pallas_call | solution.py:593
  547.1 139.7 %experts_backward.1 = (bf16[8192,2176]{1,0:T(8,128)(2,1)}, f32[1,2048,768]{2,1,0:T(8,128)}, f32[1,2048,768]{2,1,0:T(8,128)}, f32[1,768,2048]{2,1,0:T(8,128)}) custom-call(bf16[8192,2176]{1,0:T(8,128)(2,1)} %bitcast.62, bf16[4096,2048]{1,0:T(8,128)(2,1)} %all-gather.2.cloned.1.call-done.cota_ref, bf16[4096,2048]{1,0:T(8,128)(2,1)} %bitcast.90, ...), custom_call_target="tpu_custom_call" | custom-call | flops 85000003584 | bytes 150000000 | tf_op jit(solution)/shard_map/experts_backward/pallas_call | solution.py:618
  686.9 232.5 %scatter_all.2 = f32[4,64,2176]{2,1,0:T(8,128)} custom-call(bf16[2,2,2,4,4,64,2176]{6,5,4,3,2,1,0:T(8,128)(2,1)} %bitcast.63), custom_call_target="tpu_custom_call" | custom-call | tf_op jit(solution)/shard_map/scatter_all/pallas_call | solution.py:307
  919.5 1.2 fusion.24
  920.7 1.1 subtract_convert_fusion
  921.9 3.1 multiply_reduce_fusion.1
  925.1 2.0 fusion.28
  927.1 8.3 convolution_convert_fusion.1
  938.2 4.8 fusion.29
  943.1 61.2 %attention_backward.1 = (f32[4,32,2048]{2,1,0:T(8,128)}, bf16[256,4096]{1,0:T(8,128)(2,1)}, bf16[1024,512]{1,0:T(8,128)(2,1)}, bf16[1024,512]{1,0:T(8,128)(2,1)}, f32[4,8,128]{2,1,0:T(8,128)}) custom-call(bf16[4,4,32,2048]{3,2,1,0:T(8,128)(2,1)} %bitcast.74, f32[256,4096]{1,0:T(8,128)} %get-tuple-element.63.refs_1_, ...), custom_call_target="tpu_custom_call" | custom-call | flops 15000000512 | bytes 20000000 | tf_op jit(solution)/shard_map/attention_backward/pallas_call | solution.py:744
  1004.3 1.8 pad_maximum_fusion.1
  1006.1 27.5 %line_scatter.1 = f32[4,64,1024]{2,1,0:T(8,128)S(1)} custom-call(bf16[4,4,64,1024]{3,2,1,0:T(8,128)(2,1)S(1)} %bitcast.53), custom_call_target="tpu_custom_call" | custom-call | tf_op jit(solution)/shard_map/line_scatter/pallas_call | solution.py:448
  1034.4 0.9 multiply_reduce_fusion.4
  1035.6 0.7 fusion.18
  1036.4 12.0 convolution_convert_fusion
  1048.4 2.5 reduce-scatter.6.cloned.1.call-done
  1050.9 12.7 %fusion.11 = (f32[256]{0:T(256)}, bf16[2048]{0:T(1024)(128)(2,1)S(1)}, f32[256,2048]{1,0:T(8,128)}) fusion(bf16[256,2048]{1,0:T(8,128)(2,1)S(1)} %copy-done.4, f32[2048]{0:T(1024)S(1)} %copy-done.20, f32[256]{0:T(256)S(1)} %get-tuple-element.184, bf16[2048,5120]{1,0:T(8,128)(2,1)} %bitcast.59, bf16[256,512]{1,0:T(8,128)(2,1)S(1)} %slice.127, ...), kind=kOutput, calls=%fused_computation.24 | convolution fusion | flops 5380241408 | bytes 26753024 | tf_op jit(solution)/shard_map/dot_general | solution.py:779
  1064.0 1.0 copy.68
  1065.1 2.3 reshape.250
  1067.4 0.7 convert_element_type.190
  1068.1 0.7 slice_reduce_fusion
  1068.8 0.7 convert_element_type.188
  1070.2 2.0 concatenate.42
  1072.2 2.0 copy.75
  1074.9 3.2 fusion.10
  1078.0 135.3 %scatter_all.3 = (f32[4,16,5120]{2,1,0:T(8,128)}, f32[4,16,128]{2,1,0:T(8,128)}, f32[4,32,2048]{2,1,0:T(8,128)}) custom-call(bf16[2,2,2,4,4,16,5120]{6,5,4,3,2,1,0:T(8,128)(2,1)} %bitcast.60, bf16[2,2,2,4,4,16,128]{6,5,4,3,2,1,0:T(8,128)(2,1)} %bitcast.72, bf16[4,4,32,2048]{3,2,1,0:T(8,128)(2,1)} %bitcast.68), custom_call_target="tpu_custom_call" | custom-call | tf_op jit(solution)/shard_map/scatter_all/pallas_call | solution.py:307
  1213.3 2.4 slice.104
  1215.7 0.7 slice.93
  1216.5 0.7 copy.70
  1217.2 1.3 fusion.33
  1218.5 1.3 fusion.34
  1219.9 1.7 fusion.30
  1221.6 2.4 fusion.12
  1224.0 2.1 convert_element_type.193
  (137 shorter events, 10.5 us)
Async XLA Ops:
  8.0 3.3 copy-start.17
  8.0 3.3 copy-start.26
  8.0 3.3 copy-start.25
  8.0 4.2 copy-start.35
  8.1 4.2 copy-start.37
  8.1 4.2 copy-start.38
  8.1 4.2 copy-start.36
  8.1 539.0 %all-gather.2.cloned.1.call-start = ((), (), s32[]{:S(2)}) async-start(), calls=%async_computation.3 | async-start | bytes 17301504 | tf_op jit(solution)/shard_map/all_gather | solution.py:874
  11.4 168.9 %copy-start.31 = (s32[256,8]{0,1:T(8,128)S(1)}, s32[256,8]{0,1:T(8,128)}, u32[]{:S(2)}) copy-start(s32[256,8]{0,1:T(8,128)} %param.28) | copy-start | bytes 24580
  180.2 739.3 %reduce-scatter.4.cloned.1.call-start = ((), (), s32[]{:S(2)}) async-start(), calls=%async_computation.4 | async-start | bytes 37748736 | tf_op jit(solution)/shard_map/reduce_scatter | solution.py:908
  181.8 6.1 copy-start.19
  181.9 5.1 copy-start.21
  183.2 55.8 %copy-start.23 = (f32[2048]{0:T(1024)}, f32[2048]{0:T(1024)S(1)}, u32[]{:S(2)}) copy-start(f32[2048]{0:T(1024)S(1)} %reshape.258) | copy-start | bytes 24580
  183.6 55.7 %copy-start.9 = (bf16[2048,32]{1,0:T(8,128)(2,1)}, bf16[2048,32]{1,0:T(8,128)(2,1)S(1)}, u32[]{:S(2)}) copy-start(bf16[2048,32]{1,0:T(8,128)(2,1)S(1)} %reshape_reshape.28) | copy-start | bytes 393220
  183.7 3.3 copy-start.33
  183.8 3.3 copy-start.7
  191.0 38.4 %copy-start.3 = (bf16[256,2048]{1,0:T(8,128)(2,1)S(1)}, bf16[256,2048]{1,0:T(8,128)(2,1)}, u32[]{:S(2)}) copy-start(bf16[256,2048]{1,0:T(8,128)(2,1)} %param.15) | copy-start | bytes 3145732
  238.3 1.5 copy-start
  239.0 0.8 copy-start.27
  239.3 3.3 copy-start.5
  239.8 0.7 copy-start.14
  239.8 0.8 copy-start.29
  547.0 503.9 %reduce-scatter.6.cloned.1.call-start = ((), (), s32[]{:S(2)}) async-start(), calls=%async_computation.5 | async-start | bytes 18874368 | tf_op jit(solution)/shard_map/reduce_scatter | solution.py:928
  686.9 233.8 %copy-start.15 = (f32[256,32]{1,0:T(8,128)S(1)}, f32[256,32]{1,0:T(8,128)}, u32[]{:S(2)}) copy-start(f32[256,32]{1,0:T(8,128)} %copy-done.14) | copy-start | bytes 98308
  686.9 233.8 %copy-start.30 = (f32[256]{0:T(256)S(1)}, f32[256]{0:T(256)}, u32[]{:S(2)}) copy-start(f32[256]{0:T(256)} %copy-done.29) | copy-start | bytes 3076
  686.9 234.9 %copy-start.10 = (bf16[2048,32]{1,0:T(8,128)(2,1)S(1)}, bf16[2048,32]{1,0:T(8,128)(2,1)}, u32[]{:S(2)}) copy-start(bf16[2048,32]{1,0:T(8,128)(2,1)} %copy-done.9) | copy-start | bytes 393220
  686.9 234.9 %copy-start.24 = (f32[2048]{0:T(1024)S(1)}, f32[2048]{0:T(1024)}, u32[]{:S(2)}) copy-start(f32[2048]{0:T(1024)} %copy-done.23) | copy-start | bytes 24580
  686.9 234.9 %copy-start.28 = (f32[256]{0:T(256)S(1)}, f32[256]{0:T(256)}, u32[]{:S(2)}) copy-start(f32[256]{0:T(256)} %copy-done.27) | copy-start | bytes 3076
  921.8 3.2 copy-start.1
  921.9 3.2 copy-start.12
  921.9 3.2 copy-start.32
  925.1 2.1 copy-start.13
  927.1 8.3 copy-start.11
  935.4 0.7 copy-start.22
  935.4 1.1 copy-start.18
  935.4 1.9 copy-start.34
  935.4 2.5 copy-start.4
  935.4 288.6 %reduce-scatter.8.cloned.1.call-start = ((), (), s32[]{:S(2)}) async-start(), calls=%async_computation.6 | async-start | bytes 2621440 | tf_op jit(solution)/shard_map/reduce_scatter | solution.py:955
  1034.4 2.0 copy-start.20
  1050.9 12.8 %copy-start.6 = (bf16[256,2048]{1,0:T(8,128)(2,1)S(1)}, bf16[256,2048]{1,0:T(8,128)(2,1)}, u32[]{:S(2)}) copy-start(bf16[256,2048]{1,0:T(8,128)(2,1)} %copy-done.5) | copy-start | bytes 3145732
  1064.0 10.8 copy-start.8
  1078.0 143.5 %copy-start.16 = (f32[4,32,2048]{2,1,0:T(8,128)S(1)}, f32[4,32,2048]{2,1,0:T(8,128)}, u32[]{:S(2)}) copy-start(f32[4,32,2048]{2,1,0:T(8,128)} %get-tuple-element.69) | copy-start | bytes 3145732
  1213.3 8.3 copy-start.2
Sparse Core Ops, SparseCore 0:
  180.3 156.1 all-gather.1
  1051.0 52.3 reduce-scatter.7
Sparse Core Ops, SparseCore 1:
  547.1 254.0 reduce-scatter.3
  935.5 115.3 reduce-scatter.5

commit v10 on v7

--- a/solution.py
+++ b/solution.py
@@ -174,6 +174,7 @@
 
 ZORDER = (0, 3, 1, 2)
 LAGS = (1, 1, 1, 1)
+LINE_LAG = 3
 
 def rs_kernel(n_arr, n_line, parts, *refs):
     n_all = n_arr + n_line
@@ -271,13 +272,14 @@
     for u in units:
         c0(*u).start(); load(*u).start()
     n = len(units); nl = len(lines)
+    per = max(1, -(-nl // n))
     L1 = LAGS[0] * n_arr; L2 = L1 + LAGS[1] * n_arr; L3 = L2 + LAGS[2] * n_arr; dl = LAGS[3] * n_arr
     for i in range(n + L3 + (NZ - 1) * dl):
         if i < n: stage0(units[i])
         if 0 <= i - L1 < n: stage1(units[i - L1])
         if 0 <= i - L2 < n: stage2(units[i - L2])
         for k in range(NZ - 1):
-            for q in (2 * (i - k), 2 * (i - k) + 1):
+            for q in range(per * (i - LINE_LAG * k), per * (i - LINE_LAG * k) + per):
                 if 0 <= q < nl:
                     if k == 0: load(*lines[q]).wait()
                     hop(lines[q], k)
@@ -396,8 +398,8 @@
     def advance(i):
         if i == 0: line_barrier(y, x, c, s)
         for k in range(NZ - 1):
-            if 0 <= i - k < n:
-                zz, h = ups[i - k]
+            if 0 <= i - 2 * k < n:
+                zz, h = ups[i - 2 * k]
                 if k < zz:
                     @pl.when(s == k)
                     def _():
@@ -405,7 +407,7 @@
                             cu(zz, h, k).wait_recv()
                             total(acc.at[zz, h], [p_ref.at[zz, h], zu.at[zz, h]])
                         cu(zz, h, k).start()
-                zz, h = dns[i - k]
+                zz, h = dns[i - 2 * k]
                 if NZ - 1 - k > zz:
                     @pl.when(s == NZ - 1 - k)
                     def _():
@@ -939,7 +941,8 @@
         [g.astype(bf).reshape(devices, -1) for g in grads] + [jnp.zeros((devices, small_rows * 128 - used), bf)], axis=1
     ).reshape(devices * small_rows, 128)
     grad_wqkv, out_grad = lax.optimization_barrier((grad_wqkv, out_grad))
-    qkv_grad, small_grad, moe_b, out_grad = scatter_all([grad_wqkv, packed], 8, line=[moe_b, out_grad])
+    out_grad = lax.psum_scatter(out_grad, "shard", scatter_dimension=0, tiled=True).astype(f32)
+    qkv_grad, small_grad, moe_b = scatter_all([grad_wqkv, packed], 8, line=[moe_b])
     block_out = (residual + jnp.concatenate([moe_a, moe_b], axis=0)).astype(bf)
     small_grad = small_grad.reshape(-1)
     router_g, attn_g, ffn_g, query_g, key_g = [small_grad[o : o + n] for o, n in zip(starts, sizes)]

time: 1260 us -> 1230 us (0.976)
  Pallas kernels: 1130 us -> 1090 us
    pallas_call x2, Pallas kernels: 404 us -> 361 us  [rs32(): pl.pallas_call(functools.partial(rs_kernel, n, nl, parts), out_shape=[jax...]
  transfers between devices with their start and end apart: 3 -> 4, of which waited for: 0 -> 1; matrix products, arithmetic and copies ran while one was open for 6% -> 7% of each run, Pallas kernels for 64% -> 76%
where the time goes in v10:
time: 1230 us; the launch traced here: 1220 us
  Pallas kernels  1090 us (89%)
  matrix products  45.7 us (4%)
  local copies, waits for them, and re-layouts  34.4 us (3%)
  other arithmetic  28.1 us (2%)
  between operations  16.5 us (1%)
    pallas_call x2, Pallas kernels, rs32(): pl.pallas_call(functools.partial(rs_kernel, n, nl, parts), out_shape=[jax...  361 us
    pallas_call x2, Pallas kernels, ag32(): pl.pallas_call(functools.partial(ag_kernel, n, m), out_shape=[jax.ShapeDt...  358 us
    pallas_call x1, Pallas kernels, experts_backward(): pl.pallas_call(functools.partial(backward_kernel, experts, slots, SB, blo...  140 us
    pallas_call x1, Pallas kernels, experts_forward(): pl.pallas_call(functools.partial(forward_kernel, experts, slots, SB, host...  106 us
    pallas_call x1, Pallas kernels, attention_backward(): pl.pallas_call(functools.partial(attention_backward_kernel, group, hosted...  54.4 us
    pallas_call x1, Pallas kernels, attention_forward(): pl.pallas_call(functools.partial(attention_forward_kernel, group), grid=(...  38.4 us
    pallas_call x1, Pallas kernels, line_scatter(): pl.pallas_call(functools.partial(line_scatter_kernel, parts), out_shape=j...  31.7 us
  transfers between devices with their start and end apart: 4, of which 1 were waited for; matrix products, arithmetic and copies ran while one was open for 7% of the time, Pallas kernels for 76%

profile of v10, /device:TPU:18, one launch (start us, length us, event | category | flops | bytes accessed | tf_op | source)
XLA Modules:
  0.0 1219.4 jit_solution(16545587030211485784)
XLA Ops:
  8.1 0.8 copy.59
  9.1 2.3 fusion.31
  11.4 0.9 pad_maximum_fusion.4
  12.3 0.7 concatenate.34
  13.0 167.2 %gather_all.2 = (bf16[2,2,2,4,2,32,5120]{6,5,4,3,2,1,0:T(8,128)(2,1)}, bf16[2,2,2,4,2,32,128]{6,5,4,3,2,1,0:T(8,128)(2,1)}, bf16[2,2,2,4,2,64,2048]{6,5,4,3,2,1,0:T(8,128)(2,1)}, bf16[4,2,128,2048]{3,2,1,0:T(8,128)(2,1)}) custom-call(bf16[2,32,5120]{2,1,0:T(8,128)(2,1)} %bitcast.71, bf16[2,32,128]{2,1,0:T(8,128)(2,1)} %bitcast.84, ...), custom_call_target="tpu_custom_call" | custom-call | tf_op jit(solution)/shard_map/gather_all/pallas_call | solution.py:164
  180.4 1.3 reshape_reshape_reshape.6
  183.8 2.0 fusion.22
  185.7 1.3 pad_maximum_fusion.5
  187.1 0.9 multiply_reduce_fusion
  188.0 3.0 fusion.1.n_ref
  191.0 38.4 %attention_forward.1 = (f32[256,4096]{1,0:T(8,128)}, f32[256,512]{1,0:T(8,128)}, bf16[256,4096]{1,0:T(8,128)(2,1)}, bf16[1024,512]{1,0:T(8,128)(2,1)}, bf16[1024...) custom-call(bf16[1024,2048]{1,0:T(8,128)(2,1)} %fusion.1.n_ref, bf16[2048,5120]{1,0:T(8,128)(2,1)} %bitcast.56, ...), custom_call_target="tpu_custom_call" | custom-call | flops 12999999488 | bytes 45000000 | tf_op jit(solution)/shard_map/attention_forward/pallas_call | solution.py:662
  229.4 8.9 multiply_reduce_fusion.3
  240.6 2.0 concatenate.37
  242.6 190.7 %gather_all.3 = bf16[2,2,2,4,2,128,2176]{6,5,4,3,2,1,0:T(8,128)(2,1)} custom-call(bf16[2,128,2176]{2,1,0:T(8,128)(2,1)} %bitcast.69), custom_call_target="tpu_custom_call" | custom-call | tf_op jit(solution)/shard_map/gather_all/pallas_call | solution.py:164
  433.3 105.9 %experts_forward.1 = (bf16[2,2,2,4,2,64,2048]{6,5,4,3,2,1,0:T(8,128)(2,1)}, bf16[8192,2048]{1,0:T(8,128)(2,1)}, bf16[4096,2048]{1,0:T(8,128)(2,1)}, f32[4096,768]{1,0:T(8,128)}, f32[4096,768]{1,0:T(8,128)}) custom-call(bf16[2,64,2048]{2,1,0:T(8,128)(2,1)} %bitcast.83, bf16[8192,2176]{1,0:T(8,128)(2,1)} %bitcast.61, bf16[1,2048,768]{2,1,0:T(8,128)(2,1)} %wg_hbm.1, ...), custom_call_target="tpu_custom_call" | custom-call | flops 48000000000 | bytes 130000000 | tf_op jit(solution)/shard_map/experts_forward/pallas_call | solution.py:582
  539.4 139.7 %experts_backward.1 = (bf16[8192,2176]{1,0:T(8,128)(2,1)}, f32[1,2048,768]{2,1,0:T(8,128)}, f32[1,2048,768]{2,1,0:T(8,128)}, f32[1,768,2048]{2,1,0:T(8,128)}) custom-call(bf16[8192,2176]{1,0:T(8,128)(2,1)} %bitcast.62, bf16[4096,2048]{1,0:T(8,128)(2,1)} %all-gather.2.cloned.1.call-done.cota_ref, bf16[4096,2048]{1,0:T(8,128)(2,1)} %bitcast.90, ...), custom_call_target="tpu_custom_call" | custom-call | flops 85000003584 | bytes 150000000 | tf_op jit(solution)/shard_map/experts_backward/pallas_call | solution.py:607
  679.2 233.5 %scatter_all.2 = f32[4,64,2176]{2,1,0:T(8,128)} custom-call(bf16[2,2,2,4,4,64,2176]{6,5,4,3,2,1,0:T(8,128)(2,1)} %bitcast.63), custom_call_target="tpu_custom_call" | custom-call | tf_op jit(solution)/shard_map/scatter_all/pallas_call | solution.py:308
  912.8 1.2 fusion.24
  914.0 1.1 subtract_convert_fusion
  915.2 3.1 multiply_reduce_fusion.1
  918.4 2.0 fusion.28
  920.4 8.3 convolution_convert_fusion.1
  931.5 4.9 fusion.29
  936.4 54.4 %attention_backward.1 = (f32[4,32,2048]{2,1,0:T(8,128)}, bf16[256,4096]{1,0:T(8,128)(2,1)}, bf16[1024,512]{1,0:T(8,128)(2,1)}, bf16[1024,512]{1,0:T(8,128)(2,1)}, f32[4,8,128]{2,1,0:T(8,128)}) custom-call(bf16[4,4,32,2048]{3,2,1,0:T(8,128)(2,1)} %bitcast.74, f32[256,4096]{1,0:T(8,128)} %get-tuple-element.63.refs_1_, ...), custom_call_target="tpu_custom_call" | custom-call | flops 15000000512 | bytes 20000000 | tf_op jit(solution)/shard_map/attention_backward/pallas_call | solution.py:733
  990.8 1.8 pad_maximum_fusion.1
  992.6 31.7 %line_scatter.1 = f32[4,64,1024]{2,1,0:T(8,128)S(1)} custom-call(bf16[4,4,64,1024]{3,2,1,0:T(8,128)(2,1)S(1)} %bitcast.53), custom_call_target="tpu_custom_call" | custom-call | tf_op jit(solution)/shard_map/line_scatter/pallas_call | solution.py:449
  1025.2 0.9 multiply_reduce_fusion.4
  1026.4 0.7 fusion.18
  1027.1 11.9 convolution_convert_fusion
  1039.0 4.9 reduce-scatter.6.cloned.1.call-done
  1043.9 12.7 %fusion.11 = (f32[256]{0:T(256)}, bf16[2048]{0:T(1024)(128)(2,1)S(1)}, f32[256,2048]{1,0:T(8,128)}) fusion(bf16[256,2048]{1,0:T(8,128)(2,1)S(1)} %copy-done.4, f32[2048]{0:T(1024)S(1)} %copy-done.20, f32[256]{0:T(256)S(1)} %get-tuple-element.184, bf16[2048,5120]{1,0:T(8,128)(2,1)} %bitcast.59, bf16[256,512]{1,0:T(8,128)(2,1)S(1)} %slice.127, ...), kind=kOutput, calls=%fused_computation.24 | convolution fusion | flops 5380241408 | bytes 26753024 | tf_op jit(solution)/shard_map/dot_general | solution.py:768
  1057.1 1.0 copy.68
  1058.1 2.3 reshape.250
  1060.4 0.7 convert_element_type.190
  1061.1 0.7 slice_reduce_fusion
  1061.8 0.7 convert_element_type.188
  1063.2 2.0 concatenate.42
  1065.2 2.0 copy.75
  1067.9 3.2 fusion.10
  1071.1 127.9 %scatter_all.3 = (f32[4,16,5120]{2,1,0:T(8,128)}, f32[4,16,128]{2,1,0:T(8,128)}, f32[4,32,2048]{2,1,0:T(8,128)}) custom-call(bf16[2,2,2,4,4,16,5120]{6,5,4,3,2,1,0:T(8,128)(2,1)} %bitcast.60, bf16[2,2,2,4,4,16,128]{6,5,4,3,2,1,0:T(8,128)(2,1)} %bitcast.72, bf16[4,4,32,2048]{3,2,1,0:T(8,128)(2,1)} %bitcast.68), custom_call_target="tpu_custom_call" | custom-call | tf_op jit(solution)/shard_map/scatter_all/pallas_call | solution.py:308
  1199.0 2.4 slice.104
  1201.4 0.7 slice.93
  1202.2 0.7 copy.70
  1202.9 1.3 fusion.33
  1204.2 1.3 fusion.34
  1205.5 1.7 fusion.30
  1207.2 2.4 fusion.12
  1209.7 2.1 convert_element_type.193
  (137 shorter events, 10.5 us)
Async XLA Ops:
  8.0 3.3 copy-start.17
  8.0 3.3 copy-start.26
  8.0 3.3 copy-start.25
  8.0 4.2 copy-start.35
  8.1 4.2 copy-start.37
  8.1 4.2 copy-start.38
  8.1 4.2 copy-start.36
  8.1 531.3 %all-gather.2.cloned.1.call-start = ((), (), s32[]{:S(2)}) async-start(), calls=%async_computation.3 | async-start | bytes 17301504 | tf_op jit(solution)/shard_map/all_gather | solution.py:863
  11.4 168.9 %copy-start.31 = (s32[256,8]{0,1:T(8,128)S(1)}, s32[256,8]{0,1:T(8,128)}, u32[]{:S(2)}) copy-start(s32[256,8]{0,1:T(8,128)} %param.28) | copy-start | bytes 24580
  180.2 732.6 %reduce-scatter.4.cloned.1.call-start = ((), (), s32[]{:S(2)}) async-start(), calls=%async_computation.4 | async-start | bytes 37748736 | tf_op jit(solution)/shard_map/reduce_scatter | solution.py:897
  181.8 6.1 copy-start.19
  181.9 5.1 copy-start.21
  183.2 55.8 %copy-start.23 = (f32[2048]{0:T(1024)}, f32[2048]{0:T(1024)S(1)}, u32[]{:S(2)}) copy-start(f32[2048]{0:T(1024)S(1)} %reshape.258) | copy-start | bytes 24580
  183.6 55.7 %copy-start.9 = (bf16[2048,32]{1,0:T(8,128)(2,1)}, bf16[2048,32]{1,0:T(8,128)(2,1)S(1)}, u32[]{:S(2)}) copy-start(bf16[2048,32]{1,0:T(8,128)(2,1)S(1)} %reshape_reshape.28) | copy-start | bytes 393220
  183.7 3.3 copy-start.33
  183.8 3.3 copy-start.7
  191.0 38.4 %copy-start.3 = (bf16[256,2048]{1,0:T(8,128)(2,1)S(1)}, bf16[256,2048]{1,0:T(8,128)(2,1)}, u32[]{:S(2)}) copy-start(bf16[256,2048]{1,0:T(8,128)(2,1)} %param.15) | copy-start | bytes 3145732
  238.3 1.5 copy-start
  239.0 0.8 copy-start.27
  239.3 3.3 copy-start.5
  239.8 0.7 copy-start.14
  239.8 0.8 copy-start.29
  539.3 504.6 %reduce-scatter.6.cloned.1.call-start = ((), (), s32[]{:S(2)}) async-start(), calls=%async_computation.5 | async-start | bytes 18874368 | tf_op jit(solution)/shard_map/reduce_scatter | solution.py:917
  679.1 234.8 %copy-start.15 = (f32[256,32]{1,0:T(8,128)S(1)}, f32[256,32]{1,0:T(8,128)}, u32[]{:S(2)}) copy-start(f32[256,32]{1,0:T(8,128)} %copy-done.14) | copy-start | bytes 98308
  679.1 234.8 %copy-start.30 = (f32[256]{0:T(256)S(1)}, f32[256]{0:T(256)}, u32[]{:S(2)}) copy-start(f32[256]{0:T(256)} %copy-done.29) | copy-start | bytes 3076
  679.1 236.0 %copy-start.10 = (bf16[2048,32]{1,0:T(8,128)(2,1)S(1)}, bf16[2048,32]{1,0:T(8,128)(2,1)}, u32[]{:S(2)}) copy-start(bf16[2048,32]{1,0:T(8,128)(2,1)} %copy-done.9) | copy-start | bytes 393220
  679.2 236.0 %copy-start.24 = (f32[2048]{0:T(1024)S(1)}, f32[2048]{0:T(1024)}, u32[]{:S(2)}) copy-start(f32[2048]{0:T(1024)} %copy-done.23) | copy-start | bytes 24580
  679.2 236.0 %copy-start.28 = (f32[256]{0:T(256)S(1)}, f32[256]{0:T(256)}, u32[]{:S(2)}) copy-start(f32[256]{0:T(256)} %copy-done.27) | copy-start | bytes 3076
  915.1 3.2 copy-start.1
  915.1 3.2 copy-start.12
  915.2 3.2 copy-start.32
  918.4 2.1 copy-start.13
  920.4 8.3 copy-start.11
  928.7 0.7 copy-start.22
  928.7 1.1 copy-start.18
  928.7 1.9 copy-start.34
  928.7 2.5 copy-start.4
  928.7 280.9 %reduce-scatter.8.cloned.1.call-start = ((), (), s32[]{:S(2)}) async-start(), calls=%async_computation.6 | async-start | bytes 2621440 | tf_op jit(solution)/shard_map/reduce_scatter | solution.py:944
  1025.2 2.0 copy-start.20
  1043.9 12.8 %copy-start.6 = (bf16[256,2048]{1,0:T(8,128)(2,1)S(1)}, bf16[256,2048]{1,0:T(8,128)(2,1)}, u32[]{:S(2)}) copy-start(bf16[256,2048]{1,0:T(8,128)(2,1)} %copy-done.5) | copy-start | bytes 3145732
  1057.0 10.8 copy-start.8
  1071.1 136.2 %copy-start.16 = (f32[4,32,2048]{2,1,0:T(8,128)S(1)}, f32[4,32,2048]{2,1,0:T(8,128)}, u32[]{:S(2)}) copy-start(f32[4,32,2048]{2,1,0:T(8,128)} %get-tuple-element.69) | copy-start | bytes 3145732
  1199.0 8.3 copy-start.2
Sparse Core Ops, SparseCore 0:
  180.3 156.1 all-gather.1
  1044.1 52.3 reduce-scatter.7
Sparse Core Ops, SparseCore 1:
  539.4 254.9 reduce-scatter.3
  928.8 115.1 reduce-scatter.5
